TPU v7x, 8 devices: a whole 2x2x1 slice. The times are simulated.
8 devices in a mesh: dp: 1 (over z), tp: 8 (over y, x, core).
Axes of the slice: x: 2, y: 2, z: 1, core: 2. Of those that a mesh axis runs over, the one named last changes fastest.
Arguments:
- tokens: int32 [1, 2048], P('dp')
- embed_table: bfloat16 [102400, 2048], P('tp')
- w_q: bfloat16 [2048, 16, 192], P(None, 'tp')
- w_dkv: bfloat16 [2048, 576], replicated
- g_kv: float32 [512], replicated
- w_uk: bfloat16 [512, 16, 128], P(None, 'tp')
- w_uv: bfloat16 [512, 16, 128], P(None, 'tp')
- w_o: bfloat16 [16, 128, 2048], P('tp')
- g_attn: float32 [2048], replicated
- g_mlp: float32 [2048], replicated
- w_gate: bfloat16 [2048, 10944], P(None, 'tp')
- w_up: bfloat16 [2048, 10944], P(None, 'tp')
- w_down: bfloat16 [10944, 2048], P('tp')
- d_out: bfloat16 [1, 2048, 2048], P('dp', 'tp')
Outputs:
- output 1: bfloat16 [1, 2048, 2048], P('dp', 'tp')
- output 2: bfloat16 [102400, 2048], P(('dp', 'tp'))
- output 3: float32 [2048, 16, 192], P('dp', 'tp')
- output 4: float32 [2048, 576], P('dp')
- output 5: float32 [512], P('dp')
- output 6: float32 [512, 16, 128], P('dp', 'tp')
- output 7: float32 [512, 16, 128], P('dp', 'tp')
- output 8: float32 [16, 128, 2048], P(('dp', 'tp'))
- output 9: float32 [2048], P('dp')
- output 10: float32 [2048], P('dp')
- output 11: float32 [2048, 10944], P('dp', 'tp')
- output 12: float32 [2048, 10944], P('dp', 'tp')
- output 13: float32 [10944, 2048], P(('dp', 'tp'))
All inputs are finite; a program needn't handle non-finite values.
Results may differ from a plain program's by a relative error of at most 0.02.
Values are sent between devices in bfloat16 or wider.
A program may use at most 1 GiB of HBM per device.

v0:
```python
import jax
import jax.numpy as jnp
from jax import lax
from jax.sharding import PartitionSpec as P

EPSILON = 1e-6
ROPE_BASE = 10000.0


def matmul_f32(form, lhs, rhs):
    return jnp.einsum(form, lhs, rhs, preferred_element_type=jnp.float32)


def rope_tables(seq_len, rope_dim):
    inv_freq = ROPE_BASE ** (-jnp.arange(0, rope_dim, 2, dtype=jnp.float32) / rope_dim)
    angles = jnp.arange(seq_len, dtype=jnp.float32)[:, None] * inv_freq[None, :]
    return jnp.cos(angles), jnp.sin(angles)


def apply_rope(x_in, cos_t, sin_t):
    half_dim = x_in.shape[-1] // 2
    x_lo = x_in[..., :half_dim]
    x_hi = x_in[..., half_dim:]
    return jnp.concatenate([x_lo * cos_t - x_hi * sin_t, x_hi * cos_t + x_lo * sin_t], axis=-1)


def rms_norm(x_in, gain):
    inv_rms = lax.rsqrt(jnp.mean(x_in * x_in, axis=-1, keepdims=True) + EPSILON)
    return (x_in * inv_rms * gain).astype(jnp.bfloat16)


def kv_prep(latent, g_kv):
    value_a7 = g_kv.shape[0]
    cos_t, sin_t = rope_tables(latent.shape[1], latent.shape[-1] - value_a7)
    k_pe = apply_rope(latent[..., value_a7:], cos_t, sin_t).astype(jnp.bfloat16)
    return rms_norm(latent[..., :value_a7], g_kv), k_pe


def attend(query, k_nope, k_pe, value):
    seq_len = query.shape[1]
    rope_dim = k_pe.shape[-1]
    nope_dim = query.shape[-1] - rope_dim
    cos_t, sin_t = rope_tables(seq_len, rope_dim)
    q_pe = apply_rope(query[..., nope_dim:].astype(jnp.float32), cos_t[:, None, :], sin_t[:, None, :]).astype(jnp.bfloat16)
    scores = matmul_f32('bqhn,bkhn->bhqk', query[..., :nope_dim], k_nope) + matmul_f32('bqhr,bkr->bhqk', q_pe, k_pe)
    causal = jnp.arange(seq_len)[:, None] >= jnp.arange(seq_len)[None, :]
    scores = jnp.where(causal, scores * query.shape[-1] ** -0.5, -1e30)
    attn_prob = jax.nn.softmax(scores, axis=-1).astype(jnp.bfloat16)
    return matmul_f32('bhqk,bkhv->bqhv', attn_prob, value).astype(jnp.bfloat16)


def layer_pass(embedded, d_out, w_q, w_dkv, g_kv, w_uk, w_uv, w_o, g_attn, g_mlp, w_gate, w_up, w_down):
    x_attn_loc, attn_norm_pull = jax.vjp(rms_norm, embedded.astype(jnp.float32), g_attn)
    x_attn = lax.all_gather(x_attn_loc, 'tp', axis=1, tiled=True)
    query = matmul_f32('bsd,dhe->bshe', x_attn, w_q).astype(jnp.bfloat16)
    latent = matmul_f32('bsd,dc->bsc', x_attn, w_dkv)
    (c_kv, k_pe), kv_pull = jax.vjp(kv_prep, latent, g_kv)
    k_nope = matmul_f32('bsc,che->bshe', c_kv, w_uk).astype(jnp.bfloat16)
    value = matmul_f32('bsc,chv->bshv', c_kv, w_uv).astype(jnp.bfloat16)
    attn_out, attend_pull = jax.vjp(attend, query, k_nope, k_pe, value)
    attn_part = matmul_f32('bshv,hvd->bsd', attn_out, w_o).astype(jnp.bfloat16)
    attn_loc = lax.psum_scatter(attn_part, 'tp', scatter_dimension=1, tiled=True)
    residual = (embedded.astype(jnp.float32) + attn_loc.astype(jnp.float32)).astype(jnp.bfloat16)
    x_mlp_loc, mlp_norm_pull = jax.vjp(rms_norm, residual.astype(jnp.float32), g_mlp)
    x_mlp = lax.all_gather(x_mlp_loc, 'tp', axis=1, tiled=True)
    gate = matmul_f32('bsd,df->bsf', x_mlp, w_gate)
    up_proj = matmul_f32('bsd,df->bsf', x_mlp, w_up)
    gate_sig = jax.nn.sigmoid(gate)
    hidden = (gate * gate_sig * up_proj).astype(jnp.bfloat16)
    mlp_part = matmul_f32('bsf,fd->bsd', hidden, w_down).astype(jnp.bfloat16)
    mlp_loc = lax.psum_scatter(mlp_part, 'tp', scatter_dimension=1, tiled=True)
    layer_out = (residual.astype(jnp.float32) + mlp_loc.astype(jnp.float32)).astype(jnp.bfloat16)

    dy_full = lax.all_gather(d_out, 'tp', axis=1, tiled=True)
    d_hidden = matmul_f32('bsd,fd->bsf', dy_full, w_down)
    dw_down = matmul_f32('bsf,bsd->fd', hidden, dy_full)
    d_up = (d_hidden * gate * gate_sig).astype(jnp.bfloat16)
    d_gate = (d_hidden * up_proj * gate_sig * (1.0 + gate * (1.0 - gate_sig))).astype(jnp.bfloat16)
    dw_gate = matmul_f32('bsd,bsf->df', x_mlp, d_gate)
    dw_up = matmul_f32('bsd,bsf->df', x_mlp, d_up)
    dx_mlp_part = (matmul_f32('bsf,df->bsd', d_gate, w_gate) + matmul_f32('bsf,df->bsd', d_up, w_up)).astype(jnp.bfloat16)
    dx_mlp = lax.psum_scatter(dx_mlp_part, 'tp', scatter_dimension=1, tiled=True)
    d_res_norm, dg_mlp_part = mlp_norm_pull(dx_mlp)
    d_residual = d_out.astype(jnp.float32) + d_res_norm
    d_attn_full = lax.all_gather(d_residual.astype(jnp.bfloat16), 'tp', axis=1, tiled=True)
    dw_o = matmul_f32('bshv,bsd->hvd', attn_out, d_attn_full)
    d_attn_out = matmul_f32('bsd,hvd->bshv', d_attn_full, w_o).astype(jnp.bfloat16)
    d_query, d_knope, d_kpe, d_value = attend_pull(d_attn_out)
    dw_uk = matmul_f32('bsc,bshe->che', c_kv, d_knope)
    dw_uv = matmul_f32('bsc,bshv->chv', c_kv, d_value)
    d_ckv = (matmul_f32('bshe,che->bsc', d_knope, w_uk) + matmul_f32('bshv,chv->bsc', d_value, w_uv)).astype(jnp.bfloat16)
    d_latent, dg_kv_part = kv_pull((d_ckv, d_kpe))
    d_latent = d_latent.astype(jnp.bfloat16)
    dw_q = matmul_f32('bsd,bshe->dhe', x_attn, d_query)
    dw_dkv_part = matmul_f32('bsd,bsc->dc', x_attn, d_latent)
    dx_attn_part = (matmul_f32('bshe,dhe->bsd', d_query, w_q) + matmul_f32('bsc,dc->bsd', d_latent, w_dkv)).astype(jnp.bfloat16)
    dx_attn = lax.psum_scatter(dx_attn_part, 'tp', scatter_dimension=1, tiled=True)
    d_emb_norm, dg_attn_part = attn_norm_pull(dx_attn)
    d_embed = (d_residual + d_emb_norm).astype(jnp.bfloat16)
    dw_dkv, dg_kv, dg_attn, dg_mlp = lax.psum((dw_dkv_part, dg_kv_part, dg_attn_part, dg_mlp_part), 'tp')
    return layer_out, d_embed, (dw_q, dw_dkv, dg_kv, dw_uk, dw_uv, dw_o, dg_attn, dg_mlp, dw_gate, dw_up, dw_down)


def solution(mesh):
    def device_step(tokens, embed_table, w_q, w_dkv, g_kv, w_uk, w_uv, w_o, g_attn, g_mlp, w_gate, w_up, w_down, d_out):
        vocab_local, model_dim = embed_table.shape
        local_ids = tokens - lax.axis_index('tp') * vocab_local
        owned = (local_ids >= 0) & (local_ids < vocab_local)
        rows = jnp.take(embed_table, jnp.where(owned, local_ids, 0), axis=0)
        rows = jnp.where(owned[..., None], rows, jnp.zeros((), rows.dtype))
        embedded = lax.psum_scatter(rows, 'tp', scatter_dimension=1, tiled=True)
        layer_out, d_embed, weight_grads = layer_pass(embedded, d_out, w_q, w_dkv, g_kv, w_uk, w_uv, w_o, g_attn, g_mlp, w_gate, w_up, w_down)
        de_full = lax.all_gather(d_embed, 'tp', axis=1, tiled=True)
        slot_ids = jnp.where(owned, local_ids, vocab_local)
        d_table = jax.ops.segment_sum(de_full.reshape(-1, model_dim).astype(jnp.float32), slot_ids.reshape(-1), num_segments=vocab_local)
        return (layer_out, d_table.astype(jnp.bfloat16)) + weight_grads

    row_spec = P('dp', 'tp', None)
    head_spec = P(None, 'tp', None)
    in_specs = (P('dp', None), P('tp', None), head_spec, P(None, None), P(None), head_spec, head_spec, P('tp', None, None), P(None), P(None), P(None, 'tp'), P(None, 'tp'), P('tp', None), row_spec)
    out_specs = (row_spec, P(('dp', 'tp'), None), P('dp', 'tp', None), P('dp', None), P('dp'), P('dp', 'tp', None), P('dp', 'tp', None), P(('dp', 'tp'), None, None), P('dp'), P('dp'), P('dp', 'tp'), P('dp', 'tp'), P(('dp', 'tp'), None))
    return jax.shard_map(device_step, mesh=mesh, in_specs=in_specs, out_specs=out_specs, check_vma=False)
```

profile of v0, /device:TPU:0, one launch (start us, length us, event | category | flops | bytes accessed | tf_op | source)
XLA Modules:
  0.0 1274.8 jit_solution(9462471237906489465)
XLA Ops:
  8.2 103.3 %gather_fusion = bf16[2048,2048]{1,0:T(8,128)(2,1)} fusion(bf16[12800,2048]{1,0:T(8,128)(2,1)} %param.15, s32[2048]{0:T(1024)S(1)} %broadcast_clamp_fusion.1), kind=kCustom, calls=%fused_computation | custom fusion | bytes 16785408 | tf_op jit(solution)/shard_map/jit(_take)/gather | solution.py:109
  111.5 7.7 fusion.55
  119.3 64.8 %reduce-scatter.6.cloned.1.call-done = bf16[1,256,2048]{2,1,0:T(8,128)(2,1)} async-done(((bf16[1,2048,2048]{2,1,0:T(8,128)(2,1)}), bf16[1,256,2048]{2,1,0:T(8,128)(2,1)}) %reduce-scatter.6.cloned.1.call-update) | async-done | bytes 1048592 | tf_op jit(solution)/shard_map/reduce_scatter | solution.py:111
  191.7 4.1 iota_compare_fusion
  195.8 42.0 %all-gather.6.cloned.1.call-done = bf16[1,2048,2048]{2,1,0:T(8,128)(2,1)} async-done(((bf16[1,256,2048]{2,1,0:T(8,128)(2,1)}), bf16[1,2048,2048]{2,1,0:T(8,128)(2,1)}) %all-gather.6.cloned.1.call-update) | async-done | bytes 8388624 | tf_op jit(solution)/shard_map/all_gather | solution.py:54
  237.8 8.6 fusion.66
  257.1 14.2 %fusion.143 = f32[2048,2048,2]{1,0,2:T(8,128)} fusion(bf16[2048,2,32]{0,2,1:T(8,128)(2,1)S(1)} %get-tuple-element.62, bf16[2048,2,32]{0,2,1:T(8,128)(2,1)S(1)} %get-tuple-element.61, bf16[2048,32]{0,1:T(8,128)(2,1)S(1)} %get-tuple-element.58, bf16[2048,32]{0,1:T(8,128)(2,1)S(1)} %get-tuple-element.57), kind=kOutput, calls=%fused_computation.158 | convolution fusion | flops 1075314688 | bytes 34340864 | tf_op jit(solution)/shard_map/jvp(bqhr,bkr->bhqk)/dot_general | solution.py:11
  271.4 27.6 %fusion.172 = (f32[2,2048]{1,0:T(2,128)S(1)}, f32[1,2,2048,2048]{2,3,1,0:T(8,128)}) fusion(f32[2048,2048,2]{1,0,2:T(8,128)} %fusion.143, bf16[2048,2,128]{2,0,1:T(8,128)(2,1)} %convolution_convert_fusion.1, bf16[1,2048,2,192]{1,3,2,0:T(8,128)(2,1)} %copy-done.14, pred[2048,2048]{0,1:T(8,128)(4,1)} %iota_compare_fusion), kind=kOutput, calls=%fused_computation.204 | convolution fusion | flops 2181033984 | bytes 73416704 | tf_op jit(solution)/shard_map/jvp(bqhn,bkhn->bhqk)/dot_general | solution.py:11
  299.0 13.4 %fusion.21 = f32[2,2048]{1,0:T(2,128)S(1)} fusion(f32[1,2,2048,2048]{2,3,1,0:T(8,128)} %get-tuple-element.71, f32[2,2048]{1,0:T(2,128)S(1)} %get-tuple-element.70), kind=kLoop, calls=%fused_computation.28 | loop fusion | flops 16773120 | bytes 33587200 | tf_op jit(solution)/shard_map/jvp()/reduce_sum | solution.py:48
  312.4 6.9 copy-done.1
  319.3 9.0 divide_convert_fusion
  328.3 8.3 fusion.97
  337.7 5.8 fusion.57
  343.5 62.4 %reduce-scatter.8.cloned.1.call-done = bf16[1,256,2048]{2,1,0:T(8,128)(2,1)} async-done(((bf16[1,2048,2048]{2,1,0:T(8,128)(2,1)}), bf16[1,256,2048]{2,1,0:T(8,128)(2,1)}) %reduce-scatter.8.cloned.1.call-update) | async-done | bytes 1048592 | tf_op jit(solution)/shard_map/reduce_scatter | solution.py:62
  410.5 47.9 %all-gather.8.cloned.1.call-done = bf16[1,2048,2048]{2,1,0:T(8,128)(2,1)} async-done(((bf16[1,256,2048]{2,1,0:T(8,128)(2,1)}), bf16[1,2048,2048]{2,1,0:T(8,128)(2,1)}) %all-gather.8.cloned.1.call-update) | async-done | bytes 8388624 | tf_op jit(solution)/shard_map/all_gather | solution.py:65
  458.4 18.7 %fusion.43 = f32[2048,1368]{0,1:T(8,128)} fusion(bf16[2048,1368]{0,1:T(8,128)(2,1)} %param.25, bf16[1,2048,2048]{2,1,0:T(8,128)(2,1)} %all-gather.8.cloned.1.call-done), kind=kOutput, calls=%fused_computation.58 | convolution fusion | flops 11475615744 | bytes 25198592 | tf_op jit(solution)/shard_map/bsd,df->bsf/dot_general | solution.py:11
  477.1 15.6 %fusion.45 = f32[2048,1368]{0,1:T(8,128)} fusion(bf16[2048,1368]{0,1:T(8,128)(2,1)} %param.24, bf16[1,2048,2048]{2,1,0:T(8,128)(2,1)S(1)} %copy-done.73), kind=kOutput, calls=%fused_computation.60 | convolution fusion | flops 11475615744 | bytes 25198592 | tf_op jit(solution)/shard_map/bsd,df->bsf/dot_general | solution.py:11
  492.7 15.7 %all-gather.10.cloned.1.call-done = bf16[1,2048,2048]{2,1,0:T(8,128)(2,1)} async-done(((bf16[1,256,2048]{2,1,0:T(8,128)(2,1)}), bf16[1,2048,2048]{2,1,0:T(8,128)(2,1)}) %all-gather.10.cloned.1.call-update) | async-done | bytes 8388624 | tf_op jit(solution)/shard_map/all_gather | solution.py:74
  508.4 26.4 %multiply_convert_fusion = (bf16[2048,1368]{0,1:T(8,128)(2,1)}, bf16[2048,1368]{0,1:T(8,128)(2,1)}, bf16[2048,1368]{0,1:T(8,128)(2,1)}) fusion(f32[2048,1368]{0,1:T(8,128)} %fusion.45, f32[2048,1368]{0,1:T(8,128)} %fusion.43, bf16[1368,2048]{1,0:T(8,128)(2,1)} %param.26, bf16[1,2048,2048]{2,1,0:T(8,128)(2,1)} %all-gather.10.cloned.1.call-done), kind=kOutput, calls=%fused_computation.39 | convolution fusion | flops 11520442368 | bytes 53215232 | tf_op jit(solution)/shard_map/bsd,fd->bsf/dot_general | solution.py:11
  534.8 19.1 %fusion.173 = f32[2048,2048]{1,0:T(8,128)} fusion(bf16[2048,1368]{0,1:T(8,128)(2,1)} %get-tuple-element.55, bf16[2048,1368]{0,1:T(8,128)(2,1)} %param.24), kind=kOutput, calls=%fused_computation.205 | convolution fusion | flops 11475615744 | bytes 27983872 | tf_op jit(solution)/shard_map/bsf,df->bsd/dot_general | solution.py:11
  553.9 19.6 %fusion.30 = bf16[1,2048,2048]{2,1,0:T(8,128)(2,1)} fusion(f32[2048,2048]{1,0:T(8,128)} %fusion.173, bf16[2048,1368]{0,1:T(8,128)(2,1)S(1)} %copy-done.76, bf16[2048,1368]{0,1:T(8,128)(2,1)} %param.25), kind=kOutput, calls=%fused_computation.44 | convolution fusion | flops 11484004352 | bytes 36372480 | tf_op jit(solution)/shard_map/bsf,df->bsd/dot_general | solution.py:11
  573.8 62.2 %reduce-scatter.12.cloned.1.call-done = bf16[1,256,2048]{2,1,0:T(8,128)(2,1)} async-done(((bf16[1,2048,2048]{2,1,0:T(8,128)(2,1)}), bf16[1,256,2048]{2,1,0:T(8,128)(2,1)}) %reduce-scatter.12.cloned.1.call-update) | async-done | bytes 1048592 | tf_op jit(solution)/shard_map/reduce_scatter | solution.py:82
  642.7 48.4 %all-gather.12.cloned.1.call-done = bf16[1,2048,2048]{2,1,0:T(8,128)(2,1)} async-done(((bf16[1,256,2048]{2,1,0:T(8,128)(2,1)}), bf16[1,2048,2048]{2,1,0:T(8,128)(2,1)}) %all-gather.12.cloned.1.call-update) | async-done | bytes 8388624 | tf_op jit(solution)/shard_map/all_gather | solution.py:85
  691.1 7.0 fusion.100
  698.1 12.9 %fusion.94 = bf16[2048,2,128]{0,2,1:T(8,128)(2,1)} fusion(bf16[2,128,2048]{1,2,0:T(8,128)(2,1)} %fusion.100, bf16[1,2,2048,2048]{2,3,1,0:T(8,128)(2,1)} %divide_convert_fusion), kind=kOutput, calls=%fused_computation.120 | convolution fusion | flops 2148007936 | bytes 18874368 | tf_op jit(solution)/shard_map/transpose(jvp(bhqk,bkhv->bqhv))/dot_general | solution.py:11
  711.0 20.8 %fusion.10 = (f32[2,2048]{1,0:T(2,128)S(1)}, bf16[2,2048,2048]{1,2,0:T(8,128)(2,1)}) fusion(f32[1,2,2048,2048]{2,3,1,0:T(8,128)} %get-tuple-element.71, f32[2,2048]{1,0:T(2,128)S(1)} %multiply_divide_fusion, f32[2,2048]{1,0:T(2,128)S(1)} %copy-done.43, bf16[2,128,2048]{1,2,0:T(8,128)(2,1)} %fusion.100, bf16[2048,2,128]{2,0,1:T(8,128)(2,1)S(1)} %copy-done.9), kind=kOutput, calls=%fused_computation.14 | convolution fusion | flops 2197811200 | bytes 52477952 | tf_op jit(solution)/shard_map/transpose(jvp(bhqk,bkhv->bqhv))/dot_general | solution.py:11
  731.8 22.1 %fusion.88 = bf16[2048,2,128]{2,0,1:T(8,128)(2,1)} fusion(bf16[1,2048,2,192]{1,3,2,0:T(8,128)(2,1)} %copy-done.14, bf16[2,2048,2048]{1,2,0:T(8,128)(2,1)} %get-tuple-element.73, f32[1,2,2048,2048]{2,3,1,0:T(8,128)} %get-tuple-element.71, f32[2,2048]{1,0:T(2,128)S(1)} %neg.57, f32[2,2048]{1,0:T(2,128)S(1)} %copy-done.49, f32[2,2048]{1,0:T(2,128)S(1)} %copy-done.43, ...), kind=kOutput, calls=%fused_computation.118 | convolution fusion | flops 2206728192 | bytes 56672256 | tf_op jit(solution)/shard_map/transpose(jvp(bqhn,bkhn->bhqk))/dot_general | solution.py:11
  754.0 26.2 %fusion.91 = bf16[1,2048,2,128]{1,3,2,0:T(8,128)(2,1)} fusion(bf16[2048,2,128]{2,0,1:T(8,128)(2,1)S(1)} %copy-done.28, bf16[2,2048,2048]{1,2,0:T(8,128)(2,1)} %get-tuple-element.73, f32[1,2,2048,2048]{2,3,1,0:T(8,128)} %get-tuple-element.71, f32[2,2048]{1,0:T(2,128)S(1)} %neg.57, f32[2,2048]{1,0:T(2,128)S(1)} %copy-done.49, f32[2,2048]{1,0:T(2,128)S(1)} %copy-done.43, ...), kind=kOutput, calls=%fused_computation.119 | convolution fusion | flops 2206728192 | bytes 56672256 | tf_op jit(solution)/shard_map/transpose(jvp(bqhn,bkhn->bhqk))/dot_general | solution.py:11
  780.2 20.6 %fusion.122 = f32[1,2048,64]{1,2,0:T(8,128)S(1)} fusion(bf16[2048,2,32]{0,2,1:T(8,128)(2,1)S(1)} %copy-done.32, bf16[2048,2,32]{0,2,1:T(8,128)(2,1)S(1)} %copy-done.30, bf16[2,2048,2048]{1,2,0:T(8,128)(2,1)} %get-tuple-element.73, f32[1,2,2048,2048]{2,3,1,0:T(8,128)} %get-tuple-element.71, f32[2,2048]{1,0:T(2,128)S(1)} %neg.57, ...), kind=kOutput, calls=%fused_computation.130 | convolution fusion | flops 1133772800 | bytes 55623680 | tf_op jit(solution)/shard_map/transpose(jvp(bqhr,bkr->bhqk))/dot_general | solution.py:11
  800.8 19.4 %fusion.110 = f32[1,2048,2,64]{1,3,2,0:T(8,128)S(1)} fusion(bf16[2048,32]{0,1:T(8,128)(2,1)S(1)} %copy-done.39, bf16[2048,32]{0,1:T(8,128)(2,1)S(1)} %copy-done.37, bf16[2,2048,2048]{1,2,0:T(8,128)(2,1)} %get-tuple-element.73, f32[1,2,2048,2048]{2,3,1,0:T(8,128)} %get-tuple-element.71, f32[2,2048]{1,0:T(2,128)S(1)} %neg.57, f32[2,2048]{1,0:T(2,128)S(1)} %copy-done.49, ...), kind=kOutput, calls=%fused_computation.126 | convolution fusion | flops 1133510656 | bytes 55885824 | tf_op jit(solution)/shard_map/transpose(jvp(bqhr,bkr->bhqk))/dot_general | solution.py:11
  828.6 10.5 fusion.141
  839.1 10.2 fusion.56
  849.4 19.1 %convert_bitcast_fusion = bf16[1,2048,2048]{2,1,0:T(8,128)(2,1)} fusion(bf16[2048,1368]{0,1:T(8,128)(2,1)} %get-tuple-element.56, bf16[1368,2048]{1,0:T(8,128)(2,1)} %param.26), kind=kOutput, calls=%fused_computation.72 | convolution fusion | flops 11479810048 | bytes 19595264 | tf_op jit(solution)/shard_map/bsf,fd->bsd/dot_general | solution.py:11
  868.8 43.0 %reduce-scatter.14.cloned.1.call-done = bf16[1,256,2048]{2,1,0:T(8,128)(2,1)} async-done(((bf16[1,2048,2048]{2,1,0:T(8,128)(2,1)}), bf16[1,256,2048]{2,1,0:T(8,128)(2,1)}) %reduce-scatter.14.cloned.1.call-update) | async-done | bytes 1048592 | tf_op jit(solution)/shard_map/reduce_scatter | solution.py:97
  914.1 63.9 %reduce-scatter.10.cloned.1.call-done = bf16[1,256,2048]{2,1,0:T(8,128)(2,1)} async-done(((bf16[1,2048,2048]{2,1,0:T(8,128)(2,1)}), bf16[1,256,2048]{2,1,0:T(8,128)(2,1)}) %reduce-scatter.10.cloned.1.call-update) | async-done | bytes 1048592 | tf_op jit(solution)/shard_map/reduce_scatter | solution.py:71
  978.0 5.1 fusion.131
  983.3 4.4 sort
  987.7 18.5 %fusion.39 = f32[2048,1368]{0,1:T(8,128)} fusion(bf16[2048,1368]{0,1:T(8,128)(2,1)} %get-tuple-element.54, bf16[1,2048,2048]{2,1,0:T(8,128)(2,1)} %all-gather.8.cloned.1.call-done), kind=kOutput, calls=%fused_computation.54 | convolution fusion | flops 11475615744 | bytes 25198592 | tf_op jit(solution)/shard_map/bsd,bsf->df/dot_general | solution.py:11
  1006.2 18.9 %fusion.41 = f32[2048,1368]{0,1:T(8,128)} fusion(bf16[2048,1368]{0,1:T(8,128)(2,1)} %get-tuple-element.55, bf16[1,2048,2048]{2,1,0:T(8,128)(2,1)} %all-gather.8.cloned.1.call-done), kind=kOutput, calls=%fused_computation.56 | convolution fusion | flops 11475615744 | bytes 25198592 | tf_op jit(solution)/shard_map/bsd,bsf->df/dot_general | solution.py:11
  1025.2 16.9 %fusion.35 = f32[1368,2048]{1,0:T(8,128)} fusion(bf16[2048,1368]{0,1:T(8,128)(2,1)S(1)} %bitcast.301, bf16[1,2048,2048]{2,1,0:T(8,128)(2,1)} %all-gather.10.cloned.1.call-done), kind=kOutput, calls=%fused_computation.50 | convolution fusion | flops 11475615744 | bytes 25198592 | tf_op jit(solution)/shard_map/bsf,bsd->fd/dot_general | solution.py:11
  1045.0 7.0 fusion.49
  1052.1 9.1 fusion.47
  1064.3 7.1 fusion.31
  1071.4 22.8 %all-reduce.8 = (f32[512]{0:T(512)}, f32[2048]{0:T(1024)}, f32[2048]{0:T(1024)}) all-reduce(f32[512]{0:T(512)S(1)} %get-tuple-element.41, f32[2048]{0:T(1024)S(1)} %get-tuple-element.45, f32[2048]{0:T(1024)S(1)} %copy-done.58), channel_id=1, replica_groups=mesh['dp'=1,'tp'=8] {'tp'}, use_global_device_ids=true, to_apply=%region_17.18 | all-reduce | flops 4608 | bytes 36864 | tf_op jit(solution)/shard_map/psum | solution.py:100
  1094.2 11.7 bitcast_convert_fusion.1
  1105.9 106.1 %scatter_custom_fusion = f32[12800,2048]{1,0:T(8,128)} fusion(s32[2048]{0:T(1024)S(1)} %get-tuple-element.39, f32[]{:T(128)} %constant.24.clone.1, f32[2048,2048]{1,0:T(8,128)} %bitcast_convert_fusion.1, s32[2048]{0:T(1024)S(1)} %broadcast_clamp_fusion), kind=kCustom, calls=%fused_computation.3 | custom fusion | flops 4194304 | bytes 104858112 | tf_op jit(solution)/shard_map/scatter-add | solution.py:115
  1212.0 50.9 %convert_element_type.265 = bf16[12800,2048]{1,0:T(8,128)(2,1)} convert(f32[12800,2048]{1,0:T(8,128)} %scatter_custom_fusion) | non-fusion elementwise | flops 26214400 | bytes 157286400 | tf_op jit(solution)/shard_map/convert_element_type | solution.py:116
  1262.9 5.1 copy.94
  (235 shorter events, 48.7 us)
Async XLA Ops:
  7.2 230.6 %copy-start = (bf16[2048,576]{0,1:T(8,128)(2,1)S(1)}, bf16[2048,576]{0,1:T(8,128)(2,1)}, u32[]{:S(2)}) copy-start(bf16[2048,576]{0,1:T(8,128)(2,1)} %param.17) | copy-start | bytes 7077892
  7.2 176.9 %reduce-scatter.6.cloned.1.call-start = ((), (), s32[]{:S(2)}) async-start(), calls=%async_computation.5 | async-start | bytes 9437184 | tf_op jit(solution)/shard_map/reduce_scatter | solution.py:111
  119.3 67.5 %copy-start.56 = (f32[2048]{0:T(1024)S(1)}, f32[2048]{0:T(1024)}, u32[]{:S(2)}) copy-start(f32[2048]{0:T(1024)} %param.22) | copy-start | bytes 24580
  119.3 118.5 %all-gather.6.cloned.1.call-start = ((), (), s32[]{:S(2)}) async-start(), calls=%async_computation.6 | async-start | bytes 9437184 | tf_op jit(solution)/shard_map/all_gather | solution.py:54
  189.3 216.6 %reduce-scatter.8.cloned.1.call-start = ((), (), s32[]{:S(2)}) async-start(), calls=%async_computation.7 | async-start | bytes 9437184 | tf_op jit(solution)/shard_map/reduce_scatter | solution.py:62
  189.9 56.8 %copy-start.70 = (f32[32]{0:T(128)}, f32[32]{0:T(128)S(1)}, u32[]{:S(2)}) copy-start(f32[32]{0:T(128)S(1)} %multiply_power_fusion) | copy-start | bytes 388
  255.9 72.4 %copy-start.8 = (bf16[2048,2,128]{2,0,1:T(8,128)(2,1)}, bf16[2048,2,128]{2,0,1:T(8,128)(2,1)S(1)}, u32[]{:S(2)}) copy-start(bf16[2048,2,128]{2,0,1:T(8,128)(2,1)S(1)} %convolution_convert_fusion.2) | copy-start | bytes 3145732
  299.0 20.3 %copy-start.1 = (f32[1,2,2048,2048]{2,3,1,0:T(8,128)S(1)}, f32[1,2,2048,2048]{2,3,1,0:T(8,128)}, u32[]{:S(2)}) copy-start(f32[1,2,2048,2048]{2,3,1,0:T(8,128)} %get-tuple-element.71) | copy-start | bytes 100663296
  343.4 62.4 %copy-start.4 = (bf16[1,256,2048]{2,1,0:T(8,128)(2,1)S(1)}, bf16[1,256,2048]{2,1,0:T(8,128)(2,1)}, u32[]{:S(2)}) copy-start(bf16[1,256,2048]{2,1,0:T(8,128)(2,1)} %reduce-scatter.6.cloned.1.call-done) | copy-start | bytes 3145732
  343.4 65.1 %copy-start.50 = (f32[2048]{0:T(1024)S(1)}, f32[2048]{0:T(1024)}, u32[]{:S(2)}) copy-start(f32[2048]{0:T(1024)} %param.23) | copy-start | bytes 24580
  343.5 114.9 %all-gather.8.cloned.1.call-start = ((), (), s32[]{:S(2)}) async-start(), calls=%async_computation.8 | async-start | bytes 9437184 | tf_op jit(solution)/shard_map/all_gather | solution.py:65
  407.6 231.2 %copy-start.60 = (f32[256]{0:T(256)}, f32[256]{0:T(256)S(1)}, u32[]{:S(2)}) copy-start(f32[256]{0:T(256)S(1)} %fusion.160) | copy-start | bytes 3076
  409.9 98.5 %all-gather.10.cloned.1.call-start = ((), (), s32[]{:S(2)}) async-start(), calls=%async_computation.10 | async-start | bytes 9437184 | tf_op jit(solution)/shard_map/all_gather | solution.py:74
  410.5 225.5 %reduce-scatter.12.cloned.1.call-start = ((), (), s32[]{:S(2)}) async-start(), calls=%async_computation.11 | async-start | bytes 9437184 | tf_op jit(solution)/shard_map/reduce_scatter | solution.py:82
  458.4 18.7 %copy-start.73 = (bf16[1,2048,2048]{2,1,0:T(8,128)(2,1)S(1)}, bf16[1,2048,2048]{2,1,0:T(8,128)(2,1)}, u32[]{:S(2)}) copy-start(bf16[1,2048,2048]{2,1,0:T(8,128)(2,1)} %all-gather.8.cloned.1.call-done) | copy-start | bytes 25165828
  534.8 19.1 %copy-start.76 = (bf16[2048,1368]{0,1:T(8,128)(2,1)S(1)}, bf16[2048,1368]{0,1:T(8,128)(2,1)}, u32[]{:S(2)}) copy-start(bf16[2048,1368]{0,1:T(8,128)(2,1)} %get-tuple-element.54) | copy-start | bytes 16809988
  573.5 62.4 %copy-start.7 = (bf16[1,256,2048]{2,1,0:T(8,128)(2,1)S(1)}, bf16[1,256,2048]{2,1,0:T(8,128)(2,1)}, u32[]{:S(2)}) copy-start(bf16[1,256,2048]{2,1,0:T(8,128)(2,1)} %copy-done.6) | copy-start | bytes 3145732
  573.5 69.2 %copy-start.49 = (f32[2,2048]{1,0:T(2,128)S(1)}, f32[2,2048]{1,0:T(2,128)}, u32[]{:S(2)}) copy-start(f32[2,2048]{1,0:T(2,128)} %copy-done.48) | copy-start | bytes 49156
  573.5 117.6 %all-gather.12.cloned.1.call-start = ((), (), s32[]{:S(2)}) async-start(), calls=%async_computation.12 | async-start | bytes 9437184 | tf_op jit(solution)/shard_map/all_gather | solution.py:85
  642.6 269.1 %reduce-scatter.14.cloned.1.call-start = ((), (), s32[]{:S(2)}) async-start(), calls=%async_computation.13 | async-start | bytes 9437184 | tf_op jit(solution)/shard_map/reduce_scatter | solution.py:97
  731.8 22.1 %copy-start.28 = (bf16[2048,2,128]{2,0,1:T(8,128)(2,1)S(1)}, bf16[2048,2,128]{2,0,1:T(8,128)(2,1)}, u32[]{:S(2)}) copy-start(bf16[2048,2,128]{2,0,1:T(8,128)(2,1)} %convolution_convert_fusion.1) | copy-start | bytes 3145732
  754.0 26.2 %copy-start.3 = (pred[2048,2048]{0,1:T(8,128)(4,1)S(1)}, pred[2048,2048]{0,1:T(8,128)(4,1)}, u32[]{:S(2)}) copy-start(pred[2048,2048]{0,1:T(8,128)(4,1)} %iota_compare_fusion) | copy-start | bytes 12582916
  754.0 26.2 %copy-start.30 = (bf16[2048,2,32]{0,2,1:T(8,128)(2,1)S(1)}, bf16[2048,2,32]{0,2,1:T(8,128)(2,1)}, u32[]{:S(2)}) copy-start(bf16[2048,2,32]{0,2,1:T(8,128)(2,1)} %copy-done.29) | copy-start | bytes 786436
  754.0 26.2 %copy-start.32 = (bf16[2048,2,32]{0,2,1:T(8,128)(2,1)S(1)}, bf16[2048,2,32]{0,2,1:T(8,128)(2,1)}, u32[]{:S(2)}) copy-start(bf16[2048,2,32]{0,2,1:T(8,128)(2,1)} %copy-done.31) | copy-start | bytes 786436
  780.2 20.6 %copy-start.37 = (bf16[2048,32]{0,1:T(8,128)(2,1)S(1)}, bf16[2048,32]{0,1:T(8,128)(2,1)}, u32[]{:S(2)}) copy-start(bf16[2048,32]{0,1:T(8,128)(2,1)} %copy-done.36) | copy-start | bytes 393220
  780.2 20.6 %copy-start.39 = (bf16[2048,32]{0,1:T(8,128)(2,1)S(1)}, bf16[2048,32]{0,1:T(8,128)(2,1)}, u32[]{:S(2)}) copy-start(bf16[2048,32]{0,1:T(8,128)(2,1)} %copy-done.38) | copy-start | bytes 393220
  800.8 19.5 %copy-start.20 = (f32[2048,32]{0,1:T(8,128)S(1)}, f32[2048,32]{0,1:T(8,128)}, u32[]{:S(2)}) copy-start(f32[2048,32]{0,1:T(8,128)} %get-tuple-element.68) | copy-start | bytes 786436
  800.8 19.5 %copy-start.22 = (f32[2048,32]{0,1:T(8,128)S(1)}, f32[2048,32]{0,1:T(8,128)}, u32[]{:S(2)}) copy-start(f32[2048,32]{0,1:T(8,128)} %get-tuple-element.69) | copy-start | bytes 786436
  800.8 19.6 %copy-start.71 = (f32[32]{0:T(128)S(1)}, f32[32]{0:T(128)}, u32[]{:S(2)}) copy-start(f32[32]{0:T(128)} %copy-done.70) | copy-start | bytes 388
  800.8 20.9 %copy-start.17 = (bf16[2048,2,128]{2,0,1:T(8,128)(2,1)S(1)}, bf16[2048,2,128]{2,0,1:T(8,128)(2,1)}, u32[]{:S(2)}) copy-start(bf16[2048,2,128]{2,0,1:T(8,128)(2,1)} %fusion.88) | copy-start | bytes 3145732
  800.8 20.9 %copy-start.45 = (bf16[512,2,128]{2,1,0:T(2,128)(2,1)S(1)}, bf16[512,2,128]{2,1,0:T(2,128)(2,1)}, u32[]{:S(2)}) copy-start(bf16[512,2,128]{2,1,0:T(2,128)(2,1)} %param.19) | copy-start | bytes 786436
  849.4 128.6 %reduce-scatter.10.cloned.1.call-start = ((), (), s32[]{:S(2)}) async-start(), calls=%async_computation.9 | async-start | bytes 9437184 | tf_op jit(solution)/shard_map/reduce_scatter | solution.py:71
  868.5 43.3 %copy-start.5 = (bf16[1,256,2048]{2,1,0:T(8,128)(2,1)S(1)}, bf16[1,256,2048]{2,1,0:T(8,128)(2,1)}, u32[]{:S(2)}) copy-start(bf16[1,256,2048]{2,1,0:T(8,128)(2,1)} %reduce-scatter.6.cloned.1.call-done) | copy-start | bytes 3145732
  868.5 43.3 %copy-start.57 = (f32[2048]{0:T(1024)S(1)}, f32[2048]{0:T(1024)}, u32[]{:S(2)}) copy-start(f32[2048]{0:T(1024)} %param.22) | copy-start | bytes 24580
  868.5 43.3 %copy-start.65 = (f32[256]{0:T(256)S(1)}, f32[256]{0:T(256)}, u32[]{:S(2)}) copy-start(f32[256]{0:T(256)} %copy-done.64) | copy-start | bytes 3076
  868.5 45.6 %copy-start.67 = (f32[256]{0:T(256)S(1)}, f32[256]{0:T(256)}, u32[]{:S(2)}) copy-start(f32[256]{0:T(256)} %copy-done.66) | copy-start | bytes 3076
  868.5 109.5 %copy-start.51 = (f32[2048]{0:T(1024)S(1)}, f32[2048]{0:T(1024)}, u32[]{:S(2)}) copy-start(f32[2048]{0:T(1024)} %param.23) | copy-start | bytes 24580
  868.5 109.5 %copy-start.61 = (f32[256]{0:T(256)S(1)}, f32[256]{0:T(256)}, u32[]{:S(2)}) copy-start(f32[256]{0:T(256)} %copy-done.60) | copy-start | bytes 3076
  868.5 109.5 %copy-start.69 = (f32[256]{0:T(256)S(1)}, f32[256]{0:T(256)}, u32[]{:S(2)}) copy-start(f32[256]{0:T(256)} %copy-done.68) | copy-start | bytes 3076
  868.6 114.7 %copy-start.59 = (s32[1,2048]{1,0:T(1,128)S(1)}, s32[1,2048]{1,0:T(1,128)}, u32[]{:S(2)}) copy-start(s32[1,2048]{1,0:T(1,128)} %param.14) | copy-start | bytes 24580
  868.6 225.7 %all-gather.14.cloned.1.call-start = ((), (), s32[]{:S(2)}) async-start(), calls=%async_computation.14 | async-start | bytes 9437184 | tf_op jit(solution)/shard_map/all_gather | solution.py:113
  983.2 279.7 %all-reduce.11.cloned.1.call-start = ((), (), s32[]{:S(2)}) async-start(), calls=%async_computation.15 | async-start | bytes 9437184 | tf_op jit(solution)/shard_map/psum | solution.py:100
  987.7 37.4 %slice-start.4 = ((s8[5603328]{0:T(1024)(128)(4,1)}), s8[4194304]{0:T(1024)(128)(4,1)S(1)}, s32[]{:S(2)}) async-start(s8[5603328]{0:T(1024)(128)(4,1)} %bitcast.300), calls=%async_computation.20 | async-start | bytes 8388608
  987.7 56.4 %slice-start.2 = ((s8[8388608]{0:T(1024)(128)(4,1)}), s8[4194304]{0:T(1024)(128)(4,1)S(1)}, s32[]{:S(2)}) async-start(s8[8388608]{0:T(1024)(128)(4,1)} %bitcast.296), calls=%async_computation.18 | async-start | bytes 8388608
  1006.2 18.9 %slice-start.5 = ((s8[5603328]{0:T(1024)(128)(4,1)}), s8[1409024]{0:T(1024)(128)(4,1)S(1)}, s32[]{:S(2)}) async-start(s8[5603328]{0:T(1024)(128)(4,1)} %bitcast.300), calls=%async_computation.21 | async-start | bytes 2818048
  1006.2 38.0 %slice-start.3 = ((s8[8388608]{0:T(1024)(128)(4,1)}), s8[4194304]{0:T(1024)(128)(4,1)S(1)}, s32[]{:S(2)}) async-start(s8[8388608]{0:T(1024)(128)(4,1)} %bitcast.296), calls=%async_computation.19 | async-start | bytes 8388608
  1025.1 18.2 %copy-start.13 = (bf16[2048,2,128]{0,2,1:T(8,128)(2,1)S(1)}, bf16[2048,2,128]{0,2,1:T(8,128)(2,1)}, u32[]{:S(2)}) copy-start(bf16[2048,2,128]{0,2,1:T(8,128)(2,1)} %fusion.94) | copy-start | bytes 3145732
  1025.1 18.2 %copy-start.24 = (bf16[2048,512,1]{0,1,2:T(8,128)(2,1)S(1)}, bf16[2048,512,1]{0,1,2:T(8,128)(2,1)}, u32[]{:S(2)}) copy-start(bf16[2048,512,1]{0,1,2:T(8,128)(2,1)} %copy-done.23) | copy-start | bytes 6291460
  (46 other events, 253.1 us)
Sparse Core Ops, SparseCore 0:
  119.4 64.6 reduce-scatter.5
  189.4 48.3 all-gather.5
  343.6 62.2 reduce-scatter.7
  410.0 48.3 all-gather.7
  460.0 48.3 all-gather.9
  573.7 62.2 reduce-scatter.11
  642.8 48.3 all-gather.11
  849.5 62.2 reduce-scatter.13
  915.8 62.2 reduce-scatter.9
  983.3 48.4 all-gather.13
  1052.2 75.4 all-reduce.10
where the time goes:
time: 1280 us; the launch traced here: 1270 us
  waiting for transfers between devices  451 us (35%)
  matrix products  420 us (33%)
  other arithmetic  237 us (19%)
  local copies, waits for them, and re-layouts  128 us (10%)
  blocking collectives  22.8 us (2%)
  between operations  15.1 us (1%)
    dot_general x31, matrix products, matmul_f32(): return jnp.einsum(form, lhs, rhs, preferred_element_type=jnp.float32)  408 us
    scatter-add x3, other arithmetic, device_step(): jax.ops.segment_sum(de_full.reshape(-1, model_dim).astype(jnp.float32), s...  111 us
    gather x1, local copies, waits for them, and re-layouts, device_step(): rows = jnp.take(embed_table, jnp.where(owned, local_ids, 0), axis=0)  103 us
    reduce_scatter x1, waiting for transfers between devices, device_step(): embedded = lax.psum_scatter(rows, 'tp', scatter_dimension=1, tiled=True)  64.8 us
    reduce_scatter x1, waiting for transfers between devices, layer_pass(): mlp_loc = lax.psum_scatter(mlp_part, 'tp', scatter_dimension=1, tiled=True)  63.9 us
    reduce_scatter x1, waiting for transfers between devices, layer_pass(): lax.psum_scatter(attn_part, 'tp', scatter_dimension=1, tiled=True)  62.4 us
    reduce_scatter x1, waiting for transfers between devices, layer_pass(): lax.psum_scatter(dx_mlp_part, 'tp', scatter_dimension=1, tiled=True)  62.2 us
    convert_element_type x1, other arithmetic, device_step(): return (layer_out, d_table.astype(jnp.bfloat16)) + weight_grads  50.9 us
  transfers between devices with their start and end apart: 11, of which 9 were waited for; matrix products, arithmetic and copies ran while one was open for 25% of the time, Pallas kernels for 0%

commit v1 on v0

v1 whole, which is shorter than its diff:
```python
import functools

import jax
import jax.numpy as jnp
from jax import lax
from jax.experimental import pallas as pl
from jax.experimental.pallas import tpu as pltpu
from jax.sharding import PartitionSpec as P

EPSILON = 1e-6
ROPE_BASE = 10000.0
LOG2E = 1.4426950408889634
BLK = 256
RING = 16
F32 = jnp.float32
BF16 = jnp.bfloat16


def matmul_f32(form, lhs, rhs):
    return jnp.einsum(form, lhs, rhs, preferred_element_type=jnp.float32)


def dot_nn(a, b):
    return lax.dot_general(a, b, (((1,), (0,)), ((), ())), preferred_element_type=F32)


def dot_nt(a, b):
    return lax.dot_general(a, b, (((1,), (1,)), ((), ())), preferred_element_type=F32)


def rope_tables(seq_len, rope_dim):
    inv_freq = ROPE_BASE ** (-jnp.arange(0, rope_dim, 2, dtype=jnp.float32) / rope_dim)
    angles = jnp.arange(seq_len, dtype=jnp.float32)[:, None] * inv_freq[None, :]
    return jnp.cos(angles), jnp.sin(angles)


def apply_rope(x_in, cos_t, sin_t):
    half_dim = x_in.shape[-1] // 2
    x_lo = x_in[..., :half_dim]
    x_hi = x_in[..., half_dim:]
    return jnp.concatenate([x_lo * cos_t - x_hi * sin_t, x_hi * cos_t + x_lo * sin_t], axis=-1)


def unapply_rope(x_in, cos_t, sin_t):
    half_dim = x_in.shape[-1] // 2
    x_lo = x_in[..., :half_dim]
    x_hi = x_in[..., half_dim:]
    return jnp.concatenate([x_lo * cos_t + x_hi * sin_t, x_hi * cos_t - x_lo * sin_t], axis=-1)


def rms_norm(x_in, gain):
    inv_rms = lax.rsqrt(jnp.mean(x_in * x_in, axis=-1, keepdims=True) + EPSILON)
    return (x_in * inv_rms * gain).astype(jnp.bfloat16)


def kv_prep(latent, g_kv):
    value_a7 = g_kv.shape[0]
    cos_t, sin_t = rope_tables(latent.shape[0], latent.shape[-1] - value_a7)
    k_pe = apply_rope(latent[..., value_a7:], cos_t, sin_t).astype(jnp.bfloat16)
    return rms_norm(latent[..., :value_a7], g_kv), k_pe


def gather_body(slot_ref, pos_ref, cnt_ref, tab_ref, out_ref, buf, acc, sems):
    seq = acc.shape[0]
    cnt = cnt_ref[0]

    def fetch(k):
        blk = pl.multiple_of((slot_ref[k] // 8) * 8, 8)
        return pltpu.make_async_copy(tab_ref.at[pl.ds(blk, 8), :], buf.at[k % RING], sems.at[k % RING])

    def prime(k, c):
        fetch(k).start()
        return c

    lax.fori_loop(0, jnp.minimum(cnt, RING), prime, 0)

    def clear(i, c):
        acc[pl.ds(pl.multiple_of(i * 64, 64), 64), :] = jnp.zeros((64, acc.shape[1]), F32)
        return c

    lax.fori_loop(0, seq // 64, clear, 0)
    rows = lax.broadcasted_iota(jnp.int32, (8, acc.shape[1]), 0)

    def step(k, c):
        fetch(k).wait()
        blk = buf[k % RING].astype(F32)
        row = jnp.sum(jnp.where(rows == slot_ref[k] % 8, blk, 0.0), axis=0, keepdims=True)
        acc[pl.ds(pos_ref[k], 1), :] = row

        @pl.when(k + RING < cnt)
        def _():
            fetch(k + RING).start()

        return c

    lax.fori_loop(0, cnt, step, 0)

    def emit(i, c):
        at = pl.ds(pl.multiple_of(i * 64, 64), 64)
        out_ref[at, :] = acc[at, :].astype(BF16)
        return c

    lax.fori_loop(0, seq // 64, emit, 0)


def gather_rows(slots, pos, cnt, table, seq):
    dim = table.shape[1]
    return pl.pallas_call(
        gather_body,
        grid_spec=pltpu.PrefetchScalarGridSpec(
            num_scalar_prefetch=3,
            grid=(1,),
            in_specs=[pl.BlockSpec(memory_space=pl.ANY)],
            out_specs=pl.BlockSpec((seq, dim), lambda i, *_: (0, 0)),
            scratch_shapes=[pltpu.VMEM((RING, 8, dim), BF16), pltpu.VMEM((seq, dim), F32), pltpu.SemaphoreType.DMA((RING,))],
        ),
        out_shape=jax.ShapeDtypeStruct((seq, dim), BF16),
        compiler_params=pltpu.CompilerParams(vmem_limit_bytes=60 * 1024 * 1024),
        cost_estimate=pl.CostEstimate(flops=20_000_000_000, bytes_accessed=24_000_000, transcendentals=0),
        name="gather_rows",
    )(slots, pos, cnt, table)


def scatter_body(slot_ref, pos_ref, cnt_ref, de_ref, zero_ref, out_ref, wide, acc, stage, sems):
    seq = wide.shape[0]
    cnt = cnt_ref[0]

    def widen(i, c):
        at = pl.ds(pl.multiple_of(i * 64, 64), 64)
        wide[at, :] = de_ref[at, :].astype(F32)
        return c

    lax.fori_loop(0, seq // 64, widen, 0)

    def put(slot_blk, n):
        at = pl.multiple_of(slot_blk * 8, 8)
        return pltpu.make_async_copy(stage.at[n % RING], out_ref.at[pl.ds(at, 8), :], sems.at[n % RING])

    def step(k, carry):
        prev, n = carry
        slot = slot_ref[k]
        blk = slot // 8

        @pl.when(blk != prev)
        def _():
            acc[...] = jnp.zeros_like(acc)

        at = pl.ds(slot % 8, 1)
        acc[at, :] = acc[at, :] + wide[pl.ds(pos_ref[k], 1), :]
        last = slot_ref[k + 1] // 8 != blk

        @pl.when(last)
        def _():
            @pl.when(n >= RING)
            def _():
                put(blk, n).wait()

            stage[n % RING] = acc[...].astype(BF16)
            put(blk, n).start()

        return blk, n + last.astype(jnp.int32)

    _, total = lax.fori_loop(0, cnt, step, (jnp.int32(-1), jnp.int32(0)))

    def drain(i, c):
        put(0, i).wait()
        return c

    lax.fori_loop(jnp.maximum(total - RING, 0), total, drain, 0)


def scatter_rows(slots, pos, cnt, de, zeros):
    seq, dim = de.shape
    return pl.pallas_call(
        scatter_body,
        grid_spec=pltpu.PrefetchScalarGridSpec(
            num_scalar_prefetch=3,
            grid=(1,),
            in_specs=[pl.BlockSpec((seq, dim), lambda i, *_: (0, 0)), pl.BlockSpec(memory_space=pl.ANY)],
            out_specs=pl.BlockSpec(memory_space=pl.ANY),
            scratch_shapes=[pltpu.VMEM((seq, dim), F32), pltpu.VMEM((8, dim), F32), pltpu.VMEM((RING, 8, dim), BF16), pltpu.SemaphoreType.DMA((RING,))],
        ),
        out_shape=jax.ShapeDtypeStruct(zeros.shape, BF16),
        input_output_aliases={4: 0},
        compiler_params=pltpu.CompilerParams(vmem_limit_bytes=60 * 1024 * 1024),
        cost_estimate=pl.CostEstimate(flops=20_000_000_000, bytes_accessed=24_000_000, transcendentals=0),
        name="scatter_rows",
    )(slots, pos, cnt, de, zeros)


def attn_fwd_body(scale2, q_ref, k_ref, vt_ref, o_ref, lse_ref, s_scr):
    seq = q_ref.shape[1]
    tri = lax.broadcasted_iota(jnp.int32, (BLK, BLK), 0) <= lax.broadcasted_iota(jnp.int32, (BLK, BLK), 1)
    for i in range(seq // BLK):
        q_i = q_ref[0, i * BLK:(i + 1) * BLK, :]
        top = None
        for j in range(i + 1):
            s = dot_nt(k_ref[0, j * BLK:(j + 1) * BLK, :], q_i) * scale2
            if j == i:
                s = jnp.where(tri, s, -1e30)
            s_scr[j * BLK:(j + 1) * BLK, :] = s
            part = jnp.max(s.reshape(BLK // 8, 8, BLK), axis=0)
            top = part if top is None else jnp.maximum(top, part)
        top = jnp.max(top, axis=0, keepdims=True)
        den = None
        for j in range(i + 1):
            e = jnp.exp2(s_scr[j * BLK:(j + 1) * BLK, :] - top)
            s_scr[j * BLK:(j + 1) * BLK, :] = e
            part = jnp.sum(e.reshape(BLK // 8, 8, BLK), axis=0)
            den = part if den is None else den + part
        den = jnp.sum(den, axis=0, keepdims=True)
        inv = 1.0 / den
        out = None
        for j in range(i + 1):
            prob = (s_scr[j * BLK:(j + 1) * BLK, :] * inv).astype(BF16)
            part = dot_nn(vt_ref[0, :, j * BLK:(j + 1) * BLK], prob)
            out = part if out is None else out + part
        o_ref[i * BLK:(i + 1) * BLK, :] = out.T.astype(BF16)
        lse_ref[0, :, i * BLK:(i + 1) * BLK] = top + jnp.log2(den)


def attn_fwd(q, k, vt, scale):
    heads, seq, qk = q.shape
    vdim = vt.shape[1]
    return pl.pallas_call(
        functools.partial(attn_fwd_body, scale * LOG2E),
        grid=(heads,),
        in_specs=[pl.BlockSpec((1, seq, qk), lambda h: (h, 0, 0)), pl.BlockSpec((1, seq, qk), lambda h: (h, 0, 0)), pl.BlockSpec((1, vdim, seq), lambda h: (h, 0, 0))],
        out_specs=[pl.BlockSpec((seq, vdim), lambda h: (0, h)), pl.BlockSpec((1, 1, seq), lambda h: (h, 0, 0))],
        out_shape=[jax.ShapeDtypeStruct((seq, heads * vdim), BF16), jax.ShapeDtypeStruct((heads, 1, seq), F32)],
        scratch_shapes=[pltpu.VMEM((seq, BLK), F32)],
        compiler_params=pltpu.CompilerParams(vmem_limit_bytes=40 * 1024 * 1024),
        cost_estimate=pl.CostEstimate(flops=20_000_000_000, bytes_accessed=10_000_000, transcendentals=0),
        name="attn_fwd",
    )(q, k, vt)


def attn_bwd_body(scale2, scale, q_ref, k_ref, kt_ref, v_ref, do_ref, lse_ref, dlt_ref, dqt_ref, dk_ref, dv_ref, p_scr, ds_scr):
    seq = q_ref.shape[1]
    n = seq // BLK
    tri = lax.broadcasted_iota(jnp.int32, (BLK, BLK), 0) <= lax.broadcasted_iota(jnp.int32, (BLK, BLK), 1)
    for j in range(n):
        at_j = slice(j * BLK, (j + 1) * BLK)
        k_j = k_ref[0, at_j, :]
        v_j = v_ref[0, at_j, :]
        for i in range(j, n):
            at_i = slice(i * BLK, (i + 1) * BLK)
            s = dot_nt(k_j, q_ref[0, at_i, :])
            prob = jnp.exp2(s * scale2 - lse_ref[0, :, at_i])
            if i == j:
                prob = jnp.where(tri, prob, 0.0)
            dp = dot_nt(v_j, do_ref[at_i, :])
            p_scr[:, at_i] = prob.astype(BF16)
            ds_scr[at_j, at_i] = (prob * (dp - dlt_ref[0, :, at_i])).astype(BF16)
        dv_ref[0, at_j, :] = dot_nn(p_scr[:, j * BLK:], do_ref[j * BLK:, :]).astype(BF16)
        dk_ref[0, at_j, :] = dot_nn(ds_scr[at_j, j * BLK:], q_ref[0, j * BLK:, :]) * scale
    for i in range(n):
        at_i = slice(i * BLK, (i + 1) * BLK)
        dqt_ref[0, :, at_i] = dot_nn(kt_ref[0, :, :(i + 1) * BLK], ds_scr[:(i + 1) * BLK, at_i]) * scale


def attn_bwd(q, k, kt, v, do, lse, dlt, scale):
    heads, seq, qk = q.shape
    vdim = v.shape[2]
    per_head = lambda h: (h, 0, 0)
    return pl.pallas_call(
        functools.partial(attn_bwd_body, scale * LOG2E, scale),
        grid=(heads,),
        in_specs=[
            pl.BlockSpec((1, seq, qk), per_head),
            pl.BlockSpec((1, seq, qk), per_head),
            pl.BlockSpec((1, qk, seq), per_head),
            pl.BlockSpec((1, seq, vdim), per_head),
            pl.BlockSpec((seq, vdim), lambda h: (0, h)),
            pl.BlockSpec((1, 1, seq), per_head),
            pl.BlockSpec((1, 1, seq), per_head),
        ],
        out_specs=[pl.BlockSpec((1, qk, seq), per_head), pl.BlockSpec((1, seq, qk), per_head), pl.BlockSpec((1, seq, vdim), per_head)],
        out_shape=[jax.ShapeDtypeStruct((heads, qk, seq), F32), jax.ShapeDtypeStruct((heads, seq, qk), F32), jax.ShapeDtypeStruct((heads, seq, vdim), BF16)],
        scratch_shapes=[pltpu.VMEM((BLK, seq), BF16), pltpu.VMEM((seq, seq), BF16)],
        compiler_params=pltpu.CompilerParams(vmem_limit_bytes=56 * 1024 * 1024),
        cost_estimate=pl.CostEstimate(flops=50_000_000_000, bytes_accessed=16_000_000, transcendentals=0),
        name="attn_bwd",
    )(q, k, kt, v, do, lse, dlt)


def gather_seq(x):
    return lax.all_gather(x, 'tp', axis=0, tiled=True)


def scatter_seq(x):
    return lax.psum_scatter(x, 'tp', scatter_dimension=0, tiled=True)


def layer_pass(embedded, d_out, dy_full, w_q, w_dkv, g_kv, w_uk, w_uv, w_o, g_attn, g_mlp, w_gate, w_up, w_down):
    heads, qk = w_q.shape[1:]
    nope = w_uk.shape[2]
    vdim = w_uv.shape[2]
    scale = qk ** -0.5
    w_o2 = w_o.reshape(heads * vdim, -1)
    x_attn_loc, attn_norm_pull = jax.vjp(rms_norm, embedded.astype(F32), g_attn)
    x_attn = gather_seq(x_attn_loc)
    seq = x_attn.shape[0]
    cos_t, sin_t = rope_tables(seq, qk - nope)
    query = matmul_f32('sd,dhe->hse', x_attn, w_q).astype(BF16)
    latent = matmul_f32('sd,dc->sc', x_attn, w_dkv)
    (c_kv, k_pe), kv_pull = jax.vjp(kv_prep, latent, g_kv)
    k_nope = matmul_f32('sc,che->hse', c_kv, w_uk).astype(BF16)
    value = matmul_f32('sc,chv->hsv', c_kv, w_uv).astype(BF16)
    q_pe = apply_rope(query[..., nope:].astype(F32), cos_t, sin_t).astype(BF16)
    q_cat = jnp.concatenate([query[..., :nope], q_pe], axis=-1)
    k_cat = jnp.concatenate([k_nope, jnp.broadcast_to(k_pe[None], (heads,) + k_pe.shape)], axis=-1)
    attn_out, lse = attn_fwd(q_cat, k_cat, jnp.swapaxes(value, 1, 2), scale)
    attn_part = matmul_f32('sv,vd->sd', attn_out, w_o2).astype(BF16)
    attn_loc = scatter_seq(attn_part)
    residual = (embedded.astype(F32) + attn_loc.astype(F32)).astype(BF16)
    x_mlp_loc, mlp_norm_pull = jax.vjp(rms_norm, residual.astype(F32), g_mlp)
    x_mlp = gather_seq(x_mlp_loc)
    gate = matmul_f32('sd,df->sf', x_mlp, w_gate)
    up_proj = matmul_f32('sd,df->sf', x_mlp, w_up)
    gate_sig = jax.nn.sigmoid(gate)
    hidden = (gate * gate_sig * up_proj).astype(BF16)
    mlp_part = matmul_f32('sf,fd->sd', hidden, w_down).astype(BF16)
    mlp_loc = scatter_seq(mlp_part)
    layer_out = (residual.astype(F32) + mlp_loc.astype(F32)).astype(BF16)

    d_hidden = matmul_f32('sd,fd->sf', dy_full, w_down)
    dw_down = matmul_f32('sf,sd->fd', hidden, dy_full)
    d_up = (d_hidden * gate * gate_sig).astype(BF16)
    d_gate = (d_hidden * up_proj * gate_sig * (1.0 + gate * (1.0 - gate_sig))).astype(BF16)
    dw_gate = matmul_f32('sd,sf->df', x_mlp, d_gate)
    dw_up = matmul_f32('sd,sf->df', x_mlp, d_up)
    dx_mlp_part = (matmul_f32('sf,df->sd', d_gate, w_gate) + matmul_f32('sf,df->sd', d_up, w_up)).astype(BF16)
    dx_mlp = scatter_seq(dx_mlp_part)
    d_res_norm, dg_mlp_part = mlp_norm_pull(dx_mlp)
    d_residual = d_out.astype(F32) + d_res_norm
    d_attn_full = gather_seq(d_residual.astype(BF16))
    dw_o = matmul_f32('sv,sd->vd', attn_out, d_attn_full).reshape(w_o.shape)
    d_attn_out = matmul_f32('sd,vd->sv', d_attn_full, w_o2).astype(BF16)
    delta = jnp.sum((d_attn_out.astype(F32) * attn_out.astype(F32)).reshape(seq, heads, vdim), axis=-1).T.reshape(heads, 1, seq)
    d_qt, d_k, d_value = attn_bwd(q_cat, k_cat, jnp.swapaxes(k_cat, 1, 2), value, d_attn_out, lse, delta, scale)
    d_q = jnp.swapaxes(d_qt, 1, 2)
    d_query = jnp.concatenate([d_q[..., :nope], unapply_rope(d_q[..., nope:], cos_t, sin_t)], axis=-1).astype(BF16)
    d_knope = d_k[..., :nope].astype(BF16)
    d_kpe = jnp.sum(d_k[..., nope:], axis=0).astype(BF16)
    dw_uk = matmul_f32('sc,hse->che', c_kv, d_knope)
    dw_uv = matmul_f32('sc,hsv->chv', c_kv, d_value)
    d_ckv = (matmul_f32('hse,che->sc', d_knope, w_uk) + matmul_f32('hsv,chv->sc', d_value, w_uv)).astype(BF16)
    d_latent, dg_kv_part = kv_pull((d_ckv, d_kpe))
    d_latent = d_latent.astype(BF16)
    dw_q = matmul_f32('sd,hse->dhe', x_attn, d_query)
    dw_dkv_part = matmul_f32('sd,sc->dc', x_attn, d_latent)
    dx_attn_part = (matmul_f32('hse,dhe->sd', d_query, w_q) + matmul_f32('sc,dc->sd', d_latent, w_dkv)).astype(BF16)
    dx_attn = scatter_seq(dx_attn_part)
    d_emb_norm, dg_attn_part = attn_norm_pull(dx_attn)
    d_embed = (d_residual + d_emb_norm).astype(BF16)
    dw_dkv, dg_kv, dg_attn, dg_mlp = lax.psum((dw_dkv_part, dg_kv_part, dg_attn_part, dg_mlp_part), 'tp')
    return layer_out, d_embed, (dw_q, dw_dkv, dg_kv, dw_uk, dw_uv, dw_o, dg_attn, dg_mlp, dw_gate, dw_up, dw_down)


def solution(mesh):
    def device_step(tokens, embed_table, w_q, w_dkv, g_kv, w_uk, w_uv, w_o, g_attn, g_mlp, w_gate, w_up, w_down, d_out):
        vocab_local, model_dim = embed_table.shape
        seq = tokens.shape[1]
        dy_loc = d_out[0]
        dy_full = gather_seq(dy_loc)
        local_ids = tokens[0] - lax.axis_index('tp') * vocab_local
        owned = (local_ids >= 0) & (local_ids < vocab_local)
        slots, pos = lax.sort((jnp.where(owned, local_ids, vocab_local), lax.iota(jnp.int32, seq)), num_keys=1)
        slots = jnp.concatenate([slots, jnp.full((128,), vocab_local, jnp.int32)])
        cnt = jnp.sum(owned.astype(jnp.int32)).reshape(1)
        rows = gather_rows(slots, pos, cnt, embed_table, seq)
        embedded = scatter_seq(rows)
        layer_out, d_embed, weight_grads = layer_pass(embedded, dy_loc, dy_full, w_q, w_dkv, g_kv, w_uk, w_uv, w_o, g_attn, g_mlp, w_gate, w_up, w_down)
        de_full = gather_seq(d_embed)
        d_table = scatter_rows(slots, pos, cnt, de_full, jnp.zeros((vocab_local, model_dim), BF16))
        return (layer_out[None], d_table) + weight_grads

    row_spec = P('dp', 'tp', None)
    head_spec = P(None, 'tp', None)
    in_specs = (P('dp', None), P('tp', None), head_spec, P(None, None), P(None), head_spec, head_spec, P('tp', None, None), P(None), P(None), P(None, 'tp'), P(None, 'tp'), P('tp', None), row_spec)
    out_specs = (row_spec, P(('dp', 'tp'), None), P('dp', 'tp', None), P('dp', None), P('dp'), P('dp', 'tp', None), P('dp', 'tp', None), P(('dp', 'tp'), None, None), P('dp'), P('dp'), P('dp', 'tp'), P('dp', 'tp'), P(('dp', 'tp'), None))
    return jax.shard_map(device_step, mesh=mesh, in_specs=in_specs, out_specs=out_specs, check_vma=False)
```

time: 1280 us -> 963 us (0.75)
  other arithmetic: 237 us -> 58.1 us
  matrix products: 420 us -> 263 us
  Pallas kernels: 0 us -> 63.5 us
  local copies, waits for them, and re-layouts: 128 us -> 67.4 us
    dot_general x31 -> x21, matrix products: 408 us -> 245 us  [matmul_f32(): return jnp.einsum(form, lhs, rhs, preferred_element_type=jnp.float32)]
    scatter-add x3 -> x0, other arithmetic: 111 us -> none  [device_step(): jax.ops.segment_sum(de_full.reshape(-1, model_dim).astype(jnp.float32), s...]
    gather x1 -> x0, local copies, waits for them, and re-layouts: 103 us -> none  [device_step(): rows = jnp.take(embed_table, jnp.where(owned, local_ids, 0), axis=0)]
    convert_element_type x8 -> x6, other arithmetic: 80.3 us -> 12.9 us  [the longest x1 5.11 us: layer_pass(): d_embed = (d_residual + d_emb_norm).astype(BF16)]
    pallas_call x0 -> x4, Pallas kernels: none -> 63.5 us  [the longest x1 20.7 us: gather_rows(): pl.pallas_call(gather_body, grid_spec=pltpu.PrefetchScalarGridSpec(num_sc...]
    broadcast_in_dim x0 -> x2, local copies, waits for them, and re-layouts: none -> 16.9 us  [the longest x1 16.8 us: device_step(): jnp.zeros((vocab_local, model_dim), BF16)]
  transfers between devices with their start and end apart: 11 -> 11, of which waited for: 9 -> 10; matrix products, arithmetic and copies ran while one was open for 25% -> 17% of each run, Pallas kernels for 0% -> 2%
where the time goes in v1:
time: 963 us; the launch traced here: 952 us
  waiting for transfers between devices  461 us (48%)
  matrix products  263 us (27%)
  local copies, waits for them, and re-layouts  67.4 us (7%)
  Pallas kernels  63.5 us (7%)
  other arithmetic  58.1 us (6%)
  blocking collectives  22.9 us (2%)
  between operations  15 us (2%)
    reduce_scatter x5, waiting for transfers between devices, scatter_seq(): return lax.psum_scatter(x, 'tp', scatter_dimension=0, tiled=True)  298 us
    dot_general x21, matrix products, matmul_f32(): return jnp.einsum(form, lhs, rhs, preferred_element_type=jnp.float32)  245 us
    all_gather x5, waiting for transfers between devices, gather_seq(): return lax.all_gather(x, 'tp', axis=0, tiled=True)  159 us
    psum x1, blocking collectives, layer_pass(): lax.psum((dw_dkv_part, dg_kv_part, dg_attn_part, dg_mlp_part), 'tp')  22.9 us
    pallas_call x1, Pallas kernels, gather_rows(): pl.pallas_call(gather_body, grid_spec=pltpu.PrefetchScalarGridSpec(num_sc...  20.7 us
  transfers between devices with their start and end apart: 11, of which 10 were waited for; matrix products, arithmetic and copies ran while one was open for 17% of the time, Pallas kernels for 2%

profile of v1, /device:TPU:0, one launch (start us, length us, event | category | flops | bytes accessed | tf_op | source)
XLA Modules:
  0.0 952.0 jit_solution(13775413149089673867)
XLA Ops:
  8.7 5.0 sort.15
  14.4 20.7 %gather_rows.1 = bf16[2048,2048]{1,0:T(8,128)(2,1)} custom-call(s32[2176]{0:T(1024)} %concatenate.24.slot_ref, s32[2048]{0:T(1024)} %get-tuple-element.21.pos_ref, s32[1]{0:T(128)} %bitcast.1.cnt_ref, bf16[12800,2048]{1,0:T(8,128)(2,1)} %tab_ref.1), custom_call_target="tpu_custom_call" | custom-call | flops 20000000000 | bytes 24000000 | tf_op jit(solution)/shard_map/gather_rows/pallas_call | solution.py:108
  35.2 66.1 %reduce-scatter.6.cloned.1.call-done = bf16[256,2048]{1,0:T(8,128)(2,1)} async-done(((bf16[2048,2048]{1,0:T(8,128)(2,1)}), bf16[256,2048]{1,0:T(8,128)(2,1)}) %reduce-scatter.6.cloned.1.call-update) | async-done | bytes 1048592 | tf_op jit(solution)/shard_map/reduce_scatter | solution.py:292
  107.4 47.5 %all-gather.7.cloned.1.call-done = bf16[2048,2048]{1,0:T(8,128)(2,1)} async-done(((bf16[256,2048]{1,0:T(8,128)(2,1)}), bf16[2048,2048]{1,0:T(8,128)(2,1)}) %all-gather.7.cloned.1.call-update) | async-done | bytes 8388624 | tf_op jit(solution)/shard_map/all_gather | solution.py:288
  154.9 6.3 fusion.49
  162.7 3.7 copy.66
  171.3 7.5 fusion.50
  199.3 3.7 copy.73.k_ref
  203.1 3.3 subtract_convert_fusion.1
  208.3 10.5 %attn_fwd.1 = (bf16[2048,256]{1,0:T(8,128)(2,1)S(1)}, f32[2,1,2048]{2,1,0:T(1,128)S(1)}) custom-call(bf16[2,2048,192]{2,1,0:T(8,128)(2,1)S(1)} %pad_maximum_fusion.q_ref, bf16[2,2048,192]{2,1,0:T(8,128)(2,1)S(1)} %copy-done.3, bf16[2,128,2048]{2,1,0:T(8,128)(2,1)S(1)} %copy-done.5), custom_call_target="tpu_custom_call" | custom-call | flops 20000000000 | bytes 10000000 | tf_op jit(solution)/shard_map/attn_fwd/pallas_call | solution.py:225
  219.4 5.7 convolution_convert_fusion.1
  225.3 62.4 %reduce-scatter.8.cloned.1.call-done = bf16[256,2048]{1,0:T(8,128)(2,1)} async-done(((bf16[2048,2048]{1,0:T(8,128)(2,1)}), bf16[256,2048]{1,0:T(8,128)(2,1)}) %reduce-scatter.8.cloned.1.call-update) | async-done | bytes 1048592 | tf_op jit(solution)/shard_map/reduce_scatter | solution.py:292
  292.6 47.8 %all-gather.9.cloned.1.call-done = bf16[2048,2048]{1,0:T(8,128)(2,1)} async-done(((bf16[256,2048]{1,0:T(8,128)(2,1)}), bf16[2048,2048]{1,0:T(8,128)(2,1)}) %all-gather.9.cloned.1.call-update) | async-done | bytes 8388624 | tf_op jit(solution)/shard_map/all_gather | solution.py:288
  340.4 19.0 %fusion.52 = f32[2048,1368]{0,1:T(8,128)} fusion(bf16[2048,2048]{1,0:T(8,128)(2,1)} %all-gather.9.cloned.1.call-done, bf16[2048,1368]{0,1:T(8,128)(2,1)} %param.25), kind=kOutput, calls=%fused_computation.115 | convolution fusion | flops 11475615744 | bytes 25198592 | tf_op jit(solution)/shard_map/sd,df->sf/dot_general | solution.py:20
  359.4 15.6 %fusion.51 = f32[2048,1368]{0,1:T(8,128)} fusion(bf16[2048,2048]{1,0:T(8,128)(2,1)S(1)} %copy-done.46, bf16[2048,1368]{0,1:T(8,128)(2,1)} %param.24), kind=kOutput, calls=%fused_computation.114 | convolution fusion | flops 11475615744 | bytes 25198592 | tf_op jit(solution)/shard_map/sd,df->sf/dot_general | solution.py:20
  374.9 15.5 %all-gather.15.cloned.1.call-done = bf16[1,2048,2048]{2,1,0:T(8,128)(2,1)} async-done(((bf16[1,256,2048]{2,1,0:T(8,128)(2,1)}), bf16[1,2048,2048]{2,1,0:T(8,128)(2,1)}) %all-gather.15.cloned.1.call-update) | async-done | bytes 8388624 | tf_op jit(solution)/shard_map/all_gather | solution.py:288
  390.4 26.2 %multiply_convert_fusion = (bf16[2048,1368]{0,1:T(8,128)(2,1)}, bf16[2048,1368]{0,1:T(8,128)(2,1)}, bf16[2048,1368]{0,1:T(8,128)(2,1)}) fusion(f32[2048,1368]{0,1:T(8,128)} %fusion.51, f32[2048,1368]{0,1:T(8,128)} %fusion.52, bf16[1368,2048]{1,0:T(8,128)(2,1)} %param.26, bf16[1,2048,2048]{2,1,0:T(8,128)(2,1)} %all-gather.15.cloned.1.call-done), kind=kOutput, calls=%fused_computation.3 | convolution fusion | flops 11520442368 | bytes 53215232 | tf_op jit(solution)/shard_map/sd,fd->sf/dot_general | solution.py:20
  416.6 19.1 %fusion.53 = f32[2048,2048]{1,0:T(8,128)} fusion(bf16[2048,1368]{0,1:T(8,128)(2,1)} %get-tuple-element.78, bf16[2048,1368]{0,1:T(8,128)(2,1)} %param.24), kind=kOutput, calls=%fused_computation.116 | convolution fusion | flops 11475615744 | bytes 27983872 | tf_op jit(solution)/shard_map/sf,df->sd/dot_general | solution.py:20
  435.7 19.6 %add_convert_fusion = bf16[2048,2048]{1,0:T(8,128)(2,1)} fusion(f32[2048,2048]{1,0:T(8,128)} %fusion.53, bf16[2048,1368]{0,1:T(8,128)(2,1)S(1)} %copy-done.48, bf16[2048,1368]{0,1:T(8,128)(2,1)} %param.25), kind=kOutput, calls=%fused_computation.2 | convolution fusion | flops 11484004352 | bytes 36372480 | tf_op jit(solution)/shard_map/sf,df->sd/dot_general | solution.py:20
  455.7 62.1 %reduce-scatter.12.cloned.1.call-done = bf16[256,2048]{1,0:T(8,128)(2,1)} async-done(((bf16[2048,2048]{1,0:T(8,128)(2,1)}), bf16[256,2048]{1,0:T(8,128)(2,1)}) %reduce-scatter.12.cloned.1.call-update) | async-done | bytes 1048592 | tf_op jit(solution)/shard_map/reduce_scatter | solution.py:292
  521.0 3.5 fusion.40
  524.6 48.5 %all-gather.11.cloned.1.call-done = bf16[2048,2048]{1,0:T(8,128)(2,1)} async-done(((bf16[256,2048]{1,0:T(8,128)(2,1)}), bf16[2048,2048]{1,0:T(8,128)(2,1)}) %all-gather.11.cloned.1.call-update) | async-done | bytes 8388624 | tf_op jit(solution)/shard_map/all_gather | solution.py:288
  573.1 7.7 convert_multiply_fusion.14
  580.7 3.2 reshape.167
  584.0 4.7 reduce_sum.113
  589.6 16.0 %attn_bwd.1 = (f32[2,192,2048]{2,1,0:T(8,128)}, f32[2,2048,192]{2,1,0:T(8,128)}, bf16[2,2048,128]{2,1,0:T(8,128)(2,1)}) custom-call(bf16[2,2048,192]{2,1,0:T(8,128)(2,1)} %copy-done.4, bf16[2,2048,192]{2,1,0:T(8,128)(2,1)} %copy.73.k_ref, bf16[2,192,2048]{2,1,0:T(8,128)(2,1)} %get-tuple-element.86.kt_ref, bf16[2,2048,128]{2,1,0:T(8,128)(2,1)} %bitcast.104, ...), custom_call_target="tpu_custom_call" | custom-call | flops 49999998976 | bytes 16000000 | tf_op jit(solution)/shard_map/attn_bwd/pallas_call | solution.py:266
  608.4 4.4 fusion.33
  612.7 5.5 copy.78
  618.2 4.6 add_convert_fusion.2
  626.5 6.0 fusion.8
  635.0 10.4 %fusion.35 = f32[2048,2048]{1,0:T(8,128)} fusion(bf16[2048,576]{0,1:T(8,128)(2,1)S(1)} %copy-done, f32[2048,64]{0,1:T(8,128)S(1)} %pad_add_fusion, f32[2048,512]{0,1:T(8,128)S(1)} %add_add_fusion), kind=kOutput, calls=%fused_computation.82 | convolution fusion | flops 4834197504 | bytes 23855104 | tf_op jit(solution)/shard_map/sc,dc->sd/dot_general | solution.py:20
  647.4 10.3 %fusion = bf16[2048,2048]{1,0:T(8,128)(2,1)} fusion(f32[2048,2048]{1,0:T(8,128)} %fusion.35, bf16[2,2048,192]{2,1,0:T(8,128)(2,1)S(1)} %pad_maximum_fusion.1, bf16[2048,2,192]{0,2,1:T(8,128)(2,1)S(1)} %copy-done.47), kind=kOutput, calls=%fused_computation.1 | convolution fusion | flops 3229614080 | bytes 28311552 | tf_op jit(solution)/shard_map/hse,dhe->sd/dot_general | solution.py:20
  657.7 19.2 %convolution_convert_fusion = bf16[2048,2048]{1,0:T(8,128)(2,1)} fusion(bf16[2048,1368]{0,1:T(8,128)(2,1)} %get-tuple-element.79, bf16[1368,2048]{1,0:T(8,128)(2,1)} %param.26), kind=kOutput, calls=%fused_computation.11 | convolution fusion | flops 11479810048 | bytes 19595264 | tf_op jit(solution)/shard_map/sf,fd->sd/dot_general | solution.py:20
  677.0 43.0 %reduce-scatter.14.cloned.1.call-done = bf16[256,2048]{1,0:T(8,128)(2,1)} async-done(((bf16[2048,2048]{1,0:T(8,128)(2,1)}), bf16[256,2048]{1,0:T(8,128)(2,1)}) %reduce-scatter.14.cloned.1.call-update) | async-done | bytes 1048592 | tf_op jit(solution)/shard_map/reduce_scatter | solution.py:292
  722.3 64.0 %reduce-scatter.10.cloned.1.call-done = bf16[256,2048]{1,0:T(8,128)(2,1)} async-done(((bf16[2048,2048]{1,0:T(8,128)(2,1)}), bf16[256,2048]{1,0:T(8,128)(2,1)}) %reduce-scatter.10.cloned.1.call-update) | async-done | bytes 1048592 | tf_op jit(solution)/shard_map/reduce_scatter | solution.py:292
  786.3 5.1 fusion.20
  791.5 18.5 %fusion.56 = f32[2048,1368]{0,1:T(8,128)} fusion(bf16[2048,2048]{1,0:T(8,128)(2,1)} %all-gather.9.cloned.1.call-done, bf16[2048,1368]{0,1:T(8,128)(2,1)} %get-tuple-element.77), kind=kOutput, calls=%fused_computation.119 | convolution fusion | flops 11475615744 | bytes 25198592 | tf_op jit(solution)/shard_map/sd,sf->df/dot_general | solution.py:20
  810.0 18.7 %fusion.55 = f32[2048,1368]{0,1:T(8,128)} fusion(bf16[2048,2048]{1,0:T(8,128)(2,1)} %all-gather.9.cloned.1.call-done, bf16[2048,1368]{0,1:T(8,128)(2,1)} %get-tuple-element.78), kind=kOutput, calls=%fused_computation.118 | convolution fusion | flops 11475615744 | bytes 25198592 | tf_op jit(solution)/shard_map/sd,sf->df/dot_general | solution.py:20
  828.7 14.7 %fusion.1 = f32[1368,2048]{1,0:T(8,128)} fusion(bf16[2048,1368]{0,1:T(8,128)(2,1)S(1)} %bitcast.114, bf16[1,2048,2048]{2,1,0:T(8,128)(2,1)S(1)} %bitcast.110), kind=kOutput, calls=%fused_computation.7 | convolution fusion | flops 11475615744 | bytes 25198592 | tf_op jit(solution)/shard_map/sf,sd->fd/dot_general | solution.py:20
  843.4 4.2 copy.83
  853.8 10.1 %fusion.34 = f32[2048,576]{0,1:T(8,128)} fusion(bf16[2048,2048]{1,0:T(8,128)(2,1)} %all-gather.7.cloned.1.call-done, f32[2048,64]{0,1:T(8,128)S(1)} %copy-done.25, f32[2048,512]{0,1:T(8,128)S(1)} %copy-done.17), kind=kOutput, calls=%fused_computation.81 | convolution fusion | flops 4834197504 | bytes 17825792 | tf_op jit(solution)/shard_map/sd,sc->dc/dot_general | solution.py:20
  864.0 9.0 fusion.58
  873.0 7.1 fusion.54
  880.1 22.9 %all-reduce.5 = (f32[512]{0:T(512)}, f32[2048]{0:T(1024)}, f32[2048]{0:T(1024)}) all-reduce(f32[512]{0:T(512)S(1)} %copy-done.43, f32[2048]{0:T(1024)S(1)} %get-tuple-element.70, f32[2048]{0:T(1024)S(1)} %copy-done.36), channel_id=1, replica_groups=mesh['dp'=1,'tp'=8] {'tp'}, use_global_device_ids=true, to_apply=%region_17.18 | all-reduce | flops 4608 | bytes 36864 | tf_op jit(solution)/shard_map/psum | solution.py:357
  903.0 16.8 %broadcast_in_dim.19.zero_ref = bf16[12800,2048]{1,0:T(8,128)(2,1)} broadcast(bf16[]{:T(256)} %constant.39.clone.1), dimensions={} | broadcast | bytes 52428800 | tf_op jit(solution)/shard_map/broadcast_in_dim | solution.py:376
  919.9 16.3 %scatter_rows.1 = bf16[12800,2048]{1,0:T(8,128)(2,1)} custom-call(s32[2176]{0:T(1024)} %concatenate.24.slot_ref, s32[2048]{0:T(1024)} %get-tuple-element.21.pos_ref, s32[1]{0:T(128)} %bitcast.1.cnt_ref, bf16[2048,2048]{1,0:T(8,128)(2,1)} %all-gather.13.cloned.1.call-done.de_ref, ...), custom_call_target="tpu_custom_call", output_to_operand_aliasing={{}: (4, {})} | custom-call | flops 20000000000 | bytes 24000000 | tf_op jit(solution)/shard_map/scatter_rows/pallas_call | solution.py:174
  936.1 3.8 all-reduce.8.cloned.1.call-done
  940.0 5.1 copy.99
  (184 shorter events, 66.4 us)
Async XLA Ops:
  7.2 164.1 %copy-start = (bf16[2048,576]{0,1:T(8,128)(2,1)S(1)}, bf16[2048,576]{0,1:T(8,128)(2,1)}, u32[]{:S(2)}) copy-start(bf16[2048,576]{0,1:T(8,128)(2,1)} %param.17) | copy-start | bytes 7077892
  7.2 94.1 %reduce-scatter.6.cloned.1.call-start = ((), (), s32[]{:S(2)}) async-start(), calls=%async_computation.5 | async-start | bytes 9437184 | tf_op jit(solution)/shard_map/reduce_scatter | solution.py:292
  35.1 68.9 %copy-start.34 = (f32[2048]{0:T(1024)S(1)}, f32[2048]{0:T(1024)}, u32[]{:S(2)}) copy-start(f32[2048]{0:T(1024)} %param.22) | copy-start | bytes 24580
  35.1 71.4 %copy-start.28 = (bf16[512,2,128]{2,1,0:T(2,128)(2,1)S(1)}, bf16[512,2,128]{2,1,0:T(2,128)(2,1)}, u32[]{:S(2)}) copy-start(bf16[512,2,128]{2,1,0:T(2,128)(2,1)} %param.19) | copy-start | bytes 786436
  35.1 119.8 %all-gather.7.cloned.1.call-start = ((), (), s32[]{:S(2)}) async-start(), calls=%async_computation.6 | async-start | bytes 9437184 | tf_op jit(solution)/shard_map/all_gather | solution.py:288
  106.5 181.1 %reduce-scatter.8.cloned.1.call-start = ((), (), s32[]{:S(2)}) async-start(), calls=%async_computation.7 | async-start | bytes 9437184 | tf_op jit(solution)/shard_map/reduce_scatter | solution.py:292
  107.4 71.8 %copy-start.44 = (f32[32]{0:T(128)}, f32[32]{0:T(128)S(1)}, u32[]{:S(2)}) copy-start(f32[32]{0:T(128)S(1)} %multiply_power_fusion) | copy-start | bytes 388
  178.8 7.8 copy-start.37
  181.0 8.2 copy-start.30
  184.1 18.9 %copy-start.12 = (f32[2048,32]{1,0:T(8,128)}, f32[2048,32]{1,0:T(8,128)S(1)}, u32[]{:S(2)}) copy-start(f32[2048,32]{1,0:T(8,128)S(1)} %copy.68) | copy-start | bytes 786436
  208.3 10.6 %copy-start.4 = (bf16[2,2048,192]{2,1,0:T(8,128)(2,1)}, bf16[2,2048,192]{2,1,0:T(8,128)(2,1)S(1)}, u32[]{:S(2)}) copy-start(bf16[2,2048,192]{2,1,0:T(8,128)(2,1)S(1)} %pad_maximum_fusion.q_ref) | copy-start | bytes 4718596
  208.3 11.2 %copy-start.22 = (bf16[2,128,2048]{2,1,0:T(8,128)(2,1)S(1)}, bf16[2,128,2048]{2,1,0:T(8,128)(2,1)}, u32[]{:S(2)}) copy-start(bf16[2,128,2048]{2,1,0:T(8,128)(2,1)} %param.21) | copy-start | bytes 3145732
  219.4 353.6 %copy-start.1 = (bf16[2048,256]{1,0:T(8,128)(2,1)}, bf16[2048,256]{1,0:T(8,128)(2,1)S(1)}, u32[]{:S(2)}) copy-start(bf16[2048,256]{1,0:T(8,128)(2,1)S(1)} %get-tuple-element.22) | copy-start | bytes 3145732
  225.2 65.4 %copy-start.29 = (f32[2048]{0:T(1024)S(1)}, f32[2048]{0:T(1024)}, u32[]{:S(2)}) copy-start(f32[2048]{0:T(1024)} %param.23) | copy-start | bytes 24580
  225.2 115.2 %all-gather.9.cloned.1.call-start = ((), (), s32[]{:S(2)}) async-start(), calls=%async_computation.8 | async-start | bytes 9437184 | tf_op jit(solution)/shard_map/all_gather | solution.py:288
  291.9 98.5 %all-gather.15.cloned.1.call-start = ((), (), s32[]{:S(2)}) async-start(), calls=%async_computation.15 | async-start | bytes 9437184 | tf_op jit(solution)/shard_map/all_gather | solution.py:288
  292.5 225.3 %reduce-scatter.12.cloned.1.call-start = ((), (), s32[]{:S(2)}) async-start(), calls=%async_computation.10 | async-start | bytes 9437184 | tf_op jit(solution)/shard_map/reduce_scatter | solution.py:292
  340.4 19.0 %copy-start.46 = (bf16[2048,2048]{1,0:T(8,128)(2,1)S(1)}, bf16[2048,2048]{1,0:T(8,128)(2,1)}, u32[]{:S(2)}) copy-start(bf16[2048,2048]{1,0:T(8,128)(2,1)} %all-gather.9.cloned.1.call-done) | copy-start | bytes 25165828
  416.6 19.1 %copy-start.48 = (bf16[2048,1368]{0,1:T(8,128)(2,1)S(1)}, bf16[2048,1368]{0,1:T(8,128)(2,1)}, u32[]{:S(2)}) copy-start(bf16[2048,1368]{0,1:T(8,128)(2,1)} %get-tuple-element.77) | copy-start | bytes 16809988
  455.4 117.6 %all-gather.11.cloned.1.call-start = ((), (), s32[]{:S(2)}) async-start(), calls=%async_computation.11 | async-start | bytes 9437184 | tf_op jit(solution)/shard_map/all_gather | solution.py:288
  524.5 195.5 %reduce-scatter.14.cloned.1.call-start = ((), (), s32[]{:S(2)}) async-start(), calls=%async_computation.12 | async-start | bytes 9437184 | tf_op jit(solution)/shard_map/reduce_scatter | solution.py:292
  589.6 18.8 %copy-start.20 = (bf16[512,2,128]{0,2,1:T(8,128)(2,1)S(1)}, bf16[512,2,128]{0,2,1:T(8,128)(2,1)}, u32[]{:S(2)}) copy-start(bf16[512,2,128]{0,2,1:T(8,128)(2,1)} %copy.70) | copy-start | bytes 786436
  618.2 8.3 copy-start.31
  618.2 8.3 copy-start.38
  626.5 7.3 slice-start
  626.5 6.0 copy-start.33
  626.5 6.0 copy-start.21
  626.5 6.1 copy-start.45
  626.5 7.3 slice-start.1
  634.9 10.5 %copy-start.16 = (f32[2048,512]{0,1:T(8,128)}, f32[2048,512]{0,1:T(8,128)S(1)}, u32[]{:S(2)}) copy-start(f32[2048,512]{0,1:T(8,128)S(1)} %add_add_fusion) | copy-start | bytes 12582916
  634.9 10.4 %copy-start.24 = (f32[2048,64]{0,1:T(8,128)}, f32[2048,64]{0,1:T(8,128)S(1)}, u32[]{:S(2)}) copy-start(f32[2048,64]{0,1:T(8,128)S(1)} %pad_add_fusion) | copy-start | bytes 1572868
  635.0 10.4 %copy-start.18 = (bf16[2,2048,32]{2,1,0:T(8,128)(2,1)S(1)}, bf16[2,2048,32]{2,1,0:T(8,128)(2,1)}, u32[]{:S(2)}) copy-start(bf16[2,2048,32]{2,1,0:T(8,128)(2,1)} %get-tuple-element.80) | copy-start | bytes 786436
  635.0 10.4 %copy-start.19 = (bf16[2,2048,32]{2,1,0:T(8,128)(2,1)S(1)}, bf16[2,2048,32]{2,1,0:T(8,128)(2,1)}, u32[]{:S(2)}) copy-start(bf16[2,2048,32]{2,1,0:T(8,128)(2,1)} %get-tuple-element.81) | copy-start | bytes 786436
  657.7 128.6 %reduce-scatter.10.cloned.1.call-start = ((), (), s32[]{:S(2)}) async-start(), calls=%async_computation.9 | async-start | bytes 9437184 | tf_op jit(solution)/shard_map/reduce_scatter | solution.py:292
  676.9 43.1 %copy-start.8 = (bf16[256,2048]{1,0:T(8,128)(2,1)S(1)}, bf16[256,2048]{1,0:T(8,128)(2,1)}, u32[]{:S(2)}) copy-start(bf16[256,2048]{1,0:T(8,128)(2,1)} %reduce-scatter.6.cloned.1.call-done) | copy-start | bytes 3145732
  676.9 43.1 %copy-start.35 = (f32[2048]{0:T(1024)S(1)}, f32[2048]{0:T(1024)}, u32[]{:S(2)}) copy-start(f32[2048]{0:T(1024)} %param.22) | copy-start | bytes 24580
  677.0 43.1 %copy-start.40 = (f32[256]{0:T(256)S(1)}, f32[256]{0:T(256)}, u32[]{:S(2)}) copy-start(f32[256]{0:T(256)} %copy-done.39) | copy-start | bytes 3076
  677.0 45.4 %copy-start.42 = (f32[256]{0:T(256)S(1)}, f32[256]{0:T(256)}, u32[]{:S(2)}) copy-start(f32[256]{0:T(256)} %copy-done.41) | copy-start | bytes 3076
  677.0 226.0 %all-gather.13.cloned.1.call-start = ((), (), s32[]{:S(2)}) async-start(), calls=%async_computation.13 | async-start | bytes 9437184 | tf_op jit(solution)/shard_map/all_gather | solution.py:288
  791.4 148.5 %all-reduce.8.cloned.1.call-start = ((), (), s32[]{:S(2)}) async-start(), calls=%async_computation.14 | async-start | bytes 9437184 | tf_op jit(solution)/shard_map/psum | solution.py:357
  791.5 37.2 %slice-start.2 = ((s8[8388608]{0:T(1024)(128)(4,1)}), s8[4194304]{0:T(1024)(128)(4,1)S(1)}, s32[]{:S(2)}) async-start(s8[8388608]{0:T(1024)(128)(4,1)} %bitcast.109), calls=%async_computation.18 | async-start | bytes 8388608
  791.5 37.1 %slice-start.4 = ((s8[5603328]{0:T(1024)(128)(4,1)}), s8[4194304]{0:T(1024)(128)(4,1)S(1)}, s32[]{:S(2)}) async-start(s8[5603328]{0:T(1024)(128)(4,1)} %bitcast.113), calls=%async_computation.20 | async-start | bytes 8388608
  810.0 18.7 %slice-start.3 = ((s8[8388608]{0:T(1024)(128)(4,1)}), s8[4194304]{0:T(1024)(128)(4,1)S(1)}, s32[]{:S(2)}) async-start(s8[8388608]{0:T(1024)(128)(4,1)} %bitcast.109), calls=%async_computation.19 | async-start | bytes 8388608
  810.0 18.7 %slice-start.5 = ((s8[5603328]{0:T(1024)(128)(4,1)}), s8[1409024]{0:T(1024)(128)(4,1)S(1)}, s32[]{:S(2)}) async-start(s8[5603328]{0:T(1024)(128)(4,1)} %bitcast.113), calls=%async_computation.21 | async-start | bytes 2818048
  843.4 8.5 copy-start.23
  864.0 9.0 copy-start.2
  873.0 7.1 copy-start.36
  873.0 7.1 copy-start.43
  (18 other events, 42.6 us)
Sparse Core Ops, SparseCore 0:
  35.2 66.0 reduce-scatter.5
  106.6 48.3 all-gather.6
  225.3 62.2 reduce-scatter.7
  292.0 48.3 all-gather.8
  342.1 48.3 all-gather.14
  455.5 62.2 reduce-scatter.11
  524.7 48.3 all-gather.10
  657.8 62.2 reduce-scatter.13
  724.0 62.2 reduce-scatter.9
  791.6 48.3 all-gather.12
  864.1 75.8 all-reduce.7

commit v2 on v1

--- a/solution.py
+++ b/solution.py
@@ -284,6 +284,456 @@
     )(q, k, kt, v, do, lse, dlt)
 
 
+HALF = 128
+SHARD = 256
+MESH = pl.DeviceIdType.MESH
+
+
+def xor_bits(t, u):
+    out = 0
+    for b in (1, 2, 4):
+        tb = (t // b) % 2
+        ub = (u // b) % 2
+        out = out + b * (tb + ub - 2 * tb * ub)
+    return out
+
+
+def greet(t):
+    peers = [xor_bits(t, u) for u in (1, 2, 4)]
+    barrier = pltpu.get_barrier_semaphore()
+    for peer in peers:
+        pl.semaphore_signal(barrier, inc=1, device_id={'tp': peer}, device_id_type=MESH)
+    pl.semaphore_wait(barrier, 3)
+    return peers
+
+
+def half_rows(shard, half):
+    return pl.ds(pl.multiple_of(shard * SHARD + half * HALF, HALF), HALF)
+
+
+def ag_unit(i):
+    p = i // 4
+    r = i % 4
+    p0 = (3 - p) // 3
+    p3 = p // 3
+    mid = 1 - p0 - p3
+    u = p0 * (r // 2) + mid * (2 + (r % 2) * 2 + r // 2) + p3 * (6 + r // 2)
+    flip = (p - 1) * mid
+    return u, (r % 2) + flip * (1 - 2 * (r % 2))
+
+
+def ag_run(x_ref, full, send, recv, compute):
+    t = lax.axis_index('tp')
+    partner, xn, yn = greet(t)
+
+    def copy(src, shard, half, sem, u_there, dev):
+        return pltpu.make_async_remote_copy(
+            src_ref=src, dst_ref=full.at[half_rows(shard, half), :], send_sem=send.at[sem],
+            recv_sem=recv.at[u_there, half], device_id={'tp': dev}, device_id_type=MESH)
+
+    def mine(half):
+        return x_ref.at[pl.ds(half * HALF, HALF), :]
+
+    def held(u, half):
+        return full.at[half_rows(xor_bits(t, u), half), :]
+
+    own = [copy(mine(0), t, 0, 0, 2, xn), copy(mine(1), t, 1, 3, 4, yn), copy(mine(0), t, 0, 4, 1, partner), copy(mine(1), t, 1, 5, 1, partner),
+           copy(mine(1), t, 1, 1, 2, xn), copy(mine(0), t, 0, 2, 4, yn)]
+    for c in own:
+        c.start()
+    full[pl.ds(pl.multiple_of(t * SHARD, SHARD), SHARD), :] = x_ref[...]
+    fwd_y = copy(held(2, 0), xor_bits(t, 2), 0, 6, 6, yn)
+    fwd_x = copy(held(4, 1), xor_bits(t, 4), 1, 7, 6, xn)
+    fwd_p = {(u, h): copy(held(u, h), xor_bits(t, u), h, 8 + (u - 2) + h, u + 1, partner) for u in (2, 4, 6) for h in (0, 1)}
+
+    def arrive(u, h):
+        copy(held(u, h), xor_bits(t, u), h, 0, u, partner).wait_recv()
+
+    def step(i, carry):
+        @pl.when(i == 2)
+        def _():
+            arrive(1, 0)
+            arrive(1, 1)
+
+        @pl.when(i == 4)
+        def _():
+            arrive(2, 0)
+            fwd_y.start()
+            fwd_p[2, 0].start()
+            arrive(4, 1)
+            fwd_x.start()
+            fwd_p[4, 1].start()
+
+        @pl.when(i == 6)
+        def _():
+            arrive(3, 0)
+            arrive(5, 1)
+
+        @pl.when(i == 8)
+        def _():
+            arrive(2, 1)
+            fwd_p[2, 1].start()
+            arrive(4, 0)
+            fwd_p[4, 0].start()
+
+        @pl.when(i == 10)
+        def _():
+            arrive(3, 1)
+            arrive(5, 0)
+
+        @pl.when(i == 12)
+        def _():
+            arrive(6, 0)
+            fwd_p[6, 0].start()
+            arrive(6, 1)
+            fwd_p[6, 1].start()
+
+        @pl.when(i == 14)
+        def _():
+            arrive(7, 0)
+            arrive(7, 1)
+
+        u, h = ag_unit(i)
+        compute(i, xor_bits(t, u), h)
+        return carry
+
+    lax.fori_loop(0, 16, step, 0)
+    for c in own + [fwd_y, fwd_x] + list(fwd_p.values()):
+        c.wait_send()
+
+
+AG_SEMS = [pltpu.SemaphoreType.DMA((14,)), pltpu.SemaphoreType.DMA((8, 2))]
+
+
+def rs_unit(i):
+    p = i // 2
+    p0 = (1 - p % 2) * (1 - p // 2)
+    p1 = (p % 2) * (1 - p // 2)
+    p2 = (p // 2) * (1 - p % 2)
+    return p0 * 6 + p1 * 2 + p2 * 4 + 1 - i % 2
+
+
+def rs_run(stage, fp, fx, fy, send, recv, produce, finish):
+    t = lax.axis_index('tp')
+    partner, xn, yn = greet(t)
+
+    def copy(src, dst, sem, dev):
+        return pltpu.make_async_remote_copy(src_ref=src, dst_ref=dst, send_sem=send.at[sem], recv_sem=recv.at[sem], device_id={'tp': dev}, device_id_type=MESH)
+
+    def half(h):
+        return pl.ds(h * HALF, HALF)
+
+    sx = [copy(stage.at[1, half(1), :], fx.at[0], 4, xn), copy(stage.at[3, half(1), :], fx.at[1], 5, xn), copy(stage.at[3, half(0), :], fx.at[2], 6, xn)]
+    sy = [copy(stage.at[1, half(0), :], fy.at[0], 7, yn), copy(stage.at[5, half(0), :], fy.at[1], 8, yn), copy(stage.at[5, half(1), :], fy.at[2], 9, yn)]
+
+    def add(i, first, count, src, src_first):
+        def body(r, c):
+            a = pl.ds(pl.multiple_of(first + r * 32, 32), 32)
+            b = pl.ds(pl.multiple_of(src_first + r * 32, 32), 32)
+            stage[i, a, :] = (stage[i, a, :].astype(F32) + src[b, :].astype(F32)).astype(BF16)
+            return c
+
+        lax.fori_loop(0, count // 32, body, 0)
+
+    def step(i, carry):
+        p = i // 2
+        produce(i, xor_bits(t, rs_unit(i)))
+        to_partner = copy(stage.at[i], fp.at[p], p, partner)
+
+        @pl.when(i % 2 == 0)
+        def _():
+            to_partner.start()
+
+        @pl.when(i % 2 == 1)
+        def _():
+            to_partner.wait_recv()
+            add(i, 0, SHARD, fp.at[p], 0)
+
+        @pl.when(i == 1)
+        def _():
+            sx[0].start()
+            sy[0].start()
+
+        @pl.when(i == 3)
+        def _():
+            sx[1].start()
+
+        @pl.when(i == 5)
+        def _():
+            sy[1].start()
+            sy[0].wait_recv()
+            add(3, 0, HALF, fy.at[0], 0)
+            sx[2].start()
+            sx[0].wait_recv()
+            add(5, HALF, HALF, fx.at[0], 0)
+            sy[2].start()
+
+        return carry
+
+    lax.fori_loop(0, 8, step, 0)
+    sy[1].wait_recv()
+    sx[1].wait_recv()
+    sx[2].wait_recv()
+    sy[2].wait_recv()
+
+    def last(r, c):
+        lo = pl.ds(pl.multiple_of(r * 32, 32), 32)
+        hi = pl.ds(pl.multiple_of(HALF + r * 32, 32), 32)
+        finish(lo, (stage[7, lo, :].astype(F32) + fy[1, lo, :].astype(F32)) + fx[2, lo, :].astype(F32))
+        finish(hi, (stage[7, hi, :].astype(F32) + fx[1, lo, :].astype(F32)) + fy[2, lo, :].astype(F32))
+        return c
+
+    lax.fori_loop(0, HALF // 32, last, 0)
+    for q in range(4):
+        copy(stage.at[2 * q], fp.at[q], q, partner).wait_send()
+    for c in sx + sy:
+        c.wait_send()
+
+
+def rs_scratch(dim):
+    return [pltpu.VMEM((8, SHARD, dim), BF16), pltpu.VMEM((4, SHARD, dim), BF16), pltpu.VMEM((3, HALF, dim), BF16), pltpu.VMEM((3, HALF, dim), BF16),
+            pltpu.SemaphoreType.DMA((10,)), pltpu.SemaphoreType.DMA((10,))]
+
+
+VM = pl.BlockSpec(memory_space=pltpu.VMEM)
+ANY = pl.BlockSpec(memory_space=pl.ANY)
+
+
+def comm_call(body, name, cid, in_specs, out_specs, out_shape, scratch, flops):
+    return pl.pallas_call(
+        body, name=name, in_specs=in_specs, out_specs=out_specs, out_shape=out_shape, scratch_shapes=scratch,
+        compiler_params=pltpu.CompilerParams(collective_id=cid, has_side_effects=True, vmem_limit_bytes=60 * 1024 * 1024),
+        cost_estimate=pl.CostEstimate(flops=flops, bytes_accessed=20_000_000, transcendentals=0),
+    )
+
+
+def rs_rows(rows):
+    seq, dim = rows.shape
+
+    def body(rows_ref, out_ref, stage, fp, fx, fy, send, recv, load):
+        t = lax.axis_index('tp')
+
+        def fetch(i):
+            at = pl.ds(pl.multiple_of(xor_bits(t, rs_unit(i)) * SHARD, SHARD), SHARD)
+            return pltpu.make_async_copy(rows_ref.at[at, :], stage.at[i], load.at[i])
+
+        for i in range(8):
+            fetch(i).start()
+
+        def finish(at, val):
+            out_ref[at, :] = val.astype(BF16)
+
+        rs_run(stage, fp, fx, fy, send, recv, lambda i, s: fetch(i).wait(), finish)
+
+    return comm_call(body, 'rs_rows', 0, [ANY], VM, jax.ShapeDtypeStruct((SHARD, dim), BF16), rs_scratch(dim) + [pltpu.SemaphoreType.DMA((8,))], 40_000_000_000)(rows)
+
+
+def ag_proj(x, w_q, w_dkv):
+    dim = x.shape[1]
+    seq = 8 * SHARD
+    heads, _, qk = w_q.shape
+    lat = w_dkv.shape[1]
+
+    def body(x_ref, wq_ref, wl_ref, x_out, q_ref, l_ref, full, send, recv, sem):
+        def compute(i, s, h):
+            at = half_rows(s, h)
+            pltpu.make_async_copy(full.at[at, :], x_out.at[at, :], sem.at[i]).start()
+            x_b = full[at, :]
+            for hd in range(heads):
+                q_ref[hd, at, :] = dot_nn(x_b, wq_ref[hd]).astype(BF16)
+            l_ref[at, :] = dot_nn(x_b, wl_ref[...])
+
+        ag_run(x_ref, full, send, recv, compute)
+        for i in range(16):
+            at = half_rows(i // 2, i % 2)
+            pltpu.make_async_copy(full.at[at, :], x_out.at[at, :], sem.at[i]).wait()
+
+    return comm_call(body, 'ag_proj', 1, [VM, VM, VM], [ANY, VM, VM],
+                     [jax.ShapeDtypeStruct((seq, dim), BF16), jax.ShapeDtypeStruct((heads, seq, qk), BF16), jax.ShapeDtypeStruct((seq, lat), F32)],
+                     [pltpu.VMEM((seq, dim), BF16)] + AG_SEMS + [pltpu.SemaphoreType.DMA((16,))], 40_000_000_000)(x, w_q, w_dkv)
+
+
+def attn_out_rs(o, w_o):
+    dim = w_o.shape[1]
+
+    def body(o_ref, w_ref, out_ref, stage, fp, fx, fy, send, recv):
+        def produce(i, s):
+            o_b = o_ref[pl.ds(pl.multiple_of(s * SHARD, SHARD), SHARD), :]
+            for n in range(dim // 256):
+                cols = slice(n * 256, (n + 1) * 256)
+                stage[i, :, cols] = dot_nn(o_b, w_ref[:, cols]).astype(BF16)
+
+        def finish(at, val):
+            out_ref[at, :] = val.astype(BF16)
+
+        rs_run(stage, fp, fx, fy, send, recv, produce, finish)
+
+    return comm_call(body, 'attn_out_rs', 2, [VM, VM], VM, jax.ShapeDtypeStruct((SHARD, dim), BF16), rs_scratch(dim), 40_000_000_000)(o, w_o)
+
+
+def col_tiles(width):
+    return [slice(a, min(a + 256, width)) for a in range(0, width, 256)]
+
+
+def ag_mlp(z, dy, w_gate, w_up, w_down):
+    dim = z.shape[1]
+    seq = 8 * SHARD
+    ffn = w_gate.shape[1]
+    tiles = col_tiles(ffn)
+
+    def body(z_ref, dy_ref, wg_hbm, wu_hbm, wd_hbm, z_out, hid_out, dg_out, du_out, full, wg, wu, wd, dyb, st, send, recv, zsem, wsem, dsem, osem):
+        t = lax.axis_index('tp')
+        loads = [pltpu.make_async_copy(a, b, wsem.at[n]) for n, (a, b) in enumerate(((wg_hbm, wg), (wu_hbm, wu), (wd_hbm, wd)))]
+        for c in loads:
+            c.start()
+
+        def rows_of(i):
+            u, h = ag_unit(i)
+            return half_rows(xor_bits(t, u), h)
+
+        def dy_copy(i):
+            return pltpu.make_async_copy(dy_ref.at[rows_of(i), :], dyb.at[i % 2], dsem.at[i % 2])
+
+        def z_copy(i):
+            return pltpu.make_async_copy(full.at[rows_of(i), :], z_out.at[rows_of(i), :], zsem.at[i])
+
+        def out_copies(i):
+            return [pltpu.make_async_copy(st.at[n, i % 2], o.at[rows_of(i), :], osem.at[n, i % 2]) for n, o in enumerate((hid_out, dg_out, du_out))]
+
+        dy_copy(0).start()
+
+        def compute(i, s, h):
+            @pl.when(i == 0)
+            def _():
+                for c in loads:
+                    c.wait()
+
+            @pl.when(i < 15)
+            def _():
+                dy_copy(i + 1).start()
+
+            @pl.when(i >= 2)
+            def _():
+                for c in out_copies(i - 2):
+                    c.wait()
+
+            z_copy(i).start()
+            dy_copy(i).wait()
+            z_b = full[half_rows(s, h), :]
+            dy_b = dyb[i % 2]
+            for cols in tiles:
+                gate = dot_nn(z_b, wg[:, cols])
+                up = dot_nn(z_b, wu[:, cols])
+                d_hid = dot_nt(dy_b, wd[cols, :])
+                sig = jax.nn.sigmoid(gate)
+                act = gate * sig
+                st[0, i % 2, :, cols] = (act * up).astype(BF16)
+                st[1, i % 2, :, cols] = (d_hid * up * sig * (1.0 + gate * (1.0 - sig))).astype(BF16)
+                st[2, i % 2, :, cols] = (d_hid * act).astype(BF16)
+            for c in out_copies(i):
+                c.start()
+
+        ag_run(z_ref, full, send, recv, compute)
+        for i in (14, 15):
+            for c in out_copies(i):
+                c.wait()
+        for i in range(16):
+            z_copy(i).wait()
+
+    act = jax.ShapeDtypeStruct((seq, ffn), BF16)
+    return comm_call(body, 'ag_mlp', 3, [VM, ANY, ANY, ANY, ANY], [ANY] * 4, [jax.ShapeDtypeStruct((seq, dim), BF16), act, act, act],
+                     [pltpu.VMEM((seq, dim), BF16), pltpu.VMEM((dim, ffn), BF16), pltpu.VMEM((dim, ffn), BF16), pltpu.VMEM((ffn, dim), BF16),
+                      pltpu.VMEM((2, HALF, dim), BF16), pltpu.VMEM((3, 2, HALF, ffn), BF16)] + AG_SEMS
+                     + [pltpu.SemaphoreType.DMA((16,)), pltpu.SemaphoreType.DMA((3,)), pltpu.SemaphoreType.DMA((2,)), pltpu.SemaphoreType.DMA((3, 2))],
+                     80_000_000_000)(z, dy, w_gate, w_up, w_down)
+
+
+def mlp_back_rs(d_gate, d_up, w_gate, w_up):
+    ffn = d_gate.shape[1]
+    dim = w_gate.shape[0]
+
+    def body(dg_ref, du_ref, wg_hbm, wu_hbm, out_ref, stage, fp, fx, fy, send, recv, wg, wu, blk, wsem, bsem):
+        t = lax.axis_index('tp')
+        loads = [pltpu.make_async_copy(a, b, wsem.at[n]) for n, (a, b) in enumerate(((wg_hbm, wg), (wu_hbm, wu)))]
+
+        def fetch(i):
+            at = pl.ds(pl.multiple_of(xor_bits(t, rs_unit(i)) * SHARD, SHARD), SHARD)
+            return [pltpu.make_async_copy(r.at[at, :], blk.at[n, i % 2], bsem.at[n, i % 2]) for n, r in enumerate((dg_ref, du_ref))]
+
+        for c in fetch(0) + loads:
+            c.start()
+
+        def produce(i, s):
+            @pl.when(i < 7)
+            def _():
+                for c in fetch(i + 1):
+                    c.start()
+
+            for c in fetch(i):
+                c.wait()
+
+            @pl.when(i == 0)
+            def _():
+                for c in loads:
+                    c.wait()
+
+            dg_b = blk[0, i % 2]
+            du_b = blk[1, i % 2]
+            for n in range(dim // 256):
+                cols = slice(n * 256, (n + 1) * 256)
+                stage[i, :, cols] = (dot_nt(dg_b, wg[cols, :]) + dot_nt(du_b, wu[cols, :])).astype(BF16)
+
+        def finish(at, val):
+            out_ref[at, :] = val.astype(BF16)
+
+        rs_run(stage, fp, fx, fy, send, recv, produce, finish)
+
+    return comm_call(body, 'mlp_back_rs', 4, [ANY] * 4, VM, jax.ShapeDtypeStruct((SHARD, dim), BF16),
+                     rs_scratch(dim) + [pltpu.VMEM((dim, ffn), BF16), pltpu.VMEM((dim, ffn), BF16), pltpu.VMEM((2, 2, SHARD, ffn), BF16),
+                                        pltpu.SemaphoreType.DMA((2,)), pltpu.SemaphoreType.DMA((2, 2))], 60_000_000_000)(d_gate, d_up, w_gate, w_up)
+
+
+def ag_dattn(x, w_o):
+    dim = x.shape[1]
+    seq = 8 * SHARD
+    width = w_o.shape[0]
+
+    def body(x_ref, w_ref, x_out, do_ref, full, send, recv, sem):
+        def compute(i, s, h):
+            at = half_rows(s, h)
+            pltpu.make_async_copy(full.at[at, :], x_out.at[at, :], sem.at[i]).start()
+            do_ref[at, :] = dot_nt(full[at, :], w_ref[...]).astype(BF16)
+
+        ag_run(x_ref, full, send, recv, compute)
+        for i in range(16):
+            at = half_rows(i // 2, i % 2)
+            pltpu.make_async_copy(full.at[at, :], x_out.at[at, :], sem.at[i]).wait()
+
+    return comm_call(body, 'ag_dattn', 5, [VM, VM], [ANY, VM], [jax.ShapeDtypeStruct((seq, dim), BF16), jax.ShapeDtypeStruct((seq, width), BF16)],
+                     [pltpu.VMEM((seq, dim), BF16)] + AG_SEMS + [pltpu.SemaphoreType.DMA((16,))], 40_000_000_000)(x, w_o)
+
+
+def attn_back_rs(d_query, d_latent, w_q, w_dkv):
+    heads, dim, _ = w_q.shape
+
+    def body(dq_ref, dl_ref, wq_ref, wl_ref, out_ref, stage, fp, fx, fy, send, recv):
+        def produce(i, s):
+            at = pl.ds(pl.multiple_of(s * SHARD, SHARD), SHARD)
+            for n in range(dim // 256):
+                cols = slice(n * 256, (n + 1) * 256)
+                val = dot_nt(dl_ref[at, :], wl_ref[cols, :])
+                for hd in range(heads):
+                    val = val + dot_nt(dq_ref[hd, at, :], wq_ref[hd, cols, :])
+                stage[i, :, cols] = val.astype(BF16)
+
+        def finish(at, val):
+            out_ref[at, :] = val.astype(BF16)
+
+        rs_run(stage, fp, fx, fy, send, recv, produce, finish)
+
+    return comm_call(body, 'attn_back_rs', 6, [VM] * 4, VM, jax.ShapeDtypeStruct((SHARD, dim), BF16), rs_scratch(dim), 40_000_000_000)(d_query, d_latent, w_q, w_dkv)
+
+
 def gather_seq(x):
     return lax.all_gather(x, 'tp', axis=0, tiled=True)
 
@@ -299,11 +749,10 @@
     scale = qk ** -0.5
     w_o2 = w_o.reshape(heads * vdim, -1)
     x_attn_loc, attn_norm_pull = jax.vjp(rms_norm, embedded.astype(F32), g_attn)
-    x_attn = gather_seq(x_attn_loc)
+    w_q3 = jnp.swapaxes(w_q, 0, 1)
+    x_attn, query, latent = ag_proj(x_attn_loc, w_q3, w_dkv)
     seq = x_attn.shape[0]
     cos_t, sin_t = rope_tables(seq, qk - nope)
-    query = matmul_f32('sd,dhe->hse', x_attn, w_q).astype(BF16)
-    latent = matmul_f32('sd,dc->sc', x_attn, w_dkv)
     (c_kv, k_pe), kv_pull = jax.vjp(kv_prep, latent, g_kv)
     k_nope = matmul_f32('sc,che->hse', c_kv, w_uk).astype(BF16)
     value = matmul_f32('sc,chv->hsv', c_kv, w_uv).astype(BF16)
@@ -311,32 +760,22 @@
     q_cat = jnp.concatenate([query[..., :nope], q_pe], axis=-1)
     k_cat = jnp.concatenate([k_nope, jnp.broadcast_to(k_pe[None], (heads,) + k_pe.shape)], axis=-1)
     attn_out, lse = attn_fwd(q_cat, k_cat, jnp.swapaxes(value, 1, 2), scale)
-    attn_part = matmul_f32('sv,vd->sd', attn_out, w_o2).astype(BF16)
-    attn_loc = scatter_seq(attn_part)
+    attn_loc = attn_out_rs(attn_out, w_o2)
     residual = (embedded.astype(F32) + attn_loc.astype(F32)).astype(BF16)
     x_mlp_loc, mlp_norm_pull = jax.vjp(rms_norm, residual.astype(F32), g_mlp)
-    x_mlp = gather_seq(x_mlp_loc)
-    gate = matmul_f32('sd,df->sf', x_mlp, w_gate)
-    up_proj = matmul_f32('sd,df->sf', x_mlp, w_up)
-    gate_sig = jax.nn.sigmoid(gate)
-    hidden = (gate * gate_sig * up_proj).astype(BF16)
+    x_mlp, hidden, d_gate, d_up = ag_mlp(x_mlp_loc, dy_full, w_gate, w_up, w_down)
     mlp_part = matmul_f32('sf,fd->sd', hidden, w_down).astype(BF16)
     mlp_loc = scatter_seq(mlp_part)
     layer_out = (residual.astype(F32) + mlp_loc.astype(F32)).astype(BF16)
 
-    d_hidden = matmul_f32('sd,fd->sf', dy_full, w_down)
     dw_down = matmul_f32('sf,sd->fd', hidden, dy_full)
-    d_up = (d_hidden * gate * gate_sig).astype(BF16)
-    d_gate = (d_hidden * up_proj * gate_sig * (1.0 + gate * (1.0 - gate_sig))).astype(BF16)
     dw_gate = matmul_f32('sd,sf->df', x_mlp, d_gate)
     dw_up = matmul_f32('sd,sf->df', x_mlp, d_up)
-    dx_mlp_part = (matmul_f32('sf,df->sd', d_gate, w_gate) + matmul_f32('sf,df->sd', d_up, w_up)).astype(BF16)
-    dx_mlp = scatter_seq(dx_mlp_part)
+    dx_mlp = mlp_back_rs(d_gate, d_up, w_gate, w_up)
     d_res_norm, dg_mlp_part = mlp_norm_pull(dx_mlp)
     d_residual = d_out.astype(F32) + d_res_norm
-    d_attn_full = gather_seq(d_residual.astype(BF16))
+    d_attn_full, d_attn_out = ag_dattn(d_residual.astype(BF16), w_o2)
     dw_o = matmul_f32('sv,sd->vd', attn_out, d_attn_full).reshape(w_o.shape)
-    d_attn_out = matmul_f32('sd,vd->sv', d_attn_full, w_o2).astype(BF16)
     delta = jnp.sum((d_attn_out.astype(F32) * attn_out.astype(F32)).reshape(seq, heads, vdim), axis=-1).T.reshape(heads, 1, seq)
     d_qt, d_k, d_value = attn_bwd(q_cat, k_cat, jnp.swapaxes(k_cat, 1, 2), value, d_attn_out, lse, delta, scale)
     d_q = jnp.swapaxes(d_qt, 1, 2)
@@ -350,8 +789,7 @@
     d_latent = d_latent.astype(BF16)
     dw_q = matmul_f32('sd,hse->dhe', x_attn, d_query)
     dw_dkv_part = matmul_f32('sd,sc->dc', x_attn, d_latent)
-    dx_attn_part = (matmul_f32('hse,dhe->sd', d_query, w_q) + matmul_f32('sc,dc->sd', d_latent, w_dkv)).astype(BF16)
-    dx_attn = scatter_seq(dx_attn_part)
+    dx_attn = attn_back_rs(d_query, d_latent, w_q3, w_dkv)
     d_emb_norm, dg_attn_part = attn_norm_pull(dx_attn)
     d_embed = (d_residual + d_emb_norm).astype(BF16)
     dw_dkv, dg_kv, dg_attn, dg_mlp = lax.psum((dw_dkv_part, dg_kv_part, dg_attn_part, dg_mlp_part), 'tp')
@@ -370,7 +808,7 @@
         slots = jnp.concatenate([slots, jnp.full((128,), vocab_local, jnp.int32)])
         cnt = jnp.sum(owned.astype(jnp.int32)).reshape(1)
         rows = gather_rows(slots, pos, cnt, embed_table, seq)
-        embedded = scatter_seq(rows)
+        embedded = rs_rows(rows)
         layer_out, d_embed, weight_grads = layer_pass(embedded, dy_loc, dy_full, w_q, w_dkv, g_kv, w_uk, w_uv, w_o, g_attn, g_mlp, w_gate, w_up, w_down)
         de_full = gather_seq(d_embed)
         d_table = scatter_rows(slots, pos, cnt, de_full, jnp.zeros((vocab_local, model_dim), BF16))

time: 963 us -> 718 us (0.75)
  waiting for transfers between devices: 461 us -> 0.78 us
  Pallas kernels: 63.5 us -> 423 us
  matrix products: 263 us -> 106 us
  local copies, waits for them, and re-layouts: 67.4 us -> 79.5 us
    pallas_call x0 -> x7, Pallas kernels: none -> 358 us  [the longest x1 67.2 us: ag_mlp(): comm_call(body, 'ag_mlp', 3, [VM, ANY, ANY, ANY, ANY], [ANY] * 4, [jax.Sh...]
    reduce_scatter x5 -> x1, waiting for transfers between devices: 298 us -> 0.02 us  [scatter_seq(): return lax.psum_scatter(x, 'tp', scatter_dimension=0, tiled=True)]
    all_gather x5 -> x2, waiting for transfers between devices: 159 us -> 0.01 us  [gather_seq(): return lax.all_gather(x, 'tp', axis=0, tiled=True)]
    dot_general x21 -> x11, matrix products: 245 us -> 95.6 us  [matmul_f32(): return jnp.einsum(form, lhs, rhs, preferred_element_type=jnp.float32)]
    unnamed x114 -> x122, local copies, waits for them, and re-layouts: 16.8 us -> 39 us
  transfers between devices with their start and end apart: 11 -> 4, of which waited for: 10 -> 0; matrix products, arithmetic and copies ran while one was open for 17% -> 29% of each run, Pallas kernels for 2% -> 43%
where the time goes in v2:
time: 718 us; the launch traced here: 708 us
  Pallas kernels  423 us (59%)
  matrix products  106 us (15%)
  local copies, waits for them, and re-layouts  79.5 us (11%)
  other arithmetic  60.4 us (8%)
  blocking collectives  23.5 us (3%)
  between operations  14.9 us (2%)
    dot_general x11, matrix products, matmul_f32(): return jnp.einsum(form, lhs, rhs, preferred_element_type=jnp.float32)  95.6 us
    pallas_call x1, Pallas kernels, ag_mlp(): comm_call(body, 'ag_mlp', 3, [VM, ANY, ANY, ANY, ANY], [ANY] * 4, [jax.Sh...  67.2 us
    pallas_call x1, Pallas kernels, ag_dattn(): comm_call(body, 'ag_dattn', 5, [VM, VM], [ANY, VM], [jax.ShapeDtypeStruct...  58.4 us
    pallas_call x1, Pallas kernels, mlp_back_rs(): comm_call(body, 'mlp_back_rs', 4, [ANY] * 4, VM, jax.ShapeDtypeStruct((SH...  51.7 us
    pallas_call x1, Pallas kernels, attn_back_rs(): comm_call(body, 'attn_back_rs', 6, [VM] * 4, VM, jax.ShapeDtypeStruct((SH...  47.8 us
    pallas_call x1, Pallas kernels, ag_proj(): comm_call(body, 'ag_proj', 1, [VM, VM, VM], [ANY, VM, VM], [jax.ShapeDtyp...  46.1 us
    pallas_call x1, Pallas kernels, rs_rows(): comm_call(body, 'rs_rows', 0, [ANY], VM, jax.ShapeDtypeStruct((SHARD, dim...  43.4 us
    pallas_call x1, Pallas kernels, attn_out_rs(): comm_call(body, 'attn_out_rs', 2, [VM, VM], VM, jax.ShapeDtypeStruct((SHA...  43.2 us
  transfers between devices with their start and end apart: 4, of which 0 were waited for; matrix products, arithmetic and copies ran while one was open for 29% of the time, Pallas kernels for 43%

profile of v2, /device:TPU:0, one launch (start us, length us, event | category | flops | bytes accessed | tf_op | source)
XLA Modules:
  0.0 707.9 jit_solution(5572913626568552352)
XLA Ops:
  9.4 5.0 sort.15
  15.0 2.0 copy.78
  17.0 3.7 copy.75
  20.7 2.6 copy.76.wl_ref
  23.2 8.3 %copy.83.wg_hbm = bf16[2048,1368]{1,0:T(8,128)(2,1)} copy(bf16[2048,1368]{0,1:T(8,128)(2,1)} %param.24) | data formatting | bytes 11206656 | tf_op args[10]
  31.5 8.3 %copy.84.wu_hbm = bf16[2048,1368]{1,0:T(8,128)(2,1)} copy(bf16[2048,1368]{0,1:T(8,128)(2,1)} %param.25) | data formatting | bytes 11206656 | tf_op args[11]
  39.8 21.4 %gather_rows.1.rows_ref = bf16[2048,2048]{1,0:T(8,128)(2,1)} custom-call(s32[2176]{0:T(1024)} %concatenate.24.slot_ref, s32[2048]{0:T(1024)} %get-tuple-element.30.pos_ref, s32[1]{0:T(128)} %bitcast.1.cnt_ref, bf16[12800,2048]{1,0:T(8,128)(2,1)} %tab_ref.1), custom_call_target="tpu_custom_call" | custom-call | flops 20000000000 | bytes 24000000 | tf_op jit(solution)/shard_map/gather_rows/pallas_call | solution.py:108
  61.3 43.4 %rs_rows.1 = bf16[256,2048]{1,0:T(8,128)(2,1)} custom-call(bf16[2048,2048]{1,0:T(8,128)(2,1)} %gather_rows.1.rows_ref), custom_call_target="tpu_custom_call" | custom-call | flops 40000000000 | bytes 20000000 | tf_op jit(solution)/shard_map/rs_rows/pallas_call | solution.py:528
  106.8 2.5 fusion.10.x_ref
  109.3 46.1 %ag_proj.1 = (bf16[2048,2048]{1,0:T(8,128)(2,1)}, bf16[2,2048,192]{2,1,0:T(8,128)(2,1)}, f32[2048,576]{1,0:T(8,128)}) custom-call(bf16[256,2048]{1,0:T(8,128)(2,1)} %fusion.10.x_ref, bf16[2,2048,192]{2,1,0:T(8,128)(2,1)} %bitcast.70, bf16[2048,576]{1,0:T(8,128)(2,1)} %copy.76.wl_ref), custom_call_target="tpu_custom_call" | custom-call | flops 40000000000 | bytes 20000000 | tf_op jit(solution)/shard_map/ag_proj/pallas_call | solution.py:551
  155.4 2.4 slice.44
  157.8 2.5 multiply_reduce_fusion
  164.8 7.0 subtract_convert_fusion.2
  172.9 1.9 copy.79
  177.6 2.1 fusion.40
  179.6 2.7 copy.81.k_ref
  182.4 2.1 slice_convert_fusion.2
  186.9 10.8 %attn_fwd.1 = (bf16[2048,256]{1,0:T(8,128)(2,1)S(1)}, f32[2,1,2048]{2,1,0:T(1,128)S(1)}) custom-call(bf16[2,2048,192]{2,1,0:T(8,128)(2,1)S(1)} %pad_maximum_fusion.q_ref, bf16[2,2048,192]{2,1,0:T(8,128)(2,1)S(1)} %copy.81.k_ref, bf16[2,128,2048]{2,1,0:T(8,128)(2,1)S(1)} %copy.82.vt_ref), custom_call_target="tpu_custom_call" | custom-call | flops 20000000000 | bytes 10000000 | tf_op jit(solution)/shard_map/attn_fwd/pallas_call | solution.py:225
  199.3 43.2 %attn_out_rs.1 = bf16[256,2048]{1,0:T(8,128)(2,1)} custom-call(bf16[2048,256]{1,0:T(8,128)(2,1)} %copy-done.1, bf16[256,2048]{1,0:T(8,128)(2,1)} %bitcast.79), custom_call_target="tpu_custom_call" | custom-call | flops 40000000000 | bytes 20000000 | tf_op jit(solution)/shard_map/attn_out_rs/pallas_call | solution.py:571
  245.6 67.2 %ag_mlp.1 = (bf16[2048,2048]{1,0:T(8,128)(2,1)}, bf16[2048,1368]{1,0:T(8,128)(2,1)}, bf16[2048,1368]{1,0:T(8,128)(2,1)}, bf16[2048,1368]{1,0:T(8,128)(2,1)}) custom-call(bf16[256,2048]{1,0:T(8,128)(2,1)} %fusion.9.z_ref, bf16[2048,2048]{1,0:T(8,128)(2,1)} %bitcast.78, bf16[2048,1368]{1,0:T(8,128)(2,1)} %copy.83.wg_hbm, bf16[2048,1368]{1,0:T(8,128)(2,1)} %copy.84.wu_hbm, ...), custom_call_target="tpu_custom_call" | custom-call | flops 80000000000 | bytes 20000000 | tf_op jit(solution)/shard_map/ag_mlp/pallas_call | solution.py:644
  312.8 51.7 %mlp_back_rs.1 = bf16[256,2048]{1,0:T(8,128)(2,1)} custom-call(bf16[2048,1368]{1,0:T(8,128)(2,1)} %get-tuple-element.35.dg_ref, bf16[2048,1368]{1,0:T(8,128)(2,1)} %get-tuple-element.36.du_ref, bf16[2048,1368]{1,0:T(8,128)(2,1)} %copy.83.wg_hbm, bf16[2048,1368]{1,0:T(8,128)(2,1)} %copy.84.wu_hbm), custom_call_target="tpu_custom_call" | custom-call | flops 60000002048 | bytes 20000000 | tf_op jit(solution)/shard_map/mlp_back_rs/pallas_call | solution.py:691
  364.5 3.0 fusion.11
  369.3 18.4 %convolution_convert_fusion = bf16[2048,2048]{1,0:T(8,128)(2,1)} fusion(bf16[2048,1368]{1,0:T(8,128)(2,1)} %get-tuple-element.34, bf16[1368,2048]{1,0:T(8,128)(2,1)} %wd_hbm.1), kind=kOutput, calls=%fused_computation | convolution fusion | flops 11479810048 | bytes 19595264 | tf_op jit(solution)/shard_map/sf,fd->sd/dot_general | solution.py:20
  387.8 58.4 %ag_dattn.1 = (bf16[2048,2048]{1,0:T(8,128)(2,1)}, bf16[2048,256]{1,0:T(8,128)(2,1)}) custom-call(bf16[256,2048]{1,0:T(8,128)(2,1)} %fusion.33.x_ref, bf16[256,2048]{1,0:T(8,128)(2,1)} %bitcast.80), custom_call_target="tpu_custom_call" | custom-call | flops 40000000000 | bytes 20000000 | tf_op jit(solution)/shard_map/ag_dattn/pallas_call | solution.py:712
  446.2 2.7 convert_multiply_fusion.14
  449.0 2.3 reshape.167
  451.3 3.5 reduce_sum.113
  455.7 16.0 %attn_bwd.1 = (f32[2,192,2048]{2,1,0:T(8,128)}, f32[2,2048,192]{2,1,0:T(8,128)}, bf16[2,2048,128]{2,1,0:T(8,128)(2,1)}) custom-call(bf16[2,2048,192]{2,1,0:T(8,128)(2,1)} %copy-done.5, bf16[2,2048,192]{2,1,0:T(8,128)(2,1)} %copy-done.4, bf16[2,192,2048]{2,1,0:T(8,128)(2,1)} %get-tuple-element.101.kt_ref, bf16[2,2048,128]{2,1,0:T(8,128)(2,1)} %bitcast.75, ...), custom_call_target="tpu_custom_call" | custom-call | flops 49999998976 | bytes 16000000 | tf_op jit(solution)/shard_map/attn_bwd/pallas_call | solution.py:266
  473.5 5.0 copy.89
  478.6 1.9 slice.85
  480.5 2.4 fusion.30
  484.8 4.5 multiply_add_fusion.1
  491.6 2.0 pad_maximum_fusion.1.dq_ref
  496.4 47.8 %attn_back_rs.1 = bf16[256,2048]{1,0:T(8,128)(2,1)} custom-call(bf16[2,2048,192]{2,1,0:T(8,128)(2,1)} %pad_maximum_fusion.1.dq_ref, bf16[2048,576]{1,0:T(8,128)(2,1)} %add_convert_fusion.dl_ref, bf16[2,2048,192]{2,1,0:T(8,128)(2,1)} %bitcast.71, bf16[2048,576]{1,0:T(8,128)(2,1)} %copy.76.wl_ref), custom_call_target="tpu_custom_call" | custom-call | flops 40000000000 | bytes 20000000 | tf_op jit(solution)/shard_map/attn_back_rs/pallas_call | solution.py:734
  544.3 2.4 fusion.12
  546.8 4.5 fusion.15
  551.3 4.4 copy.95
  555.7 2.4 fusion.24
  561.3 8.6 %fusion.47 = f32[2048,384]{0,1} fusion(bf16[2048,384]{0,1:T(8,128)(2,1)S(1)} %bitcast.73, bf16[2048,2048]{1,0:T(8,128)(2,1)} %get-tuple-element.42), kind=kOutput, calls=%fused_computation.102 | convolution fusion | flops 3221225472 | bytes 13107200
  570.0 6.8 fusion.43
  576.8 18.8 %fusion.45 = f32[2048,1368]{0,1:T(8,128)} fusion(bf16[2048,2048]{1,0:T(8,128)(2,1)} %get-tuple-element.44, bf16[2048,1368]{1,0:T(8,128)(2,1)} %get-tuple-element.35.dg_ref), kind=kOutput, calls=%fused_computation.100 | convolution fusion | flops 11475615744 | bytes 25198592 | tf_op jit(solution)/shard_map/sd,sf->df/dot_general | solution.py:20
  595.6 17.0 %fusion.46 = f32[2048,1368]{0,1:T(8,128)} fusion(bf16[2048,2048]{1,0:T(8,128)(2,1)} %get-tuple-element.44, bf16[2048,1368]{1,0:T(8,128)(2,1)S(1)} %bitcast.85), kind=kOutput, calls=%fused_computation.101 | convolution fusion | flops 11475615744 | bytes 25198592 | tf_op jit(solution)/shard_map/sd,sf->df/dot_general | solution.py:20
  613.3 23.5 %all-reduce.5 = (f32[512]{0:T(512)}, f32[2048]{0:T(1024)}, f32[2048]{0:T(1024)}) all-reduce(f32[512]{0:T(512)S(1)} %get-tuple-element.84, f32[2048]{0:T(1024)S(1)} %get-tuple-element.88, f32[2048]{0:T(1024)S(1)} %copy-done.38), channel_id=1, replica_groups=mesh['dp'=1,'tp'=8] {'tp'}, use_global_device_ids=true, to_apply=%region_13.14 | all-reduce | flops 4608 | bytes 36864 | tf_op jit(solution)/shard_map/psum | solution.py:795
  636.8 18.6 %fusion.38 = f32[1368,2048]{1,0:T(8,128)} fusion(bf16[2048,1368]{1,0:T(8,128)(2,1)} %get-tuple-element.34, bf16[1,2048,2048]{2,1,0:T(8,128)(2,1)} %all-gather.6.cloned.1.call-done), kind=kOutput, calls=%fused_computation.94 | convolution fusion | flops 11475615744 | bytes 25198592 | tf_op jit(solution)/shard_map/sf,sd->fd/dot_general | solution.py:20
  655.4 7.1 fusion.44
  662.4 16.8 %broadcast_in_dim.19.zero_ref = bf16[12800,2048]{1,0:T(8,128)(2,1)} broadcast(bf16[]{:T(256)} %constant.37.clone.1), dimensions={} | broadcast | bytes 52428800 | tf_op jit(solution)/shard_map/broadcast_in_dim | solution.py:814
  679.3 16.7 %scatter_rows.1 = bf16[12800,2048]{1,0:T(8,128)(2,1)} custom-call(s32[2176]{0:T(1024)} %concatenate.24.slot_ref, s32[2048]{0:T(1024)} %get-tuple-element.30.pos_ref, s32[1]{0:T(128)} %bitcast.1.cnt_ref, bf16[2048,2048]{1,0:T(8,128)(2,1)} %all-gather.4.cloned.1.call-done.de_ref, ...), custom_call_target="tpu_custom_call", output_to_operand_aliasing={{}: (4, {})} | custom-call | flops 20000000000 | bytes 24000000 | tf_op jit(solution)/shard_map/scatter_rows/pallas_call | solution.py:174
  696.0 5.1 copy.116
  (165 shorter events, 35.5 us)
Async XLA Ops:
  7.2 154.4 %copy-start = (bf16[512,2,128]{2,1,0:T(2,128)(2,1)S(1)}, bf16[512,2,128]{2,1,0:T(2,128)(2,1)}, u32[]{:S(2)}) copy-start(bf16[512,2,128]{2,1,0:T(2,128)(2,1)} %param.20) | copy-start | bytes 786436
  7.2 238.4 %all-gather.6.cloned.1.call-start = ((), (), s32[]{:S(2)}) async-start(), calls=%async_computation.4 | async-start | bytes 9437184 | tf_op jit(solution)/shard_map/all_gather | solution.py:738
  7.9 538.8 %reduce-scatter.2.cloned.1.call-start = ((), (), s32[]{:S(2)}) async-start(), calls=%async_computation.1 | async-start | bytes 9437184 | tf_op jit(solution)/shard_map/reduce_scatter | solution.py:742
  15.0 5.7 copy-start.24
  61.3 45.5 %copy-start.36 = (f32[2048]{0:T(1024)S(1)}, f32[2048]{0:T(1024)}, u32[]{:S(2)}) copy-start(f32[2048]{0:T(1024)} %param.22) | copy-start | bytes 24580
  106.8 2.5 copy-start.43
  155.4 5.6 copy-start.7
  157.8 3.2 copy-start.41
  161.6 13.3 %copy-start.13 = (bf16[2048,512]{1,0:T(8,128)(2,1)}, bf16[2048,512]{1,0:T(8,128)(2,1)S(1)}, u32[]{:S(2)}) copy-start(bf16[2048,512]{1,0:T(8,128)(2,1)S(1)} %multiply_convert_fusion) | copy-start | bytes 6291460
  164.8 7.0 copy-start.49
  182.4 4.5 copy-start.4
  182.4 2.3 copy-start.18
  182.4 2.6 copy-start.20
  186.9 10.8 %copy-start.5 = (bf16[2,2048,192]{2,1,0:T(8,128)(2,1)}, bf16[2,2048,192]{2,1,0:T(8,128)(2,1)S(1)}, u32[]{:S(2)}) copy-start(bf16[2,2048,192]{2,1,0:T(8,128)(2,1)S(1)} %pad_maximum_fusion.q_ref) | copy-start | bytes 4718596
  199.3 43.2 %copy-start.8 = (bf16[256,2048]{1,0:T(8,128)(2,1)S(1)}, bf16[256,2048]{1,0:T(8,128)(2,1)}, u32[]{:S(2)}) copy-start(bf16[256,2048]{1,0:T(8,128)(2,1)} %rs_rows.1) | copy-start | bytes 3145732
  244.3 123.3 %copy-start.10 = (bf16[256,2048]{1,0:T(8,128)(2,1)}, bf16[256,2048]{1,0:T(8,128)(2,1)S(1)}, u32[]{:S(2)}) copy-start(bf16[256,2048]{1,0:T(8,128)(2,1)S(1)} %get-tuple-element.94) | copy-start | bytes 3145732
  244.3 123.3 %copy-start.39 = (f32[256]{0:T(256)}, f32[256]{0:T(256)S(1)}, u32[]{:S(2)}) copy-start(f32[256]{0:T(256)S(1)} %fusion.37) | copy-start | bytes 3076
  364.5 3.0 copy-start.15
  364.5 3.0 copy-start.17
  387.7 58.5 %copy-start.2 = (bf16[2048,256]{1,0:T(8,128)(2,1)S(1)}, bf16[2048,256]{1,0:T(8,128)(2,1)}, u32[]{:S(2)}) copy-start(bf16[2048,256]{1,0:T(8,128)(2,1)} %copy-done.1) | copy-start | bytes 3145732
  387.7 274.7 %all-gather.4.cloned.1.call-start = ((), (), s32[]{:S(2)}) async-start(), calls=%async_computation.2 | async-start | bytes 9437184 | tf_op jit(solution)/shard_map/all_gather | solution.py:738
  473.5 9.4 %slice-start = ((s8[5242880]{0:T(1024)(128)(4,1)}), s8[1048576]{0:T(1024)(128)(4,1)S(1)}, s32[]{:S(2)}) async-start(s8[5242880]{0:T(1024)(128)(4,1)} %bitcast.64), calls=%async_computation.5 | async-start | bytes 2097152
  478.6 1.9 copy-start.25
  478.6 4.3 slice-start.1
  480.4 2.4 copy-start.28
  480.5 2.4 copy-start.33
  480.5 2.4 copy-start.42
  482.9 1.8 copy-start.50
  484.8 4.9 copy-start.12
  496.4 47.8 %copy-start.9 = (bf16[256,2048]{1,0:T(8,128)(2,1)S(1)}, bf16[256,2048]{1,0:T(8,128)(2,1)}, u32[]{:S(2)}) copy-start(bf16[256,2048]{1,0:T(8,128)(2,1)} %rs_rows.1) | copy-start | bytes 3145732
  496.4 47.8 %copy-start.37 = (f32[2048]{0:T(1024)S(1)}, f32[2048]{0:T(1024)}, u32[]{:S(2)}) copy-start(f32[2048]{0:T(1024)} %param.22) | copy-start | bytes 24580
  496.4 47.8 %copy-start.44 = (f32[256]{0:T(256)S(1)}, f32[256]{0:T(256)}, u32[]{:S(2)}) copy-start(f32[256]{0:T(256)} %copy-done.43) | copy-start | bytes 3076
  544.2 2.5 copy-start.46
  544.2 2.5 copy-start.11
  544.2 2.5 copy-start.16
  544.2 2.5 copy-start.31
  544.2 2.5 copy-start.40
  544.3 2.5 copy-start.48
  551.3 4.5 copy-start.14
  551.3 144.7 %all-reduce.8.cloned.1.call-start = ((), (), s32[]{:S(2)}) async-start(), calls=%async_computation.3 | async-start | bytes 9437184 | tf_op jit(solution)/shard_map/psum | solution.py:795
  555.7 3.6 copy-start.29
  559.4 2.0 copy-start.26
  559.4 10.6 %slice-start.2 = ((s8[8388608]{0:T(1024)(128)(4,1)}), s8[4194304]{0:T(1024)(128)(4,1)S(1)}, s32[]{:S(2)}) async-start(s8[8388608]{0:T(1024)(128)(4,1)} %bitcast.82), calls=%async_computation.7 | async-start | bytes 8388608
  561.3 8.6 %copy-start.23 = (bf16[2048,576]{1,0:T(8,128)(2,1)S(1)}, bf16[2048,576]{1,0:T(8,128)(2,1)}, u32[]{:S(2)}) copy-start(bf16[2048,576]{1,0:T(8,128)(2,1)} %add_convert_fusion.dl_ref) | copy-start | bytes 7077892
  561.3 8.6 %slice-start.3 = ((s8[8388608]{0:T(1024)(128)(4,1)}), s8[4194304]{0:T(1024)(128)(4,1)S(1)}, s32[]{:S(2)}) async-start(s8[8388608]{0:T(1024)(128)(4,1)} %bitcast.82), calls=%async_computation.8 | async-start | bytes 8388608
  570.0 25.6 %slice-start.4 = ((s8[5767168]{0:T(1024)(128)(4,1)}), s8[1572864]{0:T(1024)(128)(4,1)S(1)}, s32[]{:S(2)}) async-start(s8[5767168]{0:T(1024)(128)(4,1)} %bitcast.84), calls=%async_computation.9 | async-start | bytes 3145728
  576.8 18.8 %slice-start.5 = ((s8[5767168]{0:T(1024)(128)(4,1)}), s8[4194304]{0:T(1024)(128)(4,1)S(1)}, s32[]{:S(2)}) async-start(s8[5767168]{0:T(1024)(128)(4,1)} %bitcast.84), calls=%async_computation.10 | async-start | bytes 8388608
  636.8 18.6 %copy-start.3 = (bf16[2048,256]{1,0:T(8,128)(2,1)S(1)}, bf16[2048,256]{1,0:T(8,128)(2,1)}, u32[]{:S(2)}) copy-start(bf16[2048,256]{1,0:T(8,128)(2,1)} %copy-done.1) | copy-start | bytes 3145732
  (13 other events, 14.3 us)
Sparse Core Ops, SparseCore 0:
  9.8 51.1 all-gather.5
  387.8 78.7 reduce-scatter.1
  551.4 48.3 all-gather.3
  612.7 76.3 all-reduce.7

commit v3 on v2

v3 whole, which is shorter than its diff:
```python
import functools

import jax
import jax.numpy as jnp
import numpy as np
from jax import lax
from jax.experimental import pallas as pl
from jax.experimental.pallas import tpu as pltpu
from jax.sharding import PartitionSpec as P

EPSILON = 1e-6
ROPE_BASE = 10000.0
LOG2E = 1.4426950408889634
BLK = 256
RING = 16
F32 = jnp.float32
BF16 = jnp.bfloat16


def matmul_f32(form, lhs, rhs):
    return jnp.einsum(form, lhs, rhs, preferred_element_type=jnp.float32)


def dot_nn(a, b):
    return lax.dot_general(a, b, (((1,), (0,)), ((), ())), preferred_element_type=F32)


def dot_nt(a, b):
    return lax.dot_general(a, b, (((1,), (1,)), ((), ())), preferred_element_type=F32)


def rope_tables(seq_len, rope_dim):
    inv_freq = np.float32(ROPE_BASE) ** (-np.arange(0, rope_dim, 2, dtype=np.float32) / np.float32(rope_dim))
    angles = (np.arange(seq_len, dtype=np.float32)[:, None] * inv_freq[None, :]).astype(np.float64)
    cos, sin = np.cos(angles), np.sin(angles)
    return (jnp.asarray(np.concatenate([cos, cos], axis=1), dtype=F32), jnp.asarray(np.concatenate([-sin, sin], axis=1), dtype=F32))


def swap_halves(x):
    half = x.shape[1] // 2
    return jnp.concatenate([x[:, half:], x[:, :half]], axis=1)


def rope(x, cos_t, sin_t):
    return x * cos_t + swap_halves(x) * sin_t


def unrope(x, cos_t, sin_t):
    return x * cos_t - swap_halves(x) * sin_t


def rms_inv(x):
    return lax.rsqrt(jnp.mean(x * x, axis=-1, keepdims=True) + EPSILON)


def rms_back(x, gain, dy):
    inv = rms_inv(x)
    gd = dy * gain
    mix = jnp.mean(gd * x, axis=-1, keepdims=True)
    return inv * gd - x * (inv * inv * inv * mix), jnp.sum(dy * (x * inv), axis=0, keepdims=True)


def gather_body(slot_ref, pos_ref, cnt_ref, tab_ref, out_ref, buf, acc, sems):
    seq = acc.shape[0]
    cnt = cnt_ref[0]

    def fetch(k):
        blk = pl.multiple_of((slot_ref[k] // 8) * 8, 8)
        return pltpu.make_async_copy(tab_ref.at[pl.ds(blk, 8), :], buf.at[k % RING], sems.at[k % RING])

    def prime(k, c):
        fetch(k).start()
        return c

    lax.fori_loop(0, jnp.minimum(cnt, RING), prime, 0)

    def clear(i, c):
        acc[pl.ds(pl.multiple_of(i * 64, 64), 64), :] = jnp.zeros((64, acc.shape[1]), F32)
        return c

    lax.fori_loop(0, seq // 64, clear, 0)
    rows = lax.broadcasted_iota(jnp.int32, (8, acc.shape[1]), 0)

    def step(k, c):
        fetch(k).wait()
        blk = buf[k % RING].astype(F32)
        row = jnp.sum(jnp.where(rows == slot_ref[k] % 8, blk, 0.0), axis=0, keepdims=True)
        acc[pl.ds(pos_ref[k], 1), :] = row

        @pl.when(k + RING < cnt)
        def _():
            fetch(k + RING).start()

        return c

    lax.fori_loop(0, cnt, step, 0)

    def emit(i, c):
        at = pl.ds(pl.multiple_of(i * 64, 64), 64)
        out_ref[at, :] = acc[at, :].astype(BF16)
        return c

    lax.fori_loop(0, seq // 64, emit, 0)


def gather_rows(slots, pos, cnt, table, seq):
    dim = table.shape[1]
    return pl.pallas_call(
        gather_body,
        grid_spec=pltpu.PrefetchScalarGridSpec(
            num_scalar_prefetch=3,
            grid=(1,),
            in_specs=[pl.BlockSpec(memory_space=pl.ANY)],
            out_specs=pl.BlockSpec((seq, dim), lambda i, *_: (0, 0)),
            scratch_shapes=[pltpu.VMEM((RING, 8, dim), BF16), pltpu.VMEM((seq, dim), F32), pltpu.SemaphoreType.DMA((RING,))],
        ),
        out_shape=jax.ShapeDtypeStruct((seq, dim), BF16),
        compiler_params=pltpu.CompilerParams(vmem_limit_bytes=60 * 1024 * 1024),
        cost_estimate=pl.CostEstimate(flops=20_000_000_000, bytes_accessed=24_000_000, transcendentals=0),
        name="gather_rows",
    )(slots, pos, cnt, table)


def scatter_body(slot_ref, pos_ref, cnt_ref, de_ref, zero_ref, out_ref, wide, acc, stage, sems):
    seq = wide.shape[0]
    cnt = cnt_ref[0]

    def widen(i, c):
        at = pl.ds(pl.multiple_of(i * 64, 64), 64)
        wide[at, :] = de_ref[at, :].astype(F32)
        return c

    lax.fori_loop(0, seq // 64, widen, 0)

    def put(slot_blk, n):
        at = pl.multiple_of(slot_blk * 8, 8)
        return pltpu.make_async_copy(stage.at[n % RING], out_ref.at[pl.ds(at, 8), :], sems.at[n % RING])

    def step(k, carry):
        prev, n = carry
        slot = slot_ref[k]
        blk = slot // 8

        @pl.when(blk != prev)
        def _():
            acc[...] = jnp.zeros_like(acc)

        at = pl.ds(slot % 8, 1)
        acc[at, :] = acc[at, :] + wide[pl.ds(pos_ref[k], 1), :]
        last = slot_ref[k + 1] // 8 != blk

        @pl.when(last)
        def _():
            @pl.when(n >= RING)
            def _():
                put(blk, n).wait()

            stage[n % RING] = acc[...].astype(BF16)
            put(blk, n).start()

        return blk, n + last.astype(jnp.int32)

    _, total = lax.fori_loop(0, cnt, step, (jnp.int32(-1), jnp.int32(0)))

    def drain(i, c):
        put(0, i).wait()
        return c

    lax.fori_loop(jnp.maximum(total - RING, 0), total, drain, 0)


def scatter_rows(slots, pos, cnt, de, zeros):
    seq, dim = de.shape[0], zeros.shape[1]
    return pl.pallas_call(
        scatter_body,
        grid_spec=pltpu.PrefetchScalarGridSpec(
            num_scalar_prefetch=3,
            grid=(1,),
            in_specs=[pl.BlockSpec((seq, dim), lambda i, *_: (0, 0)), pl.BlockSpec(memory_space=pl.ANY)],
            out_specs=pl.BlockSpec(memory_space=pl.ANY),
            scratch_shapes=[pltpu.VMEM((seq, dim), F32), pltpu.VMEM((8, dim), F32), pltpu.VMEM((RING, 8, dim), BF16), pltpu.SemaphoreType.DMA((RING,))],
        ),
        out_shape=jax.ShapeDtypeStruct(zeros.shape, BF16),
        input_output_aliases={4: 0},
        compiler_params=pltpu.CompilerParams(vmem_limit_bytes=60 * 1024 * 1024),
        cost_estimate=pl.CostEstimate(flops=20_000_000_000, bytes_accessed=24_000_000, transcendentals=0),
        name="scatter_rows",
    )(slots, pos, cnt, de, zeros)


def zero_rows(rows, dim, after):
    step = 800

    def body(after_ref, out_ref, blank, sem):
        blank[...] = jnp.zeros_like(blank)
        copies = [pltpu.make_async_copy(blank, out_ref.at[pl.ds(n * step, step), :], sem.at[n]) for n in range(rows // step)]
        for c in copies:
            c.start()
        for c in copies:
            c.wait()

    return pl.pallas_call(
        body,
        in_specs=[pl.BlockSpec(memory_space=pl.ANY)],
        out_specs=pl.BlockSpec(memory_space=pl.ANY),
        out_shape=jax.ShapeDtypeStruct((rows, dim), BF16),
        scratch_shapes=[pltpu.VMEM((step, dim), BF16), pltpu.SemaphoreType.DMA((rows // step,))],
        cost_estimate=pl.CostEstimate(flops=15_000_000_000, bytes_accessed=52_000_000, transcendentals=0),
        name="zero_rows",
    )(after)


def attn_fwd_body(scale2, q_ref, k_ref, vt_ref, o_ref, lse_ref, s_scr):
    seq = q_ref.shape[1]
    tri = lax.broadcasted_iota(jnp.int32, (BLK, BLK), 0) <= lax.broadcasted_iota(jnp.int32, (BLK, BLK), 1)
    for i in range(seq // BLK):
        q_i = q_ref[0, i * BLK:(i + 1) * BLK, :]
        top = None
        for j in range(i + 1):
            s = dot_nt(k_ref[0, j * BLK:(j + 1) * BLK, :], q_i) * scale2
            if j == i:
                s = jnp.where(tri, s, -1e30)
            s_scr[j * BLK:(j + 1) * BLK, :] = s
            part = jnp.max(s.reshape(BLK // 8, 8, BLK), axis=0)
            top = part if top is None else jnp.maximum(top, part)
        top = jnp.max(top, axis=0, keepdims=True)
        den = None
        for j in range(i + 1):
            e = jnp.exp2(s_scr[j * BLK:(j + 1) * BLK, :] - top)
            s_scr[j * BLK:(j + 1) * BLK, :] = e
            part = jnp.sum(e.reshape(BLK // 8, 8, BLK), axis=0)
            den = part if den is None else den + part
        den = jnp.sum(den, axis=0, keepdims=True)
        inv = 1.0 / den
        out = None
        for j in range(i + 1):
            prob = (s_scr[j * BLK:(j + 1) * BLK, :] * inv).astype(BF16)
            part = dot_nn(vt_ref[0, :, j * BLK:(j + 1) * BLK], prob)
            out = part if out is None else out + part
        o_ref[i * BLK:(i + 1) * BLK, :] = out.T.astype(BF16)
        lse_ref[0, :, i * BLK:(i + 1) * BLK] = top + jnp.log2(den)


def attn_fwd(q, k, vt, scale):
    heads, seq, qk = q.shape
    vdim = vt.shape[1]
    return pl.pallas_call(
        functools.partial(attn_fwd_body, scale * LOG2E),
        grid=(heads,),
        in_specs=[pl.BlockSpec((1, seq, qk), lambda h: (h, 0, 0)), pl.BlockSpec((1, seq, qk), lambda h: (h, 0, 0)), pl.BlockSpec((1, vdim, seq), lambda h: (h, 0, 0))],
        out_specs=[pl.BlockSpec((seq, vdim), lambda h: (0, h)), pl.BlockSpec((1, 1, seq), lambda h: (h, 0, 0))],
        out_shape=[jax.ShapeDtypeStruct((seq, heads * vdim), BF16), jax.ShapeDtypeStruct((heads, 1, seq), F32)],
        scratch_shapes=[pltpu.VMEM((seq, BLK), F32)],
        compiler_params=pltpu.CompilerParams(vmem_limit_bytes=40 * 1024 * 1024),
        cost_estimate=pl.CostEstimate(flops=20_000_000_000, bytes_accessed=10_000_000, transcendentals=0),
        name="attn_fwd",
    )(q, k, vt)


def attn_bwd_body(scale2, scale, q_ref, k_ref, kt_ref, v_ref, do_ref, o_ref, lse_ref, cos_ref, sin_ref, dq_ref, dk_ref, dkp_ref, dv_ref, p_scr, ds_scr, dlt):
    seq = q_ref.shape[1]
    nope = dk_ref.shape[2]
    n = seq // BLK
    tri = lax.broadcasted_iota(jnp.int32, (BLK, BLK), 0) <= lax.broadcasted_iota(jnp.int32, (BLK, BLK), 1)
    for i in range(n):
        at_i = slice(i * BLK, (i + 1) * BLK)
        both = do_ref[at_i, :].astype(F32) * o_ref[at_i, :].astype(F32)
        dlt[:, at_i] = jnp.sum(both.T, axis=0, keepdims=True)
    for j in range(n):
        at_j = slice(j * BLK, (j + 1) * BLK)
        k_j = k_ref[0, at_j, :]
        v_j = v_ref[0, at_j, :]
        for i in range(j, n):
            at_i = slice(i * BLK, (i + 1) * BLK)
            s = dot_nt(k_j, q_ref[0, at_i, :])
            prob = jnp.exp2(s * scale2 - lse_ref[0, :, at_i])
            if i == j:
                prob = jnp.where(tri, prob, 0.0)
            dp = dot_nt(v_j, do_ref[at_i, :])
            p_scr[:, at_i] = prob.astype(BF16)
            ds_scr[at_j, at_i] = (prob * (dp - dlt[:, at_i])).astype(BF16)
        dv_ref[0, at_j, :] = dot_nn(p_scr[:, j * BLK:], do_ref[j * BLK:, :]).astype(BF16)
        dk = dot_nn(ds_scr[at_j, j * BLK:], q_ref[0, j * BLK:, :]) * scale
        dk_ref[0, at_j, :] = dk[:, :nope].astype(BF16)
        dkp_ref[0, at_j, :] = dk[:, nope:]
    for i in range(n):
        at_i = slice(i * BLK, (i + 1) * BLK)
        dq = dot_nn(kt_ref[0, :, :(i + 1) * BLK], ds_scr[:(i + 1) * BLK, at_i]) * scale
        half = (dq.shape[0] - nope) // 2
        lo, hi = dq[nope:nope + half, :], dq[nope + half:, :]
        cos_b, sin_b = cos_ref[:, at_i], sin_ref[:, at_i]
        dq_ref[0, :nope, at_i] = dq[:nope, :].astype(BF16)
        dq_ref[0, nope:nope + half, at_i] = (lo * cos_b + hi * sin_b).astype(BF16)
        dq_ref[0, nope + half:, at_i] = (hi * cos_b - lo * sin_b).astype(BF16)


def attn_bwd(q, k, kt, v, do, o, lse, cos_t, sin_t, scale):
    heads, seq, qk = q.shape
    vdim = v.shape[2]
    pe = 2 * cos_t.shape[0]
    per_head = lambda h: (h, 0, 0)
    return pl.pallas_call(
        functools.partial(attn_bwd_body, scale * LOG2E, scale),
        grid=(heads,),
        in_specs=[
            pl.BlockSpec((1, seq, qk), per_head),
            pl.BlockSpec((1, seq, qk), per_head),
            pl.BlockSpec((1, qk, seq), per_head),
            pl.BlockSpec((1, seq, vdim), per_head),
            pl.BlockSpec((seq, vdim), lambda h: (0, h)),
            pl.BlockSpec((seq, vdim), lambda h: (0, h)),
            pl.BlockSpec((1, 1, seq), per_head),
            pl.BlockSpec((pe // 2, seq), lambda h: (0, 0)),
            pl.BlockSpec((pe // 2, seq), lambda h: (0, 0)),
        ],
        out_specs=[pl.BlockSpec((1, qk, seq), per_head), pl.BlockSpec((1, seq, qk - pe), per_head), pl.BlockSpec((1, seq, pe), per_head), pl.BlockSpec((1, seq, vdim), per_head)],
        out_shape=[jax.ShapeDtypeStruct((heads, qk, seq), BF16), jax.ShapeDtypeStruct((heads, seq, qk - pe), BF16), jax.ShapeDtypeStruct((heads, seq, pe), F32), jax.ShapeDtypeStruct((heads, seq, vdim), BF16)],
        scratch_shapes=[pltpu.VMEM((BLK, seq), BF16), pltpu.VMEM((seq, seq), BF16), pltpu.VMEM((1, seq), F32)],
        compiler_params=pltpu.CompilerParams(vmem_limit_bytes=56 * 1024 * 1024),
        cost_estimate=pl.CostEstimate(flops=20_000_000_000, bytes_accessed=16_000_000, transcendentals=0),
        name="attn_bwd",
    )(q, k, kt, v, do, o, lse, cos_t, sin_t)


HALF = 128
SHARD = 256
MESH = pl.DeviceIdType.MESH


def xor_bits(t, u):
    out = 0
    for b in (1, 2, 4):
        tb = (t // b) % 2
        ub = (u // b) % 2
        out = out + b * (tb + ub - 2 * tb * ub)
    return out


def greet(t):
    peers = [xor_bits(t, u) for u in (1, 2, 4)]
    barrier = pltpu.get_barrier_semaphore()
    for peer in peers:
        pl.semaphore_signal(barrier, inc=1, device_id={'tp': peer}, device_id_type=MESH)
    pl.semaphore_wait(barrier, 3)
    return peers


def half_rows(shard, half):
    return pl.ds(pl.multiple_of(shard * SHARD + half * HALF, HALF), HALF)


def ag_unit(i):
    p = i // 4
    r = i % 4
    p0 = (3 - p) // 3
    p3 = p // 3
    mid = 1 - p0 - p3
    u = p0 * (r // 2) + mid * (2 + (r % 2) * 2 + r // 2) + p3 * (6 + r // 2)
    flip = (p - 1) * mid
    return u, (r % 2) + flip * (1 - 2 * (r % 2))


def ag_rows(t, i):
    u, h = ag_unit(i)
    return half_rows(xor_bits(t, u), h)


def ag_run(x_ref, full, send, recv, compute, before=None):
    t = lax.axis_index('tp')
    partner, xn, yn = greet(t)

    def copy(src, shard, half, sem, u_there, dev):
        return pltpu.make_async_remote_copy(
            src_ref=src, dst_ref=full.at[half_rows(shard, half), :], send_sem=send.at[sem],
            recv_sem=recv.at[u_there, half], device_id={'tp': dev}, device_id_type=MESH)

    def mine(half):
        return x_ref.at[pl.ds(half * HALF, HALF), :]

    def held(u, half):
        return full.at[half_rows(xor_bits(t, u), half), :]

    own = [copy(mine(0), t, 0, 0, 2, xn), copy(mine(1), t, 1, 3, 4, yn), copy(mine(0), t, 0, 4, 1, partner), copy(mine(1), t, 1, 5, 1, partner),
           copy(mine(1), t, 1, 1, 2, xn), copy(mine(0), t, 0, 2, 4, yn)]
    for c in own:
        c.start()
    full[pl.ds(pl.multiple_of(t * SHARD, SHARD), SHARD), :] = x_ref[...]
    fwd_y = copy(held(2, 0), xor_bits(t, 2), 0, 6, 6, yn)
    fwd_x = copy(held(4, 1), xor_bits(t, 4), 1, 7, 6, xn)
    fwd_p = {(u, h): copy(held(u, h), xor_bits(t, u), h, 8 + (u - 2) + h, u + 1, partner) for u in (2, 4, 6) for h in (0, 1)}

    def arrive(u, h):
        copy(held(u, h), xor_bits(t, u), h, 0, u, partner).wait_recv()

    def step(i, carry):
        if before is not None:
            before(i)

        @pl.when(i == 1)
        def _():
            arrive(1, 0)
            arrive(1, 1)

        @pl.when(i == 2)
        def _():
            arrive(2, 0)
            fwd_y.start()
            fwd_p[2, 0].start()
            arrive(4, 1)
            fwd_x.start()
            fwd_p[4, 1].start()

        @pl.when(i == 3)
        def _():
            arrive(3, 0)
            arrive(5, 1)

        @pl.when(i == 4)
        def _():
            arrive(2, 1)
            fwd_p[2, 1].start()
            arrive(4, 0)
            fwd_p[4, 0].start()

        @pl.when(i == 5)
        def _():
            arrive(3, 1)
            arrive(5, 0)

        @pl.when(i == 6)
        def _():
            arrive(6, 0)
            fwd_p[6, 0].start()
            arrive(6, 1)
            fwd_p[6, 1].start()

        @pl.when(i == 7)
        def _():
            arrive(7, 0)
            arrive(7, 1)

        compute(i, ag_rows(t, 2 * i), ag_rows(t, 2 * i + 1))
        return carry

    lax.fori_loop(0, 8, step, 0)
    for c in own + [fwd_y, fwd_x] + list(fwd_p.values()):
        c.wait_send()


AG_SEMS = [pltpu.SemaphoreType.DMA((14,)), pltpu.SemaphoreType.DMA((8, 2))]


def rs_run(stage, fp, fx, fy, send, recv, produce, finish, after=None):
    t = lax.axis_index('tp')
    partner, xn, yn = greet(t)

    def copy(src, dst, sem, dev):
        return pltpu.make_async_remote_copy(src_ref=src, dst_ref=dst, send_sem=send.at[sem], recv_sem=recv.at[sem], device_id={'tp': dev}, device_id_type=MESH)

    def half(h):
        return pl.ds(h * HALF, HALF)

    sx = [copy(stage.at[1, half(1), :], fx.at[0], 4, xn), copy(stage.at[3, half(0), :], fx.at[1], 5, xn), copy(stage.at[5, half(0), :], fx.at[2], 6, xn)]
    sy = [copy(stage.at[1, half(0), :], fy.at[0], 7, yn), copy(stage.at[3, half(1), :], fy.at[1], 8, yn), copy(stage.at[5, half(1), :], fy.at[2], 9, yn)]

    def add(i, first, count, src, src_first):
        def body(r, c):
            a = pl.ds(pl.multiple_of(first + r * 32, 32), 32)
            b = pl.ds(pl.multiple_of(src_first + r * 32, 32), 32)
            stage[i, a, :] = (stage[i, a, :].astype(F32) + src[b, :].astype(F32)).astype(BF16)
            return c

        lax.fori_loop(0, count // 32, body, 0)

    def step(i, carry):
        p = i // 2
        produce(i, ag_rows(t, 2 * (7 - i)), ag_rows(t, 2 * (7 - i) + 1))
        to_partner = copy(stage.at[i], fp.at[p], p, partner)

        @pl.when(i % 2 == 0)
        def _():
            to_partner.start()

        @pl.when(i % 2 == 1)
        def _():
            to_partner.wait_recv()
            add(i, 0, SHARD, fp.at[p], 0)

        @pl.when(i == 1)
        def _():
            sx[0].start()
            sy[0].start()

        @pl.when(i == 3)
        def _():
            sx[1].start()
            sy[1].start()

        @pl.when(i == 5)
        def _():
            sy[0].wait_recv()
            add(5, 0, HALF, fy.at[0], 0)
            sx[2].start()
            sx[0].wait_recv()
            add(5, HALF, HALF, fx.at[0], 0)
            sy[2].start()

        if after is not None:
            after(i)
        return carry

    lax.fori_loop(0, 8, step, 0)
    sy[1].wait_recv()
    sx[1].wait_recv()
    sx[2].wait_recv()
    sy[2].wait_recv()

    def last(r, c):
        lo = pl.ds(pl.multiple_of(r * 32, 32), 32)
        hi = pl.ds(pl.multiple_of(HALF + r * 32, 32), 32)
        finish(lo, (stage[7, lo, :].astype(F32) + fy[1, lo, :].astype(F32)) + fx[2, lo, :].astype(F32))
        finish(hi, (stage[7, hi, :].astype(F32) + fx[1, lo, :].astype(F32)) + fy[2, lo, :].astype(F32))
        return c

    lax.fori_loop(0, HALF // 32, last, 0)
    for q in range(4):
        copy(stage.at[2 * q], fp.at[q], q, partner).wait_send()
    for c in sx + sy:
        c.wait_send()


def rs_scratch(dim):
    return [pltpu.VMEM((8, SHARD, dim), BF16), pltpu.VMEM((4, SHARD, dim), BF16), pltpu.VMEM((3, HALF, dim), BF16), pltpu.VMEM((3, HALF, dim), BF16),
            pltpu.SemaphoreType.DMA((10,)), pltpu.SemaphoreType.DMA((10,))]


VM = pl.BlockSpec(memory_space=pltpu.VMEM)
ANY = pl.BlockSpec(memory_space=pl.ANY)


def comm_call(body, name, cid, in_specs, out_specs, out_shape, scratch, flops):
    return pl.pallas_call(
        body, name=name, in_specs=in_specs, out_specs=out_specs, out_shape=out_shape, scratch_shapes=scratch,
        compiler_params=pltpu.CompilerParams(collective_id=cid, has_side_effects=True, vmem_limit_bytes=60 * 1024 * 1024),
        cost_estimate=pl.CostEstimate(flops=flops, bytes_accessed=20_000_000, transcendentals=0),
    )


def rs_rows(rows, gain):
    seq, dim = rows.shape

    def body(rows_ref, g_ref, e_ref, u_ref, stage, fp, fx, fy, send, recv, load):
        t = lax.axis_index('tp')

        def fetch(i):
            return [pltpu.make_async_copy(rows_ref.at[ag_rows(t, 2 * (7 - i) + n), :], stage.at[i, n * HALF:(n + 1) * HALF, :], load.at[i, n]) for n in (0, 1)]

        for i in range(8):
            for c in fetch(i):
                c.start()

        def produce(i, r0, r1):
            for c in fetch(i):
                c.wait()

        def finish(at, val):
            e_b = val.astype(BF16)
            e_ref[at, :] = e_b
            x = e_b.astype(F32)
            u_ref[at, :] = (x * rms_inv(x) * g_ref[...]).astype(BF16)

        rs_run(stage, fp, fx, fy, send, recv, produce, finish)

    loc = jax.ShapeDtypeStruct((SHARD, dim), BF16)
    return comm_call(body, 'rs_rows', 0, [ANY, VM], [VM, VM], [loc, loc], rs_scratch(dim) + [pltpu.SemaphoreType.DMA((8, 2))], 40_000_000_000)(rows, gain)


def ag_proj(x, w_q, w_dkv, g_kv, w_uk, w_uv, cos_t, sin_t):
    dim = x.shape[1]
    seq = 8 * SHARD
    heads, qk, _ = w_q.shape
    lat = w_dkv.shape[0]
    rank, nope = w_uk.shape[1:]
    vdim = w_uv.shape[2]

    def body(x_ref, wq_ref, wl_hbm, g_ref, wk_ref, wv_ref, cos_ref, sin_ref, x_out, q_ref, l_ref, c_ref, k_ref, kt_ref, v_ref, vt_ref, full, send, recv, sem, wl, wsem):
        w_load = pltpu.make_async_copy(wl_hbm, wl, wsem.at[0])
        w_load.start()

        def compute(i, r0, r1):
            @pl.when(i == 0)
            def _():
                w_load.wait()

            x_b = jnp.concatenate([full[r0, :], full[r1, :]], axis=0)
            l_b = dot_nt(x_b, wl[...])
            kv = l_b[:, :rank]
            c_b = (kv * rms_inv(kv) * g_ref[...]).astype(BF16)
            q_all = [dot_nt(x_b, wq_ref[hd]).astype(BF16) for hd in range(heads)]
            k_all = [dot_nn(c_b, wk_ref[hd]) for hd in range(heads)]
            v_all = [dot_nn(c_b, wv_ref[hd]) for hd in range(heads)]
            for n, at in enumerate((r0, r1)):
                part = slice(n * HALF, (n + 1) * HALF)
                pltpu.make_async_copy(full.at[at, :], x_out.at[at, :], sem.at[2 * i + n]).start()
                cos_b = cos_ref[at, :]
                sin_b = sin_ref[at, :]
                l_ref[at, :] = l_b[part, :]
                c_ref[at, :] = c_b[part, :]
                pe = rope(l_b[part, rank:], cos_b, sin_b)
                for hd in range(heads):
                    q_b, k_b, v_b = q_all[hd][part, :], k_all[hd][part, :], v_all[hd][part, :]
                    q_ref[hd, at, :nope] = q_b[:, :nope]
                    q_ref[hd, at, nope:] = rope(q_b[:, nope:].astype(F32), cos_b, sin_b).astype(BF16)
                    k_ref[hd, at, :nope] = k_b.astype(BF16)
                    k_ref[hd, at, nope:] = pe.astype(BF16)
                    kt_ref[hd, :nope, at] = k_b.T.astype(BF16)
                    kt_ref[hd, nope:, at] = pe.T.astype(BF16)
                    v_ref[hd, at, :] = v_b.astype(BF16)
                    vt_ref[hd, :, at] = v_b.T.astype(BF16)

        ag_run(x_ref, full, send, recv, compute)
        for i in range(16):
            at = half_rows(i // 2, i % 2)
            pltpu.make_async_copy(full.at[at, :], x_out.at[at, :], sem.at[i]).wait()

    shapes = [((seq, dim), BF16), ((heads, seq, qk), BF16), ((seq, lat), F32), ((seq, rank), BF16), ((heads, seq, qk), BF16), ((heads, qk, seq), BF16), ((heads, seq, vdim), BF16), ((heads, vdim, seq), BF16)]
    return comm_call(body, 'ag_proj', 1, [VM, VM, ANY] + [VM] * 5, [ANY] + [VM] * 7, [jax.ShapeDtypeStruct(s, d) for s, d in shapes],
                     [pltpu.VMEM((seq, dim), BF16)] + AG_SEMS + [pltpu.SemaphoreType.DMA((16,)), pltpu.VMEM((lat, dim), BF16), pltpu.SemaphoreType.DMA((1,))], 40_000_000_000)(x, w_q, w_dkv, g_kv, w_uk, w_uv, cos_t, sin_t)


def attn_out_rs(o, w_o, e_loc, gain, dy, w_down):
    dim = w_o.shape[1]
    seq = dy.shape[0]
    ffn = w_down.shape[0]
    tiles = col_tiles(ffn)

    def body(o_ref, w_ref, e_ref, g_ref, dy_ref, wd_hbm, h_ref, z_ref, dh_ref, stage, fp, fx, fy, send, recv, wd, dyb, st, wsem, dsem, osem):
        def block(i):
            return pl.ds(pl.multiple_of(i * SHARD, SHARD), SHARD)

        def dy_copy(i):
            return pltpu.make_async_copy(dy_ref.at[block(i), :], dyb.at[i % 2], dsem.at[i % 2])

        def dh_copy(i):
            return pltpu.make_async_copy(st.at[i % 2], dh_ref.at[block(i), :], osem.at[i % 2])

        w_load = pltpu.make_async_copy(wd_hbm, wd, wsem.at[0])
        w_load.start()
        dy_copy(0).start()

        def produce(i, r0, r1):
            o_b = jnp.concatenate([o_ref[r0, :], o_ref[r1, :]], axis=0)
            for n in range(dim // 256):
                cols = slice(n * 256, (n + 1) * 256)
                stage[i, :, cols] = dot_nn(o_b, w_ref[:, cols]).astype(BF16)

        def after(i):
            @pl.when(i == 0)
            def _():
                w_load.wait()

            @pl.when(i < 7)
            def _():
                dy_copy(i + 1).start()

            @pl.when(i >= 2)
            def _():
                dh_copy(i - 2).wait()

            dy_copy(i).wait()
            dy_b = dyb[i % 2]
            for cols in tiles:
                st[i % 2, :, cols] = dot_nt(dy_b, wd[cols, :])
            dh_copy(i).start()

        def finish(at, val):
            h_b = (e_ref[at, :].astype(F32) + val.astype(BF16).astype(F32)).astype(BF16)
            h_ref[at, :] = h_b
            x = h_b.astype(F32)
            z_ref[at, :] = (x * rms_inv(x) * g_ref[...]).astype(BF16)

        rs_run(stage, fp, fx, fy, send, recv, produce, finish, after)
        dh_copy(6).wait()
        dh_copy(7).wait()

    loc = jax.ShapeDtypeStruct((SHARD, dim), BF16)
    return comm_call(body, 'attn_out_rs', 2, [VM] * 4 + [ANY] * 2, [VM, VM, ANY], [loc, loc, jax.ShapeDtypeStruct((seq, ffn), F32)],
                     rs_scratch(dim) + [pltpu.VMEM((ffn, dim), BF16), pltpu.VMEM((2, SHARD, dim), BF16), pltpu.VMEM((2, SHARD, ffn), F32),
                                        pltpu.SemaphoreType.DMA((1,)), pltpu.SemaphoreType.DMA((2,)), pltpu.SemaphoreType.DMA((2,))], 40_000_000_000)(o, w_o, e_loc, gain, dy, w_down)


def col_tiles(width):
    return [slice(a, min(a + 256, width)) for a in range(0, width, 256)]


def ag_mlp(z, dh, w_gate, w_up):
    dim = z.shape[1]
    seq = 8 * SHARD
    ffn = w_gate.shape[0]
    tiles = col_tiles(ffn)

    def body(z_ref, dh_ref, wg_hbm, wu_hbm, z_out, hid_out, dg_out, du_out, full, wg, wu, dhb, st, send, recv, zsem, wsem, dsem, osem):
        t = lax.axis_index('tp')
        loads = [pltpu.make_async_copy(a, b, wsem.at[n]) for n, (a, b) in enumerate(((wg_hbm, wg), (wu_hbm, wu)))]
        for c in loads:
            c.start()

        def dh_copies(i):
            return [pltpu.make_async_copy(dh_ref.at[ag_rows(t, 2 * i + n), :], dhb.at[i % 2, n * HALF:(n + 1) * HALF, :], dsem.at[i % 2, n]) for n in (0, 1)]

        def z_copy(i):
            return pltpu.make_async_copy(full.at[ag_rows(t, i), :], z_out.at[ag_rows(t, i), :], zsem.at[i])

        def out_copies(i):
            return [pltpu.make_async_copy(st.at[n, i % 2, m * HALF:(m + 1) * HALF, :], o.at[ag_rows(t, 2 * i + m), :], osem.at[n, i % 2, m])
                    for n, o in enumerate((hid_out, dg_out, du_out)) for m in (0, 1)]

        for c in dh_copies(0):
            c.start()

        def compute(i, r0, r1):
            @pl.when(i == 0)
            def _():
                for c in loads:
                    c.wait()

            @pl.when(i < 7)
            def _():
                for c in dh_copies(i + 1):
                    c.start()

            @pl.when(i >= 2)
            def _():
                for c in out_copies(i - 2):
                    c.wait()

            z_copy(2 * i).start()
            z_copy(2 * i + 1).start()
            for c in dh_copies(i):
                c.wait()
            z_b = jnp.concatenate([full[r0, :], full[r1, :]], axis=0)
            for cols in tiles:
                gate = dot_nt(z_b, wg[cols, :])
                up = dot_nt(z_b, wu[cols, :])
                d_hid = dhb[i % 2, :, cols]
                sig = jax.nn.sigmoid(gate)
                act = gate * sig
                st[0, i % 2, :, cols] = (act * up).astype(BF16)
                st[1, i % 2, :, cols] = (d_hid * up * sig * (1.0 + gate * (1.0 - sig))).astype(BF16)
                st[2, i % 2, :, cols] = (d_hid * act).astype(BF16)
            for c in out_copies(i):
                c.start()

        ag_run(z_ref, full, send, recv, compute)
        for i in (6, 7):
            for c in out_copies(i):
                c.wait()
        for i in range(16):
            z_copy(i).wait()

    act = jax.ShapeDtypeStruct((seq, ffn), BF16)
    return comm_call(body, 'ag_mlp', 3, [VM, ANY, ANY, ANY], [ANY] * 4, [jax.ShapeDtypeStruct((seq, dim), BF16), act, act, act],
                     [pltpu.VMEM((seq, dim), BF16), pltpu.VMEM((ffn, dim), BF16), pltpu.VMEM((ffn, dim), BF16),
                      pltpu.VMEM((2, SHARD, ffn), F32), pltpu.VMEM((3, 2, SHARD, ffn), BF16)] + AG_SEMS
                     + [pltpu.SemaphoreType.DMA((16,)), pltpu.SemaphoreType.DMA((2,)), pltpu.SemaphoreType.DMA((2, 2)), pltpu.SemaphoreType.DMA((3, 2, 2))],
                     60_000_000_000)(z, dh, w_gate, w_up)


def mlp_back_rs(d_gate, d_up, w_gate, w_up, h_loc, gain, dy):
    ffn, dim = w_gate.shape

    def body(dg_ref, du_ref, wg_hbm, wu_hbm, h_ref, g_ref, dy_ref, res_ref, resb_ref, dgain_ref, stage, fp, fx, fy, send, recv, wg, wu, blk, wsem, bsem):
        t = lax.axis_index('tp')
        loads = [pltpu.make_async_copy(a, b, wsem.at[n]) for n, (a, b) in enumerate(((wg_hbm, wg), (wu_hbm, wu)))]

        def fetch(i):
            return [pltpu.make_async_copy(r.at[ag_rows(t, 2 * (7 - i) + m), :], blk.at[n, i % 2, m * HALF:(m + 1) * HALF, :], bsem.at[n, i % 2, m])
                    for n, r in enumerate((dg_ref, du_ref)) for m in (0, 1)]

        for c in fetch(0) + loads:
            c.start()

        def produce(i, r0, r1):
            @pl.when(i < 7)
            def _():
                for c in fetch(i + 1):
                    c.start()

            for c in fetch(i):
                c.wait()

            @pl.when(i == 0)
            def _():
                for c in loads:
                    c.wait()

            dg_b = blk[0, i % 2]
            du_b = blk[1, i % 2]
            for n in range(dim // 256):
                cols = slice(n * 256, (n + 1) * 256)
                stage[i, :, cols] = (dot_nn(dg_b, wg[:, cols]) + dot_nn(du_b, wu[:, cols])).astype(BF16)

        dgain_ref[...] = jnp.zeros_like(dgain_ref)

        def finish(at, val):
            d_x, d_g = rms_back(h_ref[at, :].astype(F32), g_ref[...], val.astype(BF16).astype(F32))
            dgain_ref[...] = dgain_ref[...] + d_g
            res = dy_ref[at, :].astype(F32) + d_x
            res_ref[at, :] = res
            resb_ref[at, :] = res.astype(BF16)

        rs_run(stage, fp, fx, fy, send, recv, produce, finish)

    loc = lambda d: jax.ShapeDtypeStruct((SHARD, dim), d)
    return comm_call(body, 'mlp_back_rs', 4, [ANY] * 4 + [VM] * 3, [VM] * 3, [loc(F32), loc(BF16), jax.ShapeDtypeStruct((1, dim), F32)],
                     rs_scratch(dim) + [pltpu.VMEM((ffn, dim), BF16), pltpu.VMEM((ffn, dim), BF16), pltpu.VMEM((2, 2, SHARD, ffn), BF16),
                                        pltpu.SemaphoreType.DMA((2,)), pltpu.SemaphoreType.DMA((2, 2, 2))], 60_000_000_000)(d_gate, d_up, w_gate, w_up, h_loc, gain, dy)


def ag_dattn(x, w_o, hidden, w_down):
    dim = x.shape[1]
    seq, ffn = hidden.shape
    width = w_o.shape[0]

    def body(x_ref, w_ref, hid_ref, wd_hbm, x_out, do_ref, y_out, full, send, recv, sem, wd, hb, yb, wsem, hsem, ysem):
        def block(i):
            return pl.ds(pl.multiple_of(i * SHARD, SHARD), SHARD)

        def h_copy(i):
            return pltpu.make_async_copy(hid_ref.at[block(i), :], hb.at[i % 2], hsem.at[i % 2])

        def y_copy(i):
            return pltpu.make_async_copy(yb.at[i % 2], y_out.at[block(i), :], ysem.at[i % 2])

        w_load = pltpu.make_async_copy(wd_hbm, wd, wsem.at[0])
        w_load.start()
        h_copy(0).start()

        def before(i):
            @pl.when(i == 0)
            def _():
                w_load.wait()

            @pl.when(i < 7)
            def _():
                h_copy(i + 1).start()

            @pl.when(i >= 2)
            def _():
                y_copy(i - 2).wait()

            h_copy(i).wait()
            h_b = hb[i % 2]
            for n in range(dim // 256):
                cols = slice(n * 256, (n + 1) * 256)
                yb[i % 2, :, cols] = dot_nn(h_b, wd[:, cols]).astype(BF16)
            y_copy(i).start()

        def compute(i, r0, r1):
            x_b = jnp.concatenate([full[r0, :], full[r1, :]], axis=0)
            d_o = dot_nt(x_b, w_ref[...]).astype(BF16)
            for n, at in enumerate((r0, r1)):
                pltpu.make_async_copy(full.at[at, :], x_out.at[at, :], sem.at[2 * i + n]).start()
                do_ref[at, :] = d_o[n * HALF:(n + 1) * HALF, :]

        ag_run(x_ref, full, send, recv, compute, before)
        y_copy(6).wait()
        y_copy(7).wait()
        for i in range(16):
            at = half_rows(i // 2, i % 2)
            pltpu.make_async_copy(full.at[at, :], x_out.at[at, :], sem.at[i]).wait()

    big = jax.ShapeDtypeStruct((seq, dim), BF16)
    return comm_call(body, 'ag_dattn', 5, [VM, VM, ANY, ANY], [ANY, VM, ANY], [big, jax.ShapeDtypeStruct((seq, width), BF16), big],
                     [pltpu.VMEM((seq, dim), BF16)] + AG_SEMS + [pltpu.SemaphoreType.DMA((16,)), pltpu.VMEM((ffn, dim), BF16), pltpu.VMEM((2, SHARD, ffn), BF16),
                      pltpu.VMEM((2, SHARD, dim), BF16), pltpu.SemaphoreType.DMA((1,)), pltpu.SemaphoreType.DMA((2,)), pltpu.SemaphoreType.DMA((2,))], 40_000_000_000)(x, w_o, hidden, w_down)


def sum_small(x):
    width = x.shape[1]

    def body(x_ref, out_ref, buf, send, recv):
        t = lax.axis_index('tp')
        peers = [xor_bits(t, u) for u in range(1, 8)]
        barrier = pltpu.get_barrier_semaphore()
        for peer in peers:
            pl.semaphore_signal(barrier, inc=1, device_id={'tp': peer}, device_id_type=MESH)
        pl.semaphore_wait(barrier, 7)
        copies = [pltpu.make_async_remote_copy(src_ref=x_ref, dst_ref=buf.at[t], send_sem=send.at[n], recv_sem=recv.at[n], device_id={'tp': peer}, device_id_type=MESH)
                  for n, peer in enumerate(peers)]
        for c in copies:
            c.start()
        buf[t] = x_ref[...]
        for c in copies:
            c.wait()
        total = buf[0]
        for d in range(1, 8):
            total = total + buf[d]
        out_ref[...] = total

    return comm_call(body, 'sum_small', 7, [VM], VM, jax.ShapeDtypeStruct(x.shape, F32),
                     [pltpu.VMEM((8, 1, width), F32), pltpu.SemaphoreType.DMA((7,)), pltpu.SemaphoreType.DMA((7,))], 1_000_000_000)(x)


def attn_back_rs(d_query, d_knope, d_kpe, d_value, latent, g_kv, w_uk, w_uv, w_q, w_dkv, cos_t, sin_t, e_loc, g_attn, d_res):
    heads, _, dim = w_q.shape
    seq, lat = latent.shape
    rank = w_uk.shape[1]
    wide = -(-(dim + lat) // 128) * 128

    def body(dq_ref, dk_ref, dkp_ref, dv_ref, l_ref, gkv_ref, wk_ref, wv_ref, wq_ref, wl_ref, cos_ref, sin_ref, e_ref, g_ref, res_ref,
             de_ref, dgkv_ref, dgain_ref, stage, fp, fx, fy, send, recv):
        dgkv_ref[...] = jnp.zeros_like(dgkv_ref)
        dgain_ref[...] = jnp.zeros_like(dgain_ref)

        def produce(i, r0, r1):
            def both(ref, *lead):
                return jnp.concatenate([ref[lead + (r0, slice(None))], ref[lead + (r1, slice(None))]], axis=0)

            d_c = None
            for hd in range(heads):
                part = dot_nt(both(dk_ref, hd), wk_ref[hd]) + dot_nt(both(dv_ref, hd), wv_ref[hd])
                d_c = part if d_c is None else d_c + part
            d_kv, d_g = rms_back(both(l_ref)[:, :rank], gkv_ref[...], d_c.astype(BF16).astype(F32))
            dgkv_ref[...] = dgkv_ref[...] + d_g
            d_pe = both(dkp_ref, 0)
            for hd in range(1, heads):
                d_pe = d_pe + both(dkp_ref, hd)
            d_pe = unrope(d_pe.astype(BF16).astype(F32), both(cos_ref), both(sin_ref))
            stage[i, :, dim:dim + rank] = d_kv.astype(BF16)
            stage[i, :, dim + rank:dim + lat] = d_pe.astype(BF16)
            stage[i, :, dim + lat:] = jnp.zeros((SHARD, wide - dim - lat), BF16)
            dl_b = stage[i, :, dim:dim + lat]
            dq_b = [jnp.concatenate([dq_ref[hd, :, r].astype(F32).T for r in (r0, r1)], axis=0).astype(BF16) for hd in range(heads)]
            for n in range(dim // 256):
                cols = slice(n * 256, (n + 1) * 256)
                val = dot_nn(dl_b, wl_ref[:, cols])
                for hd in range(heads):
                    val = val + dot_nn(dq_b[hd], wq_ref[hd, :, cols])
                stage[i, :, cols] = val.astype(BF16)

        def finish(at, val):
            d_x, d_g = rms_back(e_ref[at, :].astype(F32), g_ref[...], val[:, :dim].astype(BF16).astype(F32))
            dgain_ref[...] = dgain_ref[...] + d_g
            de_ref[at, :dim] = (res_ref[at, :] + d_x).astype(BF16)
            de_ref[at, dim:] = val[:, dim:].astype(BF16)

        rs_run(stage, fp, fx, fy, send, recv, produce, finish)

    return comm_call(body, 'attn_back_rs', 6, [VM] * 15, [VM] * 3,
                     [jax.ShapeDtypeStruct((SHARD, wide), BF16), jax.ShapeDtypeStruct((1, rank), F32), jax.ShapeDtypeStruct((1, dim), F32)],
                     rs_scratch(wide), 40_000_000_000)(d_query, d_knope, d_kpe, d_value, latent, g_kv, w_uk, w_uv, w_q, w_dkv, cos_t, sin_t, e_loc, g_attn, d_res)


def gather_seq(x):
    return lax.all_gather(x, 'tp', axis=0, tiled=True)


def scatter_seq(x):
    return lax.psum_scatter(x, 'tp', scatter_dimension=0, tiled=True)


def solution(mesh):
    def device_step(tokens, embed_table, w_q, w_dkv, g_kv, w_uk, w_uv, w_o, g_attn, g_mlp, w_gate, w_up, w_down, d_out):
        vocab_local, model_dim = embed_table.shape
        seq = tokens.shape[1]
        heads, qk = w_q.shape[1:]
        vdim = w_uv.shape[2]
        scale = qk ** -0.5
        dy_loc = d_out[0]
        gkv, gat, gml = g_kv.reshape(1, -1), g_attn.reshape(1, -1), g_mlp.reshape(1, -1)
        wuk, wuv = (jnp.swapaxes(w, 0, 1) for w in (w_uk, w_uv))
        wq, wl, wg, wu = jnp.transpose(w_q, (1, 2, 0)), w_dkv.T, w_gate.T, w_up.T
        wo = w_o.reshape(heads * vdim, model_dim)
        cos_t, sin_t = rope_tables(seq, qk - w_uk.shape[2])

        dy_full = gather_seq(dy_loc)
        local_ids = tokens[0] - lax.axis_index('tp') * vocab_local
        owned = (local_ids >= 0) & (local_ids < vocab_local)
        slots, pos = lax.sort((jnp.where(owned, local_ids, vocab_local), lax.iota(jnp.int32, seq)), num_keys=1)
        slots = jnp.concatenate([slots, jnp.full((128,), vocab_local, jnp.int32)])
        cnt = jnp.sum(owned.astype(jnp.int32)).reshape(1)
        rows = gather_rows(slots, pos, cnt, embed_table, seq)
        e_loc, u_loc = rs_rows(rows, gat)
        u, q, latent, c_kv, k, kt, v, vt = ag_proj(u_loc, wq, wl, gkv, wuk, wuv, cos_t, sin_t)
        o, lse = attn_fwd(q, k, vt, scale)
        h_loc, z_loc, d_hidden = attn_out_rs(o, wo, e_loc, gml, dy_full, w_down)
        z, hidden, d_gate, d_up = ag_mlp(z_loc, d_hidden, wg, wu)
        d_res, d_res_b, dg_mlp = mlp_back_rs(d_gate, d_up, wg, wu, h_loc, gml, dy_loc)
        d_res_full, d_o, mlp_part = ag_dattn(d_res_b, wo, hidden, w_down)

        mlp_loc = scatter_seq(mlp_part)
        half = cos_t.shape[1] // 2
        d_query, d_knope, d_kpe, d_value = attn_bwd(q, k, kt, v, d_o, o, lse, cos_t[:, :half].T, sin_t[:, half:].T, scale)
        dw_gate = matmul_f32('sd,sf->df', z, d_gate)
        dw_up = matmul_f32('sd,sf->df', z, d_up)
        dw_gate, dw_up, mlp_loc, d_query = lax.optimization_barrier((dw_gate, dw_up, mlp_loc, d_query))
        layer_out = (h_loc.astype(F32) + mlp_loc.astype(F32)).astype(BF16)
        back, dg_kv, dg_attn = attn_back_rs(d_query, d_knope, d_kpe, d_value, latent, gkv, wuk, wuv, wq, wl, cos_t, sin_t, e_loc, gat, d_res)

        back_full = gather_seq(back)
        dw_down = matmul_f32('sf,sd->fd', hidden, dy_full)
        dw_q = matmul_f32('sd,hes->dhe', u, d_query)
        dw_uk = matmul_f32('sc,hse->che', c_kv, d_knope)
        dw_uv = matmul_f32('sc,hsv->chv', c_kv, d_value)
        dw_o = matmul_f32('sv,sd->vd', o, d_res_full).reshape(w_o.shape)
        gains = sum_small(jnp.concatenate([dg_kv, dg_attn, dg_mlp], axis=1))[0]
        zeros = zero_rows(vocab_local, model_dim, back)
        back_full, dw_down, dw_q, dw_uk, dw_uv, dw_o, gains, zeros = lax.optimization_barrier((back_full, dw_down, dw_q, dw_uk, dw_uv, dw_o, gains, zeros))
        dw_dkv = matmul_f32('sd,sc->dc', u, back_full[:, model_dim:model_dim + w_dkv.shape[1]])
        d_table = scatter_rows(slots, pos, cnt, back_full, zeros)
        rank = g_kv.shape[0]
        dg_kv, dg_attn, dg_mlp = gains[:rank], gains[rank:rank + model_dim], gains[rank + model_dim:]
        return layer_out[None], d_table, dw_q, dw_dkv, dg_kv, dw_uk, dw_uv, dw_o, dg_attn, dg_mlp, dw_gate, dw_up, dw_down

    row_spec = P('dp', 'tp', None)
    head_spec = P(None, 'tp', None)
    in_specs = (P('dp', None), P('tp', None), head_spec, P(None, None), P(None), head_spec, head_spec, P('tp', None, None), P(None), P(None), P(None, 'tp'), P(None, 'tp'), P('tp', None), row_spec)
    out_specs = (row_spec, P(('dp', 'tp'), None), P('dp', 'tp', None), P('dp', None), P('dp'), P('dp', 'tp', None), P('dp', 'tp', None), P(('dp', 'tp'), None, None), P('dp'), P('dp'), P('dp', 'tp'), P('dp', 'tp'), P(('dp', 'tp'), None))
    return jax.shard_map(device_step, mesh=mesh, in_specs=in_specs, out_specs=out_specs, check_vma=False)
```

time: 718 us -> 589 us (0.82)
  local copies, waits for them, and re-layouts: 79.5 us -> 12.1 us
  other arithmetic: 60.4 us -> 9.21 us
  Pallas kernels: 423 us -> 450 us
  blocking collectives: 23.5 us -> 0 us
  matrix products: 106 us -> 83 us
  waiting for transfers between devices: 0.78 us -> 9.33 us
    unnamed x122 -> x38, local copies, waits for them, and re-layouts: 39 us -> 8.42 us
    pallas_call x7 -> x9, Pallas kernels: 358 us -> 385 us  [the longest x1 63.3 us: attn_back_rs(): comm_call(body, 'attn_back_rs', 6, [VM] * 15, [VM] * 3, [jax.ShapeDtypeSt...]
    psum x1 -> x0, blocking collectives: 23.5 us -> none  [layer_pass(): lax.psum((dw_dkv_part, dg_kv_part, dg_attn_part, dg_mlp_part), 'tp')]
    broadcast_in_dim x2 -> x0, local copies, waits for them, and re-layouts: 16.9 us -> none  [the longest x1 16.8 us: device_step(): jnp.zeros((vocab_local, model_dim), BF16)]
    reduce_sum x7 -> x0, other arithmetic: 16.4 us -> none  [the longest x3 5.8 us: rms_norm(): inv_rms = lax.rsqrt(jnp.mean(x_in * x_in, axis=-1, keepdims=True) + EPSILON)]
    convert_element_type x9 -> x0, other arithmetic: 14.6 us -> none  [the longest x1 4.48 us: layer_pass(): d_embed = (d_residual + d_emb_norm).astype(BF16)]
    dot_general x11 -> x8, matrix products: 95.6 us -> 83 us  [matmul_f32(): return jnp.einsum(form, lhs, rhs, preferred_element_type=jnp.float32)]
    unnamed x2 -> x0, matrix products: 10.3 us -> none
  transfers between devices with their start and end apart: 4 -> 3, of which waited for: 0 -> 1; matrix products, arithmetic and copies ran while one was open for 29% -> 15% of each run, Pallas kernels for 43% -> 31%
where the time goes in v3:
time: 589 us; the launch traced here: 578 us
  Pallas kernels  450 us (76%)
  matrix products  83 us (14%)
  between operations  14.5 us (2%)
  local copies, waits for them, and re-layouts  12.1 us (2%)
  waiting for transfers between devices  9.33 us (2%)
  other arithmetic  9.21 us (2%)
    dot_general x8, matrix products, matmul_f32(): return jnp.einsum(form, lhs, rhs, preferred_element_type=jnp.float32)  83 us
    pallas_call x1, Pallas kernels, attn_back_rs(): comm_call(body, 'attn_back_rs', 6, [VM] * 15, [VM] * 3, [jax.ShapeDtypeSt...  63.3 us
    pallas_call x1, Pallas kernels, rs_rows(): comm_call(body, 'rs_rows', 0, [ANY, VM], [VM, VM], [loc, loc], rs_scratch...  57.7 us
    pallas_call x1, Pallas kernels, mlp_back_rs(): comm_call(body, 'mlp_back_rs', 4, [ANY] * 4 + [VM] * 3, [VM] * 3, [loc(F3...  52.1 us
    pallas_call x1, Pallas kernels, ag_proj(): comm_call(body, 'ag_proj', 1, [VM, VM, ANY] + [VM] * 5, [ANY] + [VM] * 7,...  49.9 us
    pallas_call x1, Pallas kernels, ag_mlp(): comm_call(body, 'ag_mlp', 3, [VM, ANY, ANY, ANY], [ANY] * 4, [jax.ShapeDt...  47.1 us
    pallas_call x1, Pallas kernels, attn_out_rs(): comm_call(body, 'attn_out_rs', 2, [VM] * 4 + [ANY] * 2, [VM, VM, ANY], [l...  46.6 us
    pallas_call x1, Pallas kernels, ag_dattn(): comm_call(body, 'ag_dattn', 5, [VM, VM, ANY, ANY], [ANY, VM, ANY], [big,...  43.1 us
  transfers between devices with their start and end apart: 3, of which 1 were waited for; matrix products, arithmetic and copies ran while one was open for 15% of the time, Pallas kernels for 31%

profile of v3, /device:TPU:0, one launch (start us, length us, event | category | flops | bytes accessed | tf_op | source)
XLA Modules:
  0.0 578.4 jit_solution(2351704505666360029)
XLA Ops:
  7.2 0.0 all-gather.6.cloned.1.call-start
  7.2 0.7 all-gather.6.cloned.1.call-update
  7.9 0.0 reduce-scatter.2.cloned.1.call-start
  8.0 0.7 broadcast_subtract_fusion
  8.7 0.7 convert_reduce_fusion
  9.4 5.0 sort.15
  14.4 0.6 concatenate.6.slot_ref
  15.0 1.9 copy_bitcast_fusion
  16.9 20.6 %gather_rows.1.rows_ref = bf16[2048,2048]{1,0:T(8,128)(2,1)} custom-call(s32[2176]{0:T(1024)} %concatenate.6.slot_ref, s32[2048]{0:T(1024)} %get-tuple-element.60.pos_ref, s32[1]{0:T(128)} %bitcast.1.cnt_ref, bf16[12800,2048]{1,0:T(8,128)(2,1)} %tab_ref.1), custom_call_target="tpu_custom_call" | custom-call | flops 20000000000 | bytes 24000000 | tf_op jit(solution)/shard_map/gather_rows/pallas_call | solution.py:108
  37.5 57.7 %rs_rows.1 = (bf16[256,2048]{1,0:T(8,128)(2,1)}, bf16[256,2048]{1,0:T(8,128)(2,1)}) custom-call(bf16[2048,2048]{1,0:T(8,128)(2,1)} %gather_rows.1.rows_ref, f32[1,2048]{1,0:T(1,128)} %bitcast.59), custom_call_target="tpu_custom_call" | custom-call | flops 40000000000 | bytes 20000000 | tf_op jit(solution)/shard_map/rs_rows/pallas_call | solution.py:575
  95.3 49.9 %ag_proj.1 = (bf16[2048,2048]{1,0:T(8,128)(2,1)}, bf16[2,2048,192]{2,1,0:T(8,128)(2,1)}, f32[2048,576]{1,0:T(8,128)}, bf16[2048,512]{1,0:T(8,128)(2,1)}, bf16[2,...) custom-call(bf16[256,2048]{1,0:T(8,128)(2,1)} %get-tuple-element.61., ...), custom_call_target="tpu_custom_call" | custom-call | flops 40000000000 | bytes 20000000 | tf_op jit(solution)/shard_map/ag_proj/pallas_call | solution.py:627
  145.2 1.6 copy-done.2
  146.8 1.6 copy-done.3
  148.3 1.2 copy-done.4
  149.6 10.3 %attn_fwd.1 = (bf16[2048,256]{1,0:T(8,128)(2,1)S(1)}, f32[2,1,2048]{2,1,0:T(1,128)S(1)}) custom-call(bf16[2,2048,192]{2,1,0:T(8,128)(2,1)S(1)} %copy-done.2, bf16[2,2048,192]{2,1,0:T(8,128)(2,1)S(1)} %copy-done.3, bf16[2,128,2048]{2,1,0:T(8,128)(2,1)S(1)} %copy-done.4), custom_call_target="tpu_custom_call" | custom-call | flops 20000000000 | bytes 10000000 | tf_op jit(solution)/shard_map/attn_fwd/pallas_call | solution.py:247
  159.9 0.0 copy-start
  159.9 1.0 copy-done
  160.9 0.6 copy-done.5
  161.5 46.6 %attn_out_rs.1 = (bf16[256,2048]{1,0:T(8,128)(2,1)}, bf16[256,2048]{1,0:T(8,128)(2,1)}, f32[2048,1368]{1,0:T(8,128)}) custom-call(bf16[2048,256]{1,0:T(8,128)(2,1)} %copy-done, bf16[256,2048]{1,0:T(8,128)(2,1)} %bitcast.55, bf16[256,2048]{1,0:T(8,128)(2,1)} %get-tuple-element.66.e_ref, f32[1,2048]{1,0:T(1,128)} %bitcast.57, bf16[2048,2048]{1,0:T(8,128)(2,1)} %bitcast.44, ...), custom_call_target="tpu_custom_call" | custom-call | flops 40000000000 | bytes 20000000 | tf_op jit(solution)/shard_map/attn_out_rs/pallas_call | solution.py:687
  208.1 47.1 %ag_mlp.1 = (bf16[2048,2048]{1,0:T(8,128)(2,1)}, bf16[2048,1368]{1,0:T(8,128)(2,1)}, bf16[2048,1368]{1,0:T(8,128)(2,1)}, bf16[2048,1368]{1,0:T(8,128)(2,1)}) custom-call(bf16[256,2048]{1,0:T(8,128)(2,1)} %get-tuple-element.68.z_ref, f32[2048,1368]{1,0:T(8,128)} %get-tuple-element.69.dh_ref, bf16[1368,2048]{1,0:T(8,128)(2,1)} %bitcast.47, ...), custom_call_target="tpu_custom_call" | custom-call | flops 60000002048 | bytes 20000000 | tf_op jit(solution)/shard_map/ag_mlp/pallas_call | solution.py:762
  255.2 52.1 %mlp_back_rs.1 = (f32[256,2048]{1,0:T(8,128)}, bf16[256,2048]{1,0:T(8,128)(2,1)}, f32[1,2048]{1,0:T(1,128)}) custom-call(bf16[2048,1368]{1,0:T(8,128)(2,1)} %get-tuple-element.71.dg_ref, bf16[2048,1368]{1,0:T(8,128)(2,1)} %get-tuple-element.72.du_ref, bf16[1368,2048]{1,0:T(8,128)(2,1)} %bitcast.48, bf16[1368,2048]{1,0:T(8,128)(2,1)} %bitcast.50, ...), custom_call_target="tpu_custom_call" | custom-call | flops 60000002048 | bytes 20000000 | tf_op jit(solution)/shard_map/mlp_back_rs/pallas_call | solution.py:815
  307.3 43.1 %ag_dattn.1 = (bf16[2048,2048]{1,0:T(8,128)(2,1)}, bf16[2048,256]{1,0:T(8,128)(2,1)}, bf16[2048,2048]{1,0:T(8,128)(2,1)}) custom-call(bf16[256,2048]{1,0:T(8,128)(2,1)} %get-tuple-element.73.x_ref, bf16[256,2048]{1,0:T(8,128)(2,1)} %bitcast.56, bf16[2048,1368]{1,0:T(8,128)(2,1)} %get-tuple-element.74.hid_ref, bf16[1368,2048]{1,0:T(8,128)(2,1)} %wd_hbm.3), custom_call_target="tpu_custom_call" | custom-call | flops 40000000000 | bytes 20000000 | tf_op jit(solution)/shard_map/ag_dattn/pallas_call | solution.py:874
  350.5 0.0 reduce-scatter.2.cloned.1.call-update
  350.5 0.0 all-gather.4.cloned.1.call-start
  350.6 17.8 %attn_bwd.1 = (bf16[2,192,2048]{2,1,0:T(8,128)(2,1)}, bf16[2,2048,128]{2,1,0:T(8,128)(2,1)}, f32[2,2048,64]{2,1,0:T(8,128)}, bf16[2,2048,128]{2,1,0:T(8,128)(2,1)}) custom-call(bf16[2,2048,192]{2,1,0:T(8,128)(2,1)} %get-tuple-element.62.q_ref, bf16[2,2048,192]{2,1,0:T(8,128)(2,1)} %get-tuple-element.63.k_ref, ...), custom_call_target="tpu_custom_call" | custom-call | flops 20000000000 | bytes 16000000 | tf_op jit(solution)/shard_map/attn_bwd/pallas_call | solution.py:302
  368.3 18.6 %fusion.14 = f32[2048,1368]{0,1:T(8,128)} fusion(bf16[2048,2048]{1,0:T(8,128)(2,1)} %get-tuple-element.70, bf16[2048,1368]{1,0:T(8,128)(2,1)} %get-tuple-element.72.du_ref), kind=kOutput, calls=%fused_computation.21 | convolution fusion | flops 11475615744 | bytes 25198592 | tf_op jit(solution)/shard_map/sd,sf->df/dot_general | solution.py:21
  386.9 17.4 %fusion.13 = f32[2048,1368]{0,1:T(8,128)} fusion(bf16[2048,2048]{1,0:T(8,128)(2,1)S(1)} %bitcast.66, bf16[2048,1368]{1,0:T(8,128)(2,1)} %get-tuple-element.71.dg_ref), kind=kOutput, calls=%fused_computation.20 | convolution fusion | flops 11475615744 | bytes 25198592 | tf_op jit(solution)/shard_map/sd,sf->df/dot_general | solution.py:21
  404.3 8.6 %reduce-scatter.2.cloned.1.call-done = bf16[256,2048]{1,0:T(8,128)(2,1)} async-done(((bf16[2048,2048]{1,0:T(8,128)(2,1)}), bf16[256,2048]{1,0:T(8,128)(2,1)}) %reduce-scatter.2.cloned.1.call-update) | async-done | bytes 1048592 | tf_op jit(solution)/shard_map/reduce_scatter | solution.py:960
  412.9 63.3 %attn_back_rs.1 = (bf16[256,2688]{1,0:T(8,128)(2,1)}, f32[1,512]{1,0:T(1,128)}, f32[1,2048]{1,0:T(1,128)}) custom-call(bf16[2,192,2048]{2,1,0:T(8,128)(2,1)} %get-tuple-element.82.dq_ref, bf16[2,2048,128]{2,1,0:T(8,128)(2,1)} %get-tuple-element.83.dk_ref, f32[2,2048,64]{2,1,0:T(8,128)} %get-tuple-element.84.dkp_ref, ...), custom_call_target="tpu_custom_call" | custom-call | flops 40000000000 | bytes 20000000 | tf_op jit(solution)/shard_map/attn_back_rs/pallas_call | solution.py:950
  476.2 0.0 copy-start.1
  476.2 0.0 all-gather.4.cloned.1.call-update
  476.2 2.7 fusion.4
  478.9 2.5 fusion.6
  481.4 7.6 %fusion.15 = f32[256,2048]{1,0:T(8,128)} fusion(bf16[2048,256]{1,0:T(8,128)(2,1)S(1)} %copy-done.1, bf16[2048,2048]{1,0:T(8,128)(2,1)} %get-tuple-element.91), kind=kOutput, calls=%fused_computation.22 | convolution fusion | flops 2147483648 | bytes 11534336 | tf_op jit(solution)/shard_map/sv,sd->vd/dot_general | solution.py:21
  489.2 15.2 %fusion.10 = f32[1368,2048]{1,0:T(8,128)} fusion(bf16[2048,1368]{1,0:T(8,128)(2,1)S(1)} %bitcast.64, bf16[1,2048,2048]{2,1,0:T(8,128)(2,1)S(1)} %bitcast.46), kind=kOutput, calls=%fused_computation.17 | convolution fusion | flops 11475615744 | bytes 25198592 | tf_op jit(solution)/shard_map/sf,sd->fd/dot_general | solution.py:21
  504.4 0.6 pad_maximum_fusion.x_ref
  505.0 8.3 %sum_small.1 = f32[1,4608]{1,0:T(1,128)} custom-call(f32[1,4608]{1,0:T(1,128)} %pad_maximum_fusion.x_ref), custom_call_target="tpu_custom_call" | custom-call | flops 1000000000 | bytes 20000000 | tf_op jit(solution)/shard_map/sum_small/pallas_call | solution.py:901
  513.4 0.8 reduce
  514.1 1.4 fusion.8
  515.5 9.0 %fusion = f32[2048,2,192]{0,2,1:T(8,128)} fusion(bf16[2,192,2048]{2,1,0:T(8,128)(2,1)} %get-tuple-element.82.dq_ref, bf16[2048,2048]{1,0:T(8,128)(2,1)} %get-tuple-element.89), kind=kOutput, calls=%fused_computation | convolution fusion | flops 3221225472 | bytes 13107200 | tf_op jit(solution)/shard_map/sd,hes->dhe/dot_general | solution.py:21
  524.5 17.0 %zero_rows.1.zero_ref = bf16[12800,2048]{1,0:T(8,128)(2,1)} custom-call(bf16[256,2688]{1,0:T(8,128)(2,1)} %get-tuple-element.88.after_ref), custom_call_target="tpu_custom_call" | custom-call | flops 15000000512 | bytes 52000000 | tf_op jit(solution)/shard_map/zero_rows/pallas_call | solution.py:202
  541.5 0.0 all-gather.4.cloned.1.call-done.de_ref
  541.5 0.6 slice.21
  542.1 0.6 fusion.12
  542.7 10.0 %fusion.2 = f32[2048,576]{0,1:T(8,128)} fusion(bf16[2048,2048]{1,0:T(8,128)(2,1)} %get-tuple-element.89, bf16[2048,2688]{1,0:T(8,128)(2,1)} %all-gather.4.cloned.1.call-done.de_ref), kind=kOutput, calls=%fused_computation.2 | convolution fusion | flops 4831838208 | bytes 15728640 | tf_op jit(solution)/shard_map/sd,sc->dc/dot_general | solution.py:21
  552.7 16.3 %scatter_rows.1 = bf16[12800,2048]{1,0:T(8,128)(2,1)} custom-call(s32[2176]{0:T(1024)} %concatenate.6.slot_ref, s32[2048]{0:T(1024)} %get-tuple-element.60.pos_ref, s32[1]{0:T(128)} %bitcast.1.cnt_ref, bf16[2048,2688]{1,0:T(8,128)(2,1)} %all-gather.4.cloned.1.call-done.de_ref, bf16[12800,2048]{1,0:T(8,128)(2,1)} %zero_rows.1.zero_ref), custom_call_target="tpu_custom_call", output_to_operand_aliasing={{}: (4, {})} | custom-call | flops 20000000000 | bytes 24000000 | tf_op jit(solution)/shard_map/scatter_rows/pallas_call | solution.py:174
  569.0 1.2 copy.34
  570.2 1.2 copy.35
  (34 shorter events, 0.1 us)
Async XLA Ops:
  7.2 154.3 %all-gather.6.cloned.1.call-start = ((), (), s32[]{:S(2)}) async-start(), calls=%async_computation.3 | async-start | bytes 9437184 | tf_op jit(solution)/shard_map/all_gather | solution.py:956
  7.9 405.0 %reduce-scatter.2.cloned.1.call-start = ((), (), s32[]{:S(2)}) async-start(), calls=%async_computation.1 | async-start | bytes 9437184 | tf_op jit(solution)/shard_map/reduce_scatter | solution.py:960
  145.2 1.6 copy-start.2
  146.7 1.6 copy-start.3
  148.3 1.2 copy-start.4
  159.9 1.0 copy-start
  160.9 0.6 copy-start.5
  350.5 191.1 %all-gather.4.cloned.1.call-start = ((), (), s32[]{:S(2)}) async-start(), calls=%async_computation.2 | async-start | bytes 12386304 | tf_op jit(solution)/shard_map/all_gather | solution.py:956
  350.5 36.4 %slice-start.4 = ((s8[8388608]{0:T(1024)(128)(4,1)}), s8[4194304]{0:T(1024)(128)(4,1)S(1)}, s32[]{:S(2)}) async-start(s8[8388608]{0:T(1024)(128)(4,1)} %bitcast.65), calls=%async_computation.8 | async-start | bytes 8388608
  368.3 18.6 %slice-start.5 = ((s8[8388608]{0:T(1024)(128)(4,1)}), s8[4194304]{0:T(1024)(128)(4,1)S(1)}, s32[]{:S(2)}) async-start(s8[8388608]{0:T(1024)(128)(4,1)} %bitcast.65), calls=%async_computation.9 | async-start | bytes 8388608
  412.9 66.0 %copy-start.11 = (bf16[2,2048,128]{2,1,0:T(8,128)(2,1)S(1)}, bf16[2,2048,128]{2,1,0:T(8,128)(2,1)}, u32[]{:S(2)}) copy-start(bf16[2,2048,128]{2,1,0:T(8,128)(2,1)} %get-tuple-element.83.dk_ref) | copy-start | bytes 3145732
  476.2 5.3 copy-start.1
  478.9 10.2 %slice-start = ((s8[8388608]{0:T(1024)(128)(4,1)}), s8[4194304]{0:T(1024)(128)(4,1)S(1)}, s32[]{:S(2)}) async-start(s8[8388608]{0:T(1024)(128)(4,1)} %bitcast.45), calls=%async_computation.4 | async-start | bytes 8388608
  478.9 10.2 %slice-start.2 = ((s8[5767168]{0:T(1024)(128)(4,1)}), s8[4194304]{0:T(1024)(128)(4,1)S(1)}, s32[]{:S(2)}) async-start(s8[5767168]{0:T(1024)(128)(4,1)} %bitcast.63), calls=%async_computation.6 | async-start | bytes 8388608
  481.4 7.6 %slice-start.1 = ((s8[8388608]{0:T(1024)(128)(4,1)}), s8[4194304]{0:T(1024)(128)(4,1)S(1)}, s32[]{:S(2)}) async-start(s8[8388608]{0:T(1024)(128)(4,1)} %bitcast.45), calls=%async_computation.5 | async-start | bytes 8388608
  481.4 7.6 %slice-start.3 = ((s8[5767168]{0:T(1024)(128)(4,1)}), s8[1572864]{0:T(1024)(128)(4,1)S(1)}, s32[]{:S(2)}) async-start(s8[5767168]{0:T(1024)(128)(4,1)} %bitcast.63), calls=%async_computation.7 | async-start | bytes 3145728
  489.1 15.3 %copy-start.8 = (f32[1,2048]{1,0:T(1,128)S(1)}, f32[1,2048]{1,0:T(1,128)}, u32[]{:S(2)}) copy-start(f32[1,2048]{1,0:T(1,128)} %get-tuple-element.94) | copy-start | bytes 24580
  489.1 15.3 %copy-start.9 = (f32[1,2048]{1,0:T(1,128)S(1)}, f32[1,2048]{1,0:T(1,128)}, u32[]{:S(2)}) copy-start(f32[1,2048]{1,0:T(1,128)} %get-tuple-element.93) | copy-start | bytes 24580
  489.1 15.3 %copy-start.10 = (f32[1,512]{1,0:T(1,128)S(1)}, f32[1,512]{1,0:T(1,128)}, u32[]{:S(2)}) copy-start(f32[1,512]{1,0:T(1,128)} %get-tuple-element.92) | copy-start | bytes 6148
  489.1 25.0 %copy-start.6 = (bf16[256,2048]{1,0:T(8,128)(2,1)S(1)}, bf16[256,2048]{1,0:T(8,128)(2,1)}, u32[]{:S(2)}) copy-start(bf16[256,2048]{1,0:T(8,128)(2,1)} %get-tuple-element.67.h_ref) | copy-start | bytes 3145732
  489.1 25.0 %copy-start.7 = (bf16[256,2048]{1,0:T(8,128)(2,1)S(1)}, bf16[256,2048]{1,0:T(8,128)(2,1)}, u32[]{:S(2)}) copy-start(bf16[256,2048]{1,0:T(8,128)(2,1)} %reduce-scatter.2.cloned.1.call-done) | copy-start | bytes 3145732
Sparse Core Ops, SparseCore 0:
  9.8 63.3 all-gather.5
  350.6 62.2 reduce-scatter.1
  476.3 61.2 all-gather.3

commit v4 on v0

v4 whole, which is shorter than its diff:
```python
import functools

import jax
import jax.numpy as jnp
import numpy as np
from jax import lax
from jax.experimental import pallas as pl
from jax.experimental.pallas import tpu as pltpu
from jax.sharding import PartitionSpec as P

EPSILON = 1e-6
ROPE_BASE = 10000.0
LOG2E = 1.4426950408889634
BLK = 256
RING = 16
LANES = 128
ROWS = 64
VMEM_CAP = 60 * 1024 * 1024
BUSY = 40_000_000_000
NEG = -1e30
F32 = jnp.float32
BF16 = jnp.bfloat16


def matmul_f32(form, lhs, rhs):
    return jnp.einsum(form, lhs, rhs, preferred_element_type=jnp.float32)


def dot_nn(a, b):
    return jnp.dot(a, b, preferred_element_type=F32)


def dot_nt(a, b):
    return lax.dot_general(a, b, (((1,), (1,)), ((), ())), preferred_element_type=F32)


def tile(i):
    return slice(i * BLK, (i + 1) * BLK)


def rows_at(first, count):
    return pl.ds(pl.multiple_of(first, count), count)


def sems(*shape):
    return pltpu.SemaphoreType.DMA(shape)


def loop(count, step):
    def body(i, carry):
        step(i)
        return carry

    lax.fori_loop(0, count, body, 0)


VM = pl.BlockSpec(memory_space=pltpu.VMEM)
ANY = pl.BlockSpec(memory_space=pl.ANY)


def rope_tables(seq_len, rope_dim):
    inv_freq = np.float32(ROPE_BASE) ** (-np.arange(0, rope_dim, 2, dtype=np.float32) / np.float32(rope_dim))
    angles = (np.arange(seq_len, dtype=np.float32)[:, None] * inv_freq[None, :]).astype(np.float64)
    cos, sin = np.cos(angles), np.sin(angles)
    return (jnp.asarray(np.concatenate([cos, cos], axis=1), dtype=F32), jnp.asarray(np.concatenate([-sin, sin], axis=1), dtype=F32))


def swap_halves(x):
    half = x.shape[1] // 2
    return jnp.concatenate([x[:, half:], x[:, :half]], axis=1)


def rope(x, cos_t, sin_t):
    return x * cos_t + swap_halves(x) * sin_t


def unrope(x, cos_t, sin_t):
    return x * cos_t - swap_halves(x) * sin_t


def rms_inv(x):
    return lax.rsqrt(jnp.mean(x * x, axis=-1, keepdims=True) + EPSILON)


def rms_back(x, gain, dy):
    inv = rms_inv(x)
    gd = dy * gain
    mix = jnp.mean(gd * x, axis=-1, keepdims=True)
    return inv * gd - x * (inv * inv * inv * mix), jnp.sum(dy * (x * inv), axis=0, keepdims=True)


def gather_body(slot_ref, pos_ref, cnt_ref, tab_ref, out_ref, buf, acc, sem):
    seq, dim = acc.shape
    cnt = cnt_ref[0]

    def fetch(k):
        return pltpu.make_async_copy(tab_ref.at[rows_at(slot_ref[k] // 8 * 8, 8), :], buf.at[k % RING], sem.at[k % RING])

    loop(jnp.minimum(cnt, RING), lambda k: fetch(k).start())

    def clear(i):
        acc[rows_at(i * ROWS, ROWS), :] = jnp.zeros((ROWS, dim), F32)

    loop(seq // ROWS, clear)
    rows = lax.broadcasted_iota(jnp.int32, buf.shape[1:], 0)

    def step(k):
        fetch(k).wait()
        picked = jnp.where(rows == slot_ref[k] % 8, buf[k % RING].astype(F32), 0.0)
        acc[pl.ds(pos_ref[k], 1), :] = jnp.sum(picked, axis=0, keepdims=True)

        @pl.when(k + RING < cnt)
        def _():
            fetch(k + RING).start()

    loop(cnt, step)

    def emit(i):
        at = rows_at(i * ROWS, ROWS)
        out_ref[at, :] = acc[at, :].astype(BF16)

    loop(seq // ROWS, emit)


def local_call(body, name, out, in_specs, out_specs, scratch, scalars=0, grid=(1,), **extra):
    return pl.pallas_call(
        body, name=name, out_shape=out,
        grid_spec=pltpu.PrefetchScalarGridSpec(num_scalar_prefetch=scalars, grid=grid, in_specs=in_specs, out_specs=out_specs, scratch_shapes=scratch),
        compiler_params=pltpu.CompilerParams(vmem_limit_bytes=VMEM_CAP),
        cost_estimate=pl.CostEstimate(flops=BUSY // 2, bytes_accessed=BUSY // 2000, transcendentals=0), **extra)


def whole(*shape):
    return pl.BlockSpec(shape, lambda i, *_: (0,) * len(shape))


def gather_rows(slots, pos, cnt, table, seq):
    dim = table.shape[1]
    return local_call(gather_body, 'gather_rows', jax.ShapeDtypeStruct((seq, dim), BF16), [ANY], whole(seq, dim),
                      [pltpu.VMEM((RING, 8, dim), BF16), pltpu.VMEM((seq, dim), F32), sems(RING)], 3)(slots, pos, cnt, table)


def scatter_body(slot_ref, pos_ref, cnt_ref, de_ref, zero_ref, out_ref, wide, acc, stage, sem, near, nsem):
    seq, dim = wide.shape

    def load(i):
        at = rows_at(i * BLK, BLK)
        return pltpu.make_async_copy(de_ref.at[at, pl.ds(0, dim)], near.at[at, :], nsem.at[i])

    loop(seq // BLK, lambda i: load(i).start())

    def widen(i):
        load(i).wait()
        at = rows_at(i * BLK, BLK)
        wide[at, :] = near[at, :].astype(F32)

    loop(seq // BLK, widen)

    def put(blk, n):
        return pltpu.make_async_copy(stage.at[n % RING], out_ref.at[rows_at(blk * 8, 8), :], sem.at[n % RING])

    def step(k, carry):
        prev, n = carry
        slot = slot_ref[k]
        blk = slot // 8

        @pl.when(blk != prev)
        def _():
            acc[...] = jnp.zeros_like(acc)

        at = pl.ds(slot % 8, 1)
        acc[at, :] = acc[at, :] + wide[pl.ds(pos_ref[k], 1), :]
        last = slot_ref[k + 1] // 8 != blk

        @pl.when(last)
        def _():
            @pl.when(n >= RING)
            def _():
                put(blk, n).wait()

            stage[n % RING] = acc[...].astype(BF16)
            put(blk, n).start()

        return blk, n + last.astype(jnp.int32)

    _, total = lax.fori_loop(0, cnt_ref[0], step, (jnp.int32(-1), jnp.int32(0)))
    loop(jnp.minimum(total, RING), lambda i: put(0, total - 1 - i).wait())


def scatter_rows(slots, pos, cnt, de, zeros):
    seq, dim = de.shape[0], zeros.shape[1]
    return local_call(scatter_body, 'scatter_rows', jax.ShapeDtypeStruct(zeros.shape, BF16), [ANY, ANY], ANY,
                      [pltpu.VMEM((seq, dim), F32), pltpu.VMEM((8, dim), F32), pltpu.VMEM((RING, 8, dim), BF16), sems(RING), pltpu.VMEM((seq, dim), BF16), sems(seq // BLK)], 3, input_output_aliases={4: 0})(slots, pos, cnt, de, zeros)


def causal_tile():
    shape = (BLK, BLK)
    return lax.broadcasted_iota(jnp.int32, shape, 0) <= lax.broadcasted_iota(jnp.int32, shape, 1)


def fold(op, parts):
    total = functools.reduce(lambda a, b: a + b if op is jnp.sum else jnp.maximum(a, b), parts)
    return op(total, axis=0, keepdims=True)


def by_eight(op, x):
    return op(x.reshape(-1, 8, BLK), axis=0)


def attn_fwd_body(scale2, q_ref, k_ref, vt_ref, o_ref, lse_ref, s_scr):
    tri = causal_tile()
    for i in range(q_ref.shape[1] // BLK):
        q_i = q_ref[0, tile(i), :]
        tops = []
        for j in range(i + 1):
            s = dot_nt(k_ref[0, tile(j), :], q_i) * scale2
            if j == i:
                s = jnp.where(tri, s, NEG)
            s_scr[tile(j), :] = s
            tops.append(by_eight(jnp.max, s))
        top = fold(jnp.max, tops)
        dens = []
        for j in range(i + 1):
            e = jnp.exp2(s_scr[tile(j), :] - top)
            s_scr[tile(j), :] = e
            dens.append(by_eight(jnp.sum, e))
        den = fold(jnp.sum, dens)
        inv = 1.0 / den
        out = [dot_nn(vt_ref[0, :, tile(j)], (s_scr[tile(j), :] * inv).astype(BF16)) for j in range(i + 1)]
        o_ref[tile(i), :] = functools.reduce(jnp.add, out).T.astype(BF16)
        lse_ref[0, :, tile(i)] = top + jnp.log2(den)


def per_head(*shape):
    return pl.BlockSpec((1,) + shape, lambda h: (h, 0, 0))


def head_cols(seq, width):
    return pl.BlockSpec((seq, width), lambda h: (0, h))


def attn_fwd(q, k, vt, scale):
    heads, seq, qk = q.shape
    vdim = vt.shape[1]
    return local_call(functools.partial(attn_fwd_body, scale * LOG2E), 'attn_fwd',
                      [jax.ShapeDtypeStruct((seq, heads * vdim), BF16), jax.ShapeDtypeStruct((heads, 1, seq), F32)],
                      [per_head(seq, qk), per_head(seq, qk), per_head(vdim, seq)], [head_cols(seq, vdim), per_head(1, seq)],
                      [pltpu.VMEM((seq, BLK), F32)], grid=(heads,))(q, k, vt)


def attn_bwd_body(scale2, scale, q_ref, k_ref, kt_ref, v_ref, do_ref, o_ref, lse_ref, cos_ref, sin_ref, dq_ref, dk_ref, dkp_ref, dv_ref, zero_ref, p_scr, ds_scr, dlt, blank, zsem):
    seq = q_ref.shape[1]
    nope = dk_ref.shape[2]
    n = seq // BLK
    head = pl.program_id(0)
    size = blank.shape[0]
    fills = [pltpu.make_async_copy(blank, zero_ref.at[pl.ds(m * size, size), :], zsem.at[m]) for m in range(zsem.shape[0])]

    @pl.when(head == 0)
    def _():
        blank[...] = jnp.zeros_like(blank)
        for c in fills:
            c.start()

    tri = causal_tile()
    for i in range(n):
        both = do_ref[tile(i), :].astype(F32) * o_ref[tile(i), :].astype(F32)
        dlt[:, tile(i)] = jnp.sum(both.T, axis=0, keepdims=True)
    for j in range(n):
        k_j = k_ref[0, tile(j), :]
        v_j = v_ref[0, tile(j), :]
        for i in range(j, n):
            s = dot_nt(k_j, q_ref[0, tile(i), :])
            prob = jnp.exp2(s * scale2 - lse_ref[0, :, tile(i)])
            if i == j:
                prob = jnp.where(tri, prob, 0.0)
            dp = dot_nt(v_j, do_ref[tile(i), :])
            p_scr[:, tile(i)] = prob.astype(BF16)
            ds_scr[tile(j), tile(i)] = (prob * (dp - dlt[:, tile(i)])).astype(BF16)
        rest = slice(j * BLK, seq)
        dv_ref[0, tile(j), :] = dot_nn(p_scr[:, rest], do_ref[rest, :]).astype(BF16)
        dk = dot_nn(ds_scr[tile(j), rest], q_ref[0, rest, :]) * scale
        dk_ref[0, tile(j), :] = dk[:, :nope].astype(BF16)
        dkp_ref[0, tile(j), :] = dk[:, nope:]

    half = cos_ref.shape[0]
    for i in range(n):
        seen = slice(0, (i + 1) * BLK)
        dq = dot_nn(kt_ref[0, :, seen], ds_scr[seen, tile(i)]) * scale
        lo, hi = dq[nope:nope + half, :], dq[nope + half:, :]
        cos_b, sin_b = cos_ref[:, tile(i)], sin_ref[:, tile(i)]
        turned = jnp.concatenate([dq[:nope, :], lo * cos_b + hi * sin_b, hi * cos_b - lo * sin_b], axis=0)
        dq_ref[0, tile(i), :] = turned.T.astype(BF16)

    @pl.when(head == pl.num_programs(0) - 1)
    def _():
        for c in fills:
            c.wait()


def attn_bwd(q, k, kt, v, do, o, lse, cos_t, sin_t, scale, table):
    heads, seq, qk = q.shape
    vdim = v.shape[2]
    half = cos_t.shape[0]
    pe = half + half
    outs = [((seq, qk), BF16), ((seq, qk - pe), BF16), ((seq, pe), F32), ((seq, vdim), BF16)]
    return local_call(functools.partial(attn_bwd_body, scale * LOG2E, scale), 'attn_bwd', [jax.ShapeDtypeStruct((heads,) + s, d) for s, d in outs] + [jax.ShapeDtypeStruct(table, BF16)],
                      [per_head(seq, qk), per_head(seq, qk), per_head(qk, seq), per_head(seq, vdim), head_cols(seq, vdim), head_cols(seq, vdim), per_head(1, seq), whole(half, seq), whole(half, seq)],
                      [per_head(*s) for s, _ in outs] + [ANY],
                      [pltpu.VMEM((BLK, seq), BF16), pltpu.VMEM((seq, seq), BF16), pltpu.VMEM((1, seq), F32), pltpu.VMEM((table[0] // RING,) + table[1:], BF16), sems(RING)],
                      grid=(heads,))(q, k, kt, v, do, o, lse, cos_t, sin_t)


HALF = 128
SHARD = 256
STEPS = 8
MESH = pl.DeviceIdType.MESH


def xor_bits(t, u):
    out = 0
    for b in (1, 2, 4):
        tb = (t // b) % 2
        ub = (u // b) % 2
        out = out + b * (tb + ub - 2 * tb * ub)
    return out


def greet(t, others):
    peers = [xor_bits(t, u) for u in others]
    barrier = pltpu.get_barrier_semaphore()
    for peer in peers:
        pl.semaphore_signal(barrier, inc=1, device_id={'tp': peer}, device_id_type=MESH)
    pl.semaphore_wait(barrier, len(peers))
    return peers


def send_to(src, dst, send, recv, dev):
    return pltpu.make_async_remote_copy(src_ref=src, dst_ref=dst, send_sem=send, recv_sem=recv, device_id={'tp': dev}, device_id_type=MESH)


def piece_id(m, j):
    i = 2 * m + j // 2
    p, r = i // 4, i % 4
    first, last = (3 - p) // 3, p // 3
    mid = 1 - first - last
    u = first * (r // 2) + mid * (2 + (r % 2) * 2 + r // 2)
    h = r % 2 + (p - 1) * mid * (1 - 2 * (r % 2))
    near = 1 - last
    return u + last * (6 + j // 2), near * h + last * (j % 2), near * (j % 2) + last * (m % 2)


def piece(t, m, j):
    u, h, a = piece_id(m, j)
    return rows_at(xor_bits(t, u) * SHARD + h * HALF + a * ROWS, ROWS)


def pieces(t, m):
    return [piece(t, m, j) for j in range(4)]


def quarter(j):
    return pl.ds(j * ROWS, ROWS)


def join(ref, at, *lead):
    return jnp.concatenate([ref[lead + (r, slice(None))] for r in at], axis=0)


def begin(i, loads, ins, outs):
    @pl.when(i == 0)
    def _():
        for c in loads:
            c.wait()

    @pl.when(i < STEPS - 1)
    def _():
        for c in ins(i + 1):
            c.start()

    @pl.when(i >= 2)
    def _():
        for c in outs(i - 2):
            c.wait()

    for c in ins(i):
        c.wait()


def finish_all(outs):
    for i in (STEPS - 2, STEPS - 1):
        for c in outs(i):
            c.wait()


def ag_run(x_ref, full, send, recv, compute, before=None):
    t = lax.axis_index('tp')
    partner, xn, yn = greet(t, (1, 2, 4))
    sends = []

    def copy(src, shard, first, count, u_there, dev):
        place = rows_at(shard * SHARD + first, count)
        slot = first // ROWS
        c = send_to(src, full.at[place, :], send.at[len(sends)], recv.at[u_there, slot], dev)
        sends.append(c)
        return c

    def mine(h, u, dev):
        return copy(x_ref.at[pl.ds(h * HALF, HALF), :], t, h * HALF, HALF, u, dev)

    def relay(u, first, count, u_there, dev):
        shard = xor_bits(t, u)
        return copy(full.at[rows_at(shard * SHARD + first, count), :], shard, first, count, u_there, dev)

    for h, u, dev in ((0, 2, xn), (1, 4, yn), (0, 1, partner), (1, 1, partner), (1, 2, xn), (0, 4, yn)):
        mine(h, u, dev).start()
    full[rows_at(t * SHARD, SHARD), :] = x_ref[...]
    onward = {(u, h): [relay(u, h * HALF, HALF, u + 1, partner)] for u in (2, 4) for h in (0, 1)}
    for a in (0, 1):
        onward[2, 0].append(relay(2, a * ROWS, ROWS, 6, yn))
        onward[4, 1].append(relay(4, HALF + a * ROWS, ROWS, 6, xn))
    far = {(h, a): relay(6, h * HALF + a * ROWS, ROWS, 7, partner) for h in (0, 1) for a in (0, 1)}

    def arrive(u, first, count):
        place = full.at[rows_at(xor_bits(t, u) * SHARD + first, count), :]
        send_to(place, place, send.at[0], recv.at[u, first // ROWS], partner).wait_recv()

    def step(i):
        if before is not None:
            before(i)
        for m in range(1, 6):
            @pl.when(i == m)
            def _(m=m):
                for j in (0, 2):
                    u, h, _ = piece_id(m, j)
                    arrive(u, h * HALF, HALF)
                    for c in onward.get((u, h), ()):
                        c.start()

        for a in (0, 1):
            @pl.when(i == 6 + a)
            def _(a=a):
                for h in (0, 1):
                    arrive(6, h * HALF + a * ROWS, ROWS)
                    far[h, a].start()
                for h in (0, 1):
                    arrive(7, h * HALF + a * ROWS, ROWS)

        compute(i, pieces(t, i))

    loop(STEPS, step)
    for c in sends:
        c.wait_send()


AG_SEMS = [sems(18), sems(8, 4)]


def rs_run(stage, fp, fx, fy, send, recv, produce, finish, after=None, others=(1, 2, 4)):
    t = lax.axis_index('tp')
    partner, xn, yn, *_ = greet(t, others)
    sends = []

    def copy(src, dst, dev):
        n = len(sends)
        c = send_to(src, dst, send.at[n], recv.at[n], dev)
        sends.append(c)
        return c

    first, second = pl.ds(0, HALF), pl.ds(HALF, HALF)
    swap = [copy(stage.at[k, second, :], fp.at[0, pl.ds(k * HALF, HALF), :], partner) for k in (0, 1)]
    swap += [copy(stage.at[2 * p], fp.at[p], partner) for p in (1, 2, 3)]
    far_y = [copy(stage.at[k, quarter(0), :], fy.at[0, quarter(1 - k), :], yn) for k in (0, 1)]
    far_x = [copy(stage.at[k, quarter(1), :], fx.at[0, quarter(1 - k), :], xn) for k in (0, 1)]
    near_x, near_y = copy(stage.at[3, first, :], fx.at[1], xn), copy(stage.at[3, second, :], fy.at[1], yn)
    via_x, via_y = copy(stage.at[5, first, :], fx.at[2], xn), copy(stage.at[5, second, :], fy.at[2], yn)

    def add(i, start, count, src, src_start):
        def body(r):
            a = rows_at(start + r * 32, 32)
            stage[i, a, :] = (stage[i, a, :].astype(F32) + src[rows_at(src_start + r * 32, 32), :].astype(F32)).astype(BF16)

        loop(count // 32, body)

    def step(i):
        produce(i, pieces(t, STEPS - 1 - i))
        for k in (0, 1):
            @pl.when(i == k)
            def _(k=k):
                swap[k].start()
                swap[k].wait_recv()
                add(k, 0, HALF, fp.at[0], k * HALF)
                far_x[k].start()
                far_y[k].start()

        for p in (1, 2, 3):
            @pl.when(i == 2 * p)
            def _(p=p):
                swap[p + 1].start()

            @pl.when(i == 2 * p + 1)
            def _(p=p):
                swap[p + 1].wait_recv()
                add(2 * p + 1, 0, SHARD, fp.at[p], 0)

        @pl.when(i == 3)
        def _():
            near_x.start()
            near_y.start()

        @pl.when(i == 5)
        def _():
            for c in far_y:
                c.wait_recv()
            add(5, 0, HALF, fy.at[0], 0)
            via_x.start()
            for c in far_x:
                c.wait_recv()
            add(5, HALF, HALF, fx.at[0], 0)
            via_y.start()

        if after is not None:
            @pl.when(i >= 1)
            def _():
                after(i - 1)

    loop(STEPS, step)
    if after is not None:
        after(STEPS - 1)
    for c in (near_x, near_y, via_x, via_y):
        c.wait_recv()

    def last(r):
        lo, hi = rows_at(r * 32, 32), rows_at(HALF + r * 32, 32)
        finish(lo, (stage[7, lo, :].astype(F32) + fy[1, lo, :].astype(F32)) + fx[2, lo, :].astype(F32))
        finish(hi, (stage[7, hi, :].astype(F32) + fx[1, lo, :].astype(F32)) + fy[2, lo, :].astype(F32))

    loop(HALF // 32, last)
    for c in sends:
        c.wait_send()


def rs_scratch(dim):
    return [pltpu.VMEM((n, rows, dim), BF16) for n, rows in ((STEPS, SHARD), (4, SHARD), (3, HALF), (3, HALF))] + [sems(13), sems(13)]


def comm_call(body, name, cid, in_specs, out_specs, out_shape, scratch):
    return pl.pallas_call(
        body, name=name, in_specs=in_specs, out_specs=out_specs, out_shape=out_shape, scratch_shapes=scratch,
        compiler_params=pltpu.CompilerParams(collective_id=cid, has_side_effects=True, vmem_limit_bytes=VMEM_CAP),
        cost_estimate=pl.CostEstimate(flops=BUSY, bytes_accessed=BUSY // 2000, transcendentals=0))


def col_tiles(width):
    return [slice(a, min(a + BLK, width)) for a in range(0, width, BLK)]


def struct(dtype, *shape):
    return jax.ShapeDtypeStruct(shape, dtype)


def back_rms_rows(x_ref, g_ref, dgain_ref, at, dy):
    d_x, d_g = rms_back(x_ref[at, :].astype(F32), g_ref[...], dy.astype(BF16).astype(F32))
    dgain_ref[...] = dgain_ref[...] + d_g
    return d_x


def rs_rows(rows, gain):
    dim = rows.shape[1]

    def body(rows_ref, g_ref, e_ref, u_ref, stage, fp, fx, fy, send, recv, load):
        t = lax.axis_index('tp')

        def fetch(i):
            return [pltpu.make_async_copy(rows_ref.at[at, :], stage.at[i, quarter(j), :], load.at[i, j]) for j, at in enumerate(pieces(t, STEPS - 1 - i))]

        for i in range(STEPS):
            for c in fetch(i):
                c.start()

        def produce(i, at):
            for c in fetch(i):
                c.wait()

        def finish(at, val):
            e_b = val.astype(BF16)
            e_ref[at, :] = e_b
            x = e_b.astype(F32)
            u_ref[at, :] = (x * rms_inv(x) * g_ref[...]).astype(BF16)

        rs_run(stage, fp, fx, fy, send, recv, produce, finish)

    loc = struct(BF16, SHARD, dim)
    return comm_call(body, 'rs_rows', 0, [ANY, VM], [VM, VM], [loc, loc], rs_scratch(dim) + [sems(STEPS, 4)])(rows, gain)


def ag_proj(x, w_q, w_dkv, g_kv, w_uk, w_uv, cos_t, sin_t):
    seq = cos_t.shape[0]
    heads, qk, dim = w_q.shape
    lat = w_dkv.shape[0]
    rank, nope = w_uk.shape[1:]
    vdim = w_uv.shape[2]

    def body(x_ref, wq_ref, wl_hbm, g_ref, wk_ref, wv_ref, cos_ref, sin_ref, x_out, q_ref, l_ref, c_ref, k_ref, kt_ref, v_ref, vt_ref, full, send, recv, sem, wl, wsem):
        t = lax.axis_index('tp')
        w_load = pltpu.make_async_copy(wl_hbm, wl, wsem)
        w_load.start()

        def x_copies(i):
            return [pltpu.make_async_copy(full.at[at, :], x_out.at[at, :], sem.at[i, j]) for j, at in enumerate(pieces(t, i))]

        def turn(m, j):
            u, h, _ = piece_id(m, j)
            at = rows_at(xor_bits(t, u) * SHARD + h * HALF, HALF)
            for hd in range(heads):
                kt_ref[hd, :, at] = k_ref[hd, at, :].astype(F32).T.astype(BF16)
                vt_ref[hd, :, at] = v_ref[hd, at, :].astype(F32).T.astype(BF16)

        def compute(i, rows):
            @pl.when(i == 0)
            def _():
                w_load.wait()

            for c in x_copies(i):
                c.start()
            x_b = join(full, rows)
            l_b = dot_nt(x_b, wl[...])
            kv = l_b[:, :rank]
            c_b = (kv * rms_inv(kv) * g_ref[...]).astype(BF16)
            cos_b, sin_b = join(cos_ref, rows), join(sin_ref, rows)
            pe_b = rope(l_b[:, rank:], cos_b, sin_b).astype(BF16)

            def put(ref, val, *lead, cols=slice(None)):
                for j, at in enumerate(rows):
                    ref[lead + (at, cols)] = val[j * ROWS:(j + 1) * ROWS, :]

            put(l_ref, l_b)
            put(c_ref, c_b)
            for hd in range(heads):
                q_b = dot_nt(x_b, wq_ref[hd]).astype(BF16)
                put(q_ref, q_b[:, :nope], hd, cols=slice(0, nope))
                put(q_ref, rope(q_b[:, nope:].astype(F32), cos_b, sin_b).astype(BF16), hd, cols=slice(nope, qk))
                put(k_ref, dot_nn(c_b, wk_ref[hd]).astype(BF16), hd, cols=slice(0, nope))
                put(k_ref, pe_b, hd, cols=slice(nope, qk))
                put(v_ref, dot_nn(c_b, wv_ref[hd]).astype(BF16), hd)

            @pl.when(i < 6)
            def _():
                turn(i, 0)
                turn(i, 2)

            @pl.when(i == STEPS - 1)
            def _():
                for j in range(4):
                    turn(STEPS - 1, j)

        ag_run(x_ref, full, send, recv, compute)
        for i in range(STEPS):
            for c in x_copies(i):
                c.wait()

    per = [struct(BF16, heads, seq, qk), struct(F32, seq, lat), struct(BF16, seq, rank), struct(BF16, heads, seq, qk), struct(BF16, heads, qk, seq), struct(BF16, heads, seq, vdim), struct(BF16, heads, vdim, seq)]
    return comm_call(body, 'ag_proj', 1, [VM, VM, ANY] + [VM] * 5, [ANY] + [VM] * len(per), [struct(BF16, seq, dim)] + per,
                     [pltpu.VMEM((seq, dim), BF16)] + AG_SEMS + [sems(STEPS, 4), pltpu.VMEM((lat, dim), BF16), pltpu.SemaphoreType.DMA])(x, w_q, w_dkv, g_kv, w_uk, w_uv, cos_t, sin_t)


def shard_rows(i):
    return rows_at(i * SHARD, SHARD)


def stream_copies(ref, buf, sem, out=False):
    def copies(i):
        a, b = ref.at[shard_rows(i), :], buf.at[i % 2]
        return [pltpu.make_async_copy(b, a, sem.at[i % 2]) if out else pltpu.make_async_copy(a, b, sem.at[i % 2])]

    return copies


def attn_out_rs(o, w_o, e_loc, gain, dy, w_down):
    seq, dim = dy.shape
    ffn = w_down.shape[0]

    def body(o_ref, w_ref, e_ref, g_ref, dy_ref, wd_hbm, h_ref, z_ref, dh_ref, stage, fp, fx, fy, send, recv, wd, dyb, st, wsem, dsem, osem):
        ins, outs = stream_copies(dy_ref, dyb, dsem), stream_copies(dh_ref, st, osem, True)
        w_load = pltpu.make_async_copy(wd_hbm, wd, wsem)
        for c in ins(0) + [w_load]:
            c.start()

        def produce(i, at):
            o_b = join(o_ref, at)
            for cols in col_tiles(dim):
                stage[i, :, cols] = dot_nn(o_b, w_ref[:, cols]).astype(BF16)

        def after(i):
            begin(i, [w_load], ins, outs)
            dy_b = dyb[i % 2]
            for cols in col_tiles(ffn):
                st[i % 2, :, cols] = dot_nt(dy_b, wd[cols, :])
            for c in outs(i):
                c.start()

        def finish(at, val):
            h_b = (e_ref[at, :].astype(F32) + val.astype(BF16).astype(F32)).astype(BF16)
            h_ref[at, :] = h_b
            x = h_b.astype(F32)
            z_ref[at, :] = (x * rms_inv(x) * g_ref[...]).astype(BF16)

        rs_run(stage, fp, fx, fy, send, recv, produce, finish, after)
        finish_all(outs)

    loc = struct(BF16, SHARD, dim)
    return comm_call(body, 'attn_out_rs', 2, [VM] * 4 + [ANY] * 2, [VM, VM, ANY], [loc, loc, struct(F32, seq, ffn)],
                     rs_scratch(dim) + [pltpu.VMEM((ffn, dim), BF16), pltpu.VMEM((2, SHARD, dim), BF16), pltpu.VMEM((2, SHARD, ffn), F32),
                                        pltpu.SemaphoreType.DMA, sems(2), sems(2)])(o, w_o, e_loc, gain, dy, w_down)


def ag_mlp(z, dh, w_gate, w_up):
    seq, ffn = dh.shape
    dim = z.shape[1]

    def body(z_ref, dh_ref, wg_hbm, wu_hbm, z_out, hid_out, dg_out, du_out, full, wg, wu, dhb, st, send, recv, zsem, wsem, dsem, osem):
        t = lax.axis_index('tp')
        loads = [pltpu.make_async_copy(a, b, wsem.at[n]) for n, (a, b) in enumerate(((wg_hbm, wg), (wu_hbm, wu)))]

        def ins(i):
            return [pltpu.make_async_copy(dh_ref.at[at, :], dhb.at[i % 2, quarter(j), :], dsem.at[i % 2, j]) for j, at in enumerate(pieces(t, i))]

        def z_copies(i):
            return [pltpu.make_async_copy(full.at[at, :], z_out.at[at, :], zsem.at[i, j]) for j, at in enumerate(pieces(t, i))]

        def outs(i):
            return [pltpu.make_async_copy(st.at[n, i % 2, quarter(j), :], o.at[at, :], osem.at[n, i % 2, j])
                    for n, o in enumerate((hid_out, dg_out, du_out)) for j, at in enumerate(pieces(t, i))]

        for c in loads + ins(0):
            c.start()

        def compute(i, rows):
            begin(i, loads, ins, outs)
            for c in z_copies(i):
                c.start()
            z_b = join(full, rows)
            for cols in col_tiles(ffn):
                gate = dot_nt(z_b, wg[cols, :])
                up = dot_nt(z_b, wu[cols, :])
                d_hid = dhb[i % 2, :, cols]
                sig = jax.nn.sigmoid(gate)
                act = gate * sig
                for n, val in enumerate((act * up, d_hid * up * sig * (1.0 + gate * (1.0 - sig)), d_hid * act)):
                    st[n, i % 2, :, cols] = val.astype(BF16)
            for c in outs(i):
                c.start()

        ag_run(z_ref, full, send, recv, compute)
        finish_all(outs)
        for i in range(STEPS):
            for c in z_copies(i):
                c.wait()

    act = struct(BF16, seq, ffn)
    weight = pltpu.VMEM((ffn, dim), BF16)
    return comm_call(body, 'ag_mlp', 3, [VM, ANY, ANY, ANY], [ANY] * 4, [struct(BF16, seq, dim), act, act, act],
                     [pltpu.VMEM((seq, dim), BF16), weight, weight, pltpu.VMEM((2, SHARD, ffn), F32), pltpu.VMEM((3, 2, SHARD, ffn), BF16)] + AG_SEMS
                     + [sems(STEPS, 4), sems(2), sems(2, 4), sems(3, 2, 4)])(z, dh, w_gate, w_up)


def mlp_back_rs(d_gate, d_up, w_gate, w_up, h_loc, gain, dy):
    ffn, dim = w_gate.shape

    def body(dg_ref, du_ref, wg_hbm, wu_hbm, h_ref, g_ref, dy_ref, res_ref, resb_ref, dgain_ref, stage, fp, fx, fy, send, recv, wg, wu, blk, wsem, bsem):
        t = lax.axis_index('tp')
        loads = [pltpu.make_async_copy(a, b, wsem.at[n]) for n, (a, b) in enumerate(((wg_hbm, wg), (wu_hbm, wu)))]

        def ins(i):
            return [pltpu.make_async_copy(r.at[at, :], blk.at[n, i % 2, quarter(j), :], bsem.at[n, i % 2, j])
                    for n, r in enumerate((dg_ref, du_ref)) for j, at in enumerate(pieces(t, STEPS - 1 - i))]

        for c in ins(0) + loads:
            c.start()

        def produce(i, at):
            begin(i, loads, ins, lambda i: [])
            dg_b = blk[0, i % 2]
            du_b = blk[1, i % 2]
            for cols in col_tiles(dim):
                stage[i, :, cols] = (dot_nn(dg_b, wg[:, cols]) + dot_nn(du_b, wu[:, cols])).astype(BF16)

        dgain_ref[...] = jnp.zeros_like(dgain_ref)

        def finish(at, val):
            res = dy_ref[at, :].astype(F32) + back_rms_rows(h_ref, g_ref, dgain_ref, at, val)
            res_ref[at, :] = res
            resb_ref[at, :] = res.astype(BF16)

        rs_run(stage, fp, fx, fy, send, recv, produce, finish)

    weight = pltpu.VMEM((ffn, dim), BF16)
    return comm_call(body, 'mlp_back_rs', 4, [ANY] * 4 + [VM] * 3, [VM] * 3, [struct(F32, SHARD, dim), struct(BF16, SHARD, dim), struct(F32, *gain.shape)],
                     rs_scratch(dim) + [weight, weight, pltpu.VMEM((2, 2, SHARD, ffn), BF16), sems(2), sems(2, 2, 4)])(d_gate, d_up, w_gate, w_up, h_loc, gain, dy)


def ag_dattn(x, w_o, hidden, w_down):
    seq, ffn = hidden.shape
    width, dim = w_o.shape

    def body(x_ref, w_ref, hid_ref, wd_hbm, x_out, do_ref, y_out, full, send, recv, sem, wd, hb, yb, wsem, hsem, ysem):
        t = lax.axis_index('tp')
        ins, outs = stream_copies(hid_ref, hb, hsem), stream_copies(y_out, yb, ysem, True)
        w_load = pltpu.make_async_copy(wd_hbm, wd, wsem)
        for c in ins(0) + [w_load]:
            c.start()

        def x_copies(i):
            return [pltpu.make_async_copy(full.at[at, :], x_out.at[at, :], sem.at[i, j]) for j, at in enumerate(pieces(t, i))]

        def before(i):
            begin(i, [w_load], ins, outs)
            h_b = hb[i % 2]
            for cols in col_tiles(dim):
                yb[i % 2, :, cols] = dot_nn(h_b, wd[:, cols]).astype(BF16)
            for c in outs(i):
                c.start()

        def compute(i, rows):
            for c in x_copies(i):
                c.start()
            d_o = dot_nt(join(full, rows), w_ref[...]).astype(BF16)
            for j, at in enumerate(rows):
                do_ref[at, :] = d_o[j * ROWS:(j + 1) * ROWS, :]

        ag_run(x_ref, full, send, recv, compute, before)
        finish_all(outs)
        for i in range(STEPS):
            for c in x_copies(i):
                c.wait()

    big = struct(BF16, seq, dim)
    return comm_call(body, 'ag_dattn', 5, [VM, VM, ANY, ANY], [ANY, VM, ANY], [big, struct(BF16, seq, width), big],
                     [pltpu.VMEM((seq, dim), BF16)] + AG_SEMS + [sems(STEPS, 4), pltpu.VMEM((ffn, dim), BF16), pltpu.VMEM((2, SHARD, ffn), BF16),
                      pltpu.VMEM((2, SHARD, dim), BF16), pltpu.SemaphoreType.DMA, sems(2), sems(2)])(x, w_o, hidden, w_down)


def attn_back_rs(d_query, d_knope, d_kpe, d_value, latent, g_kv, w_uk, w_uv, w_q, w_dkv, cos_t, sin_t, e_loc, g_attn, d_res, dg_mlp):
    heads, _, dim = w_q.shape
    lat = latent.shape[1]
    rank = w_uk.shape[1]
    wide = -(-(dim + lat) // LANES) * LANES
    others = (1, 2, 4, 3, 5, 6, 7)
    total = (1, g_kv.shape[1] + g_attn.shape[1] + dg_mlp.shape[1])

    def body(dq_ref, dk_ref, dkp_ref, dv_ref, l_ref, gkv_ref, wk_ref, wv_ref, wq_ref, wl_ref, cos_ref, sin_ref, e_ref, g_ref, res_ref, dgm_ref,
             de_ref, sum_ref, stage, fp, fx, fy, send, recv, parts, dgkv_ref, dgain_ref, gsend, grecv):
        t = lax.axis_index('tp')
        dgkv_ref[...] = jnp.zeros_like(dgkv_ref)
        dgain_ref[...] = jnp.zeros_like(dgain_ref)

        def produce(i, at):
            d_c = functools.reduce(jnp.add, [dot_nt(join(r, at, hd), w[hd]) for hd in range(heads) for r, w in ((dk_ref, wk_ref), (dv_ref, wv_ref))])
            d_kv, d_g = rms_back(join(l_ref, at)[:, :rank], gkv_ref[...], d_c.astype(BF16).astype(F32))
            dgkv_ref[...] = dgkv_ref[...] + d_g
            d_pe = functools.reduce(jnp.add, [join(dkp_ref, at, hd) for hd in range(heads)])
            d_pe = unrope(d_pe.astype(BF16).astype(F32), join(cos_ref, at), join(sin_ref, at))
            stage[i, :, dim:dim + rank] = d_kv.astype(BF16)
            stage[i, :, dim + rank:dim + lat] = d_pe.astype(BF16)
            stage[i, :, dim + lat:] = jnp.zeros((SHARD, wide - dim - lat), BF16)
            dl_b = stage[i, :, dim:dim + lat]
            dq_b = [join(dq_ref, at, hd) for hd in range(heads)]
            for cols in col_tiles(dim):
                val = dot_nn(dl_b, wl_ref[:, cols])
                for hd in range(heads):
                    val = val + dot_nn(dq_b[hd], wq_ref[hd, :, cols])
                stage[i, :, cols] = val.astype(BF16)

        def finish(at, val):
            d_x = back_rms_rows(e_ref, g_ref, dgain_ref, at, val[:, :dim])
            de_ref[at, :dim] = (res_ref[at, :] + d_x).astype(BF16)
            de_ref[at, dim:] = val[:, dim:].astype(BF16)

        rs_run(stage, fp, fx, fy, send, recv, produce, finish, others=others)
        first = 0
        for ref in (dgkv_ref, dgain_ref, dgm_ref):
            parts[t, :, first:first + ref.shape[1]] = ref[...]
            first += ref.shape[1]
        copies = [send_to(parts.at[t], parts.at[t], gsend.at[n], grecv.at[n], xor_bits(t, u)) for n, u in enumerate(others)]
        for c in copies:
            c.start()
        for c in copies:
            c.wait()
        sum_ref[...] = functools.reduce(jnp.add, [parts[d] for d in range(STEPS)])

    count = len(others)
    return comm_call(body, 'attn_back_rs', 6, [VM] * 16, [VM] * 2, [struct(BF16, SHARD, wide), struct(F32, *total)],
                     rs_scratch(wide) + [pltpu.VMEM((STEPS,) + total, F32), pltpu.VMEM(g_kv.shape, F32), pltpu.VMEM(g_attn.shape, F32), sems(count), sems(count)])(
                         d_query, d_knope, d_kpe, d_value, latent, g_kv, w_uk, w_uv, w_q, w_dkv, cos_t, sin_t, e_loc, g_attn, d_res, dg_mlp)


def gather_seq(x):
    return lax.all_gather(x, 'tp', axis=0, tiled=True)


def scatter_seq(x):
    return lax.psum_scatter(x, 'tp', scatter_dimension=0, tiled=True)


def solution(mesh):
    def device_step(tokens, embed_table, w_q, w_dkv, g_kv, w_uk, w_uv, w_o, g_attn, g_mlp, w_gate, w_up, w_down, d_out):
        vocab_local, model_dim = embed_table.shape
        seq = tokens.shape[1]
        heads, qk = w_q.shape[1:]
        vdim = w_uv.shape[2]
        scale = qk ** -0.5
        dy_loc = d_out[0]
        gkv, gat, gml = g_kv.reshape(1, -1), g_attn.reshape(1, -1), g_mlp.reshape(1, -1)
        wuk, wuv, wq = (jnp.moveaxis(w, 1, 0) for w in (w_uk, w_uv, w_q))
        wq, wl, wg, wu = jnp.swapaxes(wq, 1, 2), w_dkv.T, w_gate.T, w_up.T
        wo = w_o.reshape(heads * vdim, model_dim)
        cos_t, sin_t = rope_tables(seq, qk - w_uk.shape[2])

        dy_full = gather_seq(dy_loc)
        local_ids = tokens[0] - lax.axis_index('tp') * vocab_local
        owned = (local_ids >= 0) & (local_ids < vocab_local)
        slots, pos = lax.sort((jnp.where(owned, local_ids, vocab_local), lax.iota(jnp.int32, seq)), num_keys=1)
        slots = jnp.concatenate([slots, jnp.full((128,), vocab_local, jnp.int32)])
        cnt = jnp.sum(owned.astype(jnp.int32)).reshape(1)
        rows = gather_rows(slots, pos, cnt, embed_table, seq)
        e_loc, u_loc = rs_rows(rows, gat)
        u, q, latent, c_kv, k, kt, v, vt = ag_proj(u_loc, wq, wl, gkv, wuk, wuv, cos_t, sin_t)
        o, lse = attn_fwd(q, k, vt, scale)
        h_loc, z_loc, d_hidden = attn_out_rs(o, wo, e_loc, gml, dy_full, w_down)
        z, hidden, d_gate, d_up = ag_mlp(z_loc, d_hidden, wg, wu)
        d_res, d_res_b, dg_mlp = mlp_back_rs(d_gate, d_up, wg, wu, h_loc, gml, dy_loc)
        d_res_full, d_o, mlp_part = ag_dattn(d_res_b, wo, hidden, w_down)

        mlp_loc = scatter_seq(mlp_part)
        half = cos_t.shape[1] // 2
        d_query, d_knope, d_kpe, d_value, zeros = attn_bwd(q, k, kt, v, d_o, o, lse, cos_t[:, :half].T, sin_t[:, half:].T, scale, embed_table.shape)
        dw_up = matmul_f32('sf,sd->fd', d_up, z)
        dw_up, d_query = lax.optimization_barrier((dw_up, d_query))
        layer_out = (h_loc.astype(F32) + mlp_loc.astype(F32)).astype(BF16)
        back, gains = attn_back_rs(d_query, d_knope, d_kpe, d_value, latent, gkv, wuk, wuv, wq, wl, cos_t, sin_t, e_loc, gat, d_res, dg_mlp)

        back_full = gather_seq(back)
        dw_gate = matmul_f32('sf,sd->fd', d_gate, z)
        dw_down = matmul_f32('sf,sd->fd', hidden, dy_full)
        dw_q = matmul_f32('sd,hse->dhe', u, d_query)
        dw_uk = matmul_f32('sc,hse->che', c_kv, d_knope)
        dw_uv = matmul_f32('sc,hsv->chv', c_kv, d_value)
        dw_o = matmul_f32('sv,sd->vd', o, d_res_full).reshape(w_o.shape)
        back_full, dw_gate, dw_down, dw_q, dw_uk, dw_uv, dw_o = lax.optimization_barrier((back_full, dw_gate, dw_down, dw_q, dw_uk, dw_uv, dw_o))
        dw_gate, dw_up = dw_gate.T, dw_up.T
        dw_dkv = matmul_f32('sc,sd->cd', back_full[:, model_dim:model_dim + w_dkv.shape[1]], u).T
        d_table = scatter_rows(slots, pos, cnt, back_full, zeros)
        gains = gains[0]
        rank = g_kv.shape[0]
        dg_kv, dg_attn, dg_mlp = gains[:rank], gains[rank:rank + model_dim], gains[rank + model_dim:]
        return layer_out[None], d_table, dw_q, dw_dkv, dg_kv, dw_uk, dw_uv, dw_o, dg_attn, dg_mlp, dw_gate, dw_up, dw_down

    row_spec = P('dp', 'tp', None)
    head_spec = P(None, 'tp', None)
    in_specs = (P('dp', None), P('tp', None), head_spec, P(None, None), P(None), head_spec, head_spec, P('tp', None, None), P(None), P(None), P(None, 'tp'), P(None, 'tp'), P('tp', None), row_spec)
    out_specs = (row_spec, P(('dp', 'tp'), None), P('dp', 'tp', None), P('dp', None), P('dp'), P('dp', 'tp', None), P('dp', 'tp', None), P(('dp', 'tp'), None, None), P('dp'), P('dp'), P('dp', 'tp'), P('dp', 'tp'), P(('dp', 'tp'), None))
    return jax.shard_map(device_step, mesh=mesh, in_specs=in_specs, out_specs=out_specs, check_vma=False)
```

time: 1280 us -> 562 us (0.44)
  waiting for transfers between devices: 451 us -> 2.87 us
  Pallas kernels: 0 us -> 436 us
  matrix products: 420 us -> 79 us
  other arithmetic: 237 us -> 8.99 us
  local copies, waits for them, and re-layouts: 128 us -> 9.22 us
  blocking collectives: 22.8 us -> 0 us
    pallas_call x0 -> x11, Pallas kernels: none -> 436 us  [the longest x1 71.3 us: attn_back_rs(): comm_call(body, 'attn_back_rs', 6, [VM] * 16, [VM] * 2, [struct(BF16, SHA...]
    dot_general x31 -> x7, matrix products: 408 us -> 73.8 us  [matmul_f32(): return jnp.einsum(form, lhs, rhs, preferred_element_type=jnp.float32)]
    reduce_scatter x5 -> x1, waiting for transfers between devices: 296 us -> 0.01 us  [scatter_seq(): return lax.psum_scatter(x, 'tp', scatter_dimension=0, tiled=True)]
    all_gather x5 -> x2, waiting for transfers between devices: 154 us -> 2.15 us  [gather_seq(): return lax.all_gather(x, 'tp', axis=0, tiled=True)]
    scatter-add x3 -> x0, other arithmetic: 111 us -> none  [device_step(): jax.ops.segment_sum(de_full.reshape(-1, model_dim).astype(jnp.float32), s...]
    gather x1 -> x0, local copies, waits for them, and re-layouts: 103 us -> none  [device_step(): rows = jnp.take(embed_table, jnp.where(owned, local_ids, 0), axis=0)]
    convert_element_type x10 -> x0, other arithmetic: 84.1 us -> none  [the longest x1 50.9 us: device_step(): return (layer_out, d_table.astype(jnp.bfloat16)) + weight_grads]
    psum x1 -> x0, blocking collectives: 22.8 us -> none  [layer_pass(): lax.psum((dw_dkv_part, dg_kv_part, dg_attn_part, dg_mlp_part), 'tp')]
  transfers between devices with their start and end apart: 11 -> 3, of which waited for: 9 -> 1; matrix products, arithmetic and copies ran while one was open for 25% -> 15% of each run, Pallas kernels for 0% -> 42%
where the time goes in v4:
time: 562 us; the launch traced here: 551 us
  Pallas kernels  436 us (78%)
  matrix products  79 us (14%)
  between operations  14.4 us (3%)
  local copies, waits for them, and re-layouts  9.22 us (2%)
  other arithmetic  8.99 us (2%)
    dot_general x7, matrix products, matmul_f32(): return jnp.einsum(form, lhs, rhs, preferred_element_type=jnp.float32)  73.8 us
    pallas_call x1, Pallas kernels, attn_back_rs(): comm_call(body, 'attn_back_rs', 6, [VM] * 16, [VM] * 2, [struct(BF16, SHA...  71.3 us
    pallas_call x1, Pallas kernels, rs_rows(): comm_call(body, 'rs_rows', 0, [ANY, VM], [VM, VM], [loc, loc], rs_scratch...  57.5 us
    pallas_call x1, Pallas kernels, mlp_back_rs(): comm_call(body, 'mlp_back_rs', 4, [ANY] * 4 + [VM] * 3, [VM] * 3, [struct...  51.6 us
    pallas_call x1, Pallas kernels, ag_proj(): comm_call(body, 'ag_proj', 1, [VM, VM, ANY] + [VM] * 5, [ANY] + [VM] * le...  48.9 us
    pallas_call x1, Pallas kernels, ag_mlp(): comm_call(body, 'ag_mlp', 3, [VM, ANY, ANY, ANY], [ANY] * 4, [struct(BF16...  48.3 us
    pallas_call x1, Pallas kernels, attn_out_rs(): comm_call(body, 'attn_out_rs', 2, [VM] * 4 + [ANY] * 2, [VM, VM, ANY], [l...  44.5 us
    pallas_call x1, Pallas kernels, ag_dattn(): comm_call(body, 'ag_dattn', 5, [VM, VM, ANY, ANY], [ANY, VM, ANY], [big,...  42.2 us
  transfers between devices with their start and end apart: 3, of which 1 were waited for; matrix products, arithmetic and copies ran while one was open for 15% of the time, Pallas kernels for 42%

profile of v4, /device:TPU:0, one launch (start us, length us, event | category | flops | bytes accessed | tf_op | source)
XLA Modules:
  0.0 551.0 jit_solution(17828360042508917389)
XLA Ops:
  7.2 0.0 all-gather.6.cloned.1.call-start
  7.2 0.7 all-gather.6.cloned.1.call-update
  7.9 0.0 reduce-scatter.2.cloned.1.call-start
  8.0 0.7 broadcast_subtract_fusion
  8.7 0.7 convert_reduce_fusion
  9.3 5.0 sort.15
  14.4 0.6 concatenate.3.slot_ref
  15.0 1.9 copy_bitcast_fusion
  16.9 21.1 %gather_rows.1.rows_ref = bf16[2048,2048]{1,0:T(8,128)(2,1)} custom-call(s32[2176]{0:T(1024)} %concatenate.3.slot_ref, s32[2048]{0:T(1024)} %get-tuple-element.57.pos_ref, s32[1]{0:T(128)} %bitcast.1.cnt_ref, bf16[12800,2048]{1,0:T(8,128)(2,1)} %tab_ref.1), custom_call_target="tpu_custom_call" | custom-call | flops 20000000000 | bytes 20000000 | tf_op jit(solution)/shard_map/gather_rows/pallas_call | solution.py:139
  37.9 57.5 %rs_rows.1 = (bf16[256,2048]{1,0:T(8,128)(2,1)}, bf16[256,2048]{1,0:T(8,128)(2,1)}) custom-call(bf16[2048,2048]{1,0:T(8,128)(2,1)} %gather_rows.1.rows_ref, f32[1,2048]{1,0:T(1,128)} %bitcast.70), custom_call_target="tpu_custom_call" | custom-call | flops 40000000000 | bytes 20000000 | tf_op jit(solution)/shard_map/rs_rows/pallas_call | solution.py:594
  95.5 48.9 %ag_proj.1 = (bf16[2048,2048]{1,0:T(8,128)(2,1)}, bf16[2,2048,192]{2,1,0:T(8,128)(2,1)}, f32[2048,576]{1,0:T(8,128)}, bf16[2048,512]{1,0:T(8,128)(2,1)}, bf16[2,...) custom-call(bf16[256,2048]{1,0:T(8,128)(2,1)} %get-tuple-element.58., ...), custom_call_target="tpu_custom_call" | custom-call | flops 40000000000 | bytes 20000000 | tf_op jit(solution)/shard_map/ag_proj/pallas_call | solution.py:663
  144.3 12.7 %attn_fwd.1 = (bf16[2048,256]{1,0:T(8,128)(2,1)}, f32[2,1,2048]{2,1,0:T(1,128)}) custom-call(bf16[2,2048,192]{2,1,0:T(8,128)(2,1)} %get-tuple-element.59.q_ref, bf16[2,2048,192]{2,1,0:T(8,128)(2,1)} %get-tuple-element.60.k_ref, bf16[2,128,2048]{2,1,0:T(8,128)(2,1)} %get-tuple-element.61.vt_ref), custom_call_target="tpu_custom_call" | custom-call | flops 20000000000 | bytes 20000000 | tf_op jit(solution)/shard_map/attn_fwd/pallas_call | solution.py:245
  157.1 44.5 %attn_out_rs.1 = (bf16[256,2048]{1,0:T(8,128)(2,1)}, bf16[256,2048]{1,0:T(8,128)(2,1)}, f32[2048,1368]{1,0:T(8,128)}) custom-call(bf16[2048,256]{1,0:T(8,128)(2,1)} %get-tuple-element.62.o_ref, bf16[256,2048]{1,0:T(8,128)(2,1)} %bitcast.66, bf16[256,2048]{1,0:T(8,128)(2,1)} %get-tuple-element.63.e_ref, f32[1,2048]{1,0:T(1,128)} %bitcast.68, ...), custom_call_target="tpu_custom_call" | custom-call | flops 40000000000 | bytes 20000000 | tf_op jit(solution)/shard_map/attn_out_rs/pallas_call | solution.py:712
  201.5 48.3 %ag_mlp.1 = (bf16[2048,2048]{1,0:T(8,128)(2,1)}, bf16[2048,1368]{1,0:T(8,128)(2,1)}, bf16[2048,1368]{1,0:T(8,128)(2,1)}, bf16[2048,1368]{1,0:T(8,128)(2,1)}) custom-call(bf16[256,2048]{1,0:T(8,128)(2,1)} %get-tuple-element.65.z_ref, f32[2048,1368]{1,0:T(8,128)} %get-tuple-element.66.dh_ref, bf16[1368,2048]{1,0:T(8,128)(2,1)} %bitcast.58, ...), custom_call_target="tpu_custom_call" | custom-call | flops 40000000000 | bytes 20000000 | tf_op jit(solution)/shard_map/ag_mlp/pallas_call | solution.py:762
  249.9 51.6 %mlp_back_rs.1 = (f32[256,2048]{1,0:T(8,128)}, bf16[256,2048]{1,0:T(8,128)(2,1)}, f32[1,2048]{1,0:T(1,128)}) custom-call(bf16[2048,1368]{1,0:T(8,128)(2,1)} %get-tuple-element.67.dg_ref, bf16[2048,1368]{1,0:T(8,128)(2,1)} %get-tuple-element.68.du_ref, bf16[1368,2048]{1,0:T(8,128)(2,1)} %bitcast.59, bf16[1368,2048]{1,0:T(8,128)(2,1)} %bitcast.61, ...), custom_call_target="tpu_custom_call" | custom-call | flops 40000000000 | bytes 20000000 | tf_op jit(solution)/shard_map/mlp_back_rs/pallas_call | solution.py:798
  301.5 42.2 %ag_dattn.1 = (bf16[2048,2048]{1,0:T(8,128)(2,1)}, bf16[2048,256]{1,0:T(8,128)(2,1)}, bf16[2048,2048]{1,0:T(8,128)(2,1)}) custom-call(bf16[256,2048]{1,0:T(8,128)(2,1)} %get-tuple-element.69.x_ref, bf16[256,2048]{1,0:T(8,128)(2,1)} %bitcast.67, bf16[2048,1368]{1,0:T(8,128)(2,1)} %get-tuple-element.70.hid_ref, bf16[1368,2048]{1,0:T(8,128)(2,1)} %wd_hbm.3), custom_call_target="tpu_custom_call" | custom-call | flops 40000000000 | bytes 20000000 | tf_op jit(solution)/shard_map/ag_dattn/pallas_call | solution.py:838
  343.7 0.0 reduce-scatter.2.cloned.1.call-update
  343.7 0.0 all-gather.4.cloned.1.call-start
  343.8 22.6 %attn_bwd.1 = (bf16[2,2048,192]{2,1,0:T(8,128)(2,1)}, bf16[2,2048,128]{2,1,0:T(8,128)(2,1)}, f32[2,2048,64]{2,1,0:T(8,128)}, bf16[2,2048,128]{2,1,0:T(8,128)(2,1)}, bf16[12800,2048]{1,0:T(8,128)(2,1)}) custom-call(bf16[2,2048,192]{2,1,0:T(8,128)(2,1)} %get-tuple-element.59.q_ref, bf16[2,2048,192]{2,1,0:T(8,128)(2,1)} %get-tuple-element.60.k_ref, ...), custom_call_target="tpu_custom_call" | custom-call | flops 20000000000 | bytes 20000000 | tf_op jit(solution)/shard_map/attn_bwd/pallas_call | solution.py:307
  366.4 18.7 %fusion.11 = f32[1368,2048]{1,0:T(8,128)} fusion(bf16[2048,1368]{1,0:T(8,128)(2,1)} %get-tuple-element.68.du_ref, bf16[2048,2048]{1,0:T(8,128)(2,1)} %get-tuple-element.72), kind=kOutput, calls=%fused_computation.17 | convolution fusion | flops 11475615744 | bytes 25198592 | tf_op jit(solution)/shard_map/sf,sd->fd/dot_general | solution.py:26
  385.0 71.3 %attn_back_rs.1 = (bf16[256,2688]{1,0:T(8,128)(2,1)}, f32[1,4608]{1,0:T(1,128)}) custom-call(bf16[2,2048,192]{2,1,0:T(8,128)(2,1)} %get-tuple-element.78.dq_ref, bf16[2,2048,128]{2,1,0:T(8,128)(2,1)} %get-tuple-element.79.dk_ref, f32[2,2048,64]{2,1,0:T(8,128)} %get-tuple-element.80.dkp_ref, bf16[2,2048,128]{2,1,0:T(8,128)(2,1)} %get-tuple-element.81.dv_ref, ...), custom_call_target="tpu_custom_call" | custom-call | flops 40000000000 | bytes 20000000 | tf_op jit(solution)/shard_map/attn_back_rs/pallas_call | solution.py:892
  456.4 0.0 all-gather.4.cloned.1.call-update
  456.4 0.0 copy-done.1
  456.4 0.0 copy-start.4
  456.4 0.0 copy-start
  456.5 2.4 copy.32
  458.9 1.3 slice.30
  460.1 2.7 fusion.2
  462.9 2.6 fusion.4
  465.5 0.0 copy-done.4
  465.5 0.6 fusion.10
  466.1 0.0 slice-start.4
  466.1 7.2 %fusion.13 = f32[256,2048]{1,0:T(8,128)} fusion(bf16[2048,256]{1,0:T(8,128)(2,1)S(1)} %copy-done, bf16[2048,2048]{1,0:T(8,128)(2,1)} %get-tuple-element.88), kind=kOutput, calls=%fused_computation.19 | convolution fusion | flops 2147483648 | bytes 11534336 | tf_op jit(solution)/shard_map/sv,sd->vd/dot_general | solution.py:26
  473.3 0.0 slice-done.3
  473.4 0.0 slice-start.5
  473.4 0.0 slice-start
  473.4 0.0 slice-start.6
  473.4 5.2 fusion.14
  478.6 0.0 slice-start.7
  478.6 17.6 %fusion.12 = f32[1368,2048]{1,0:T(8,128)} fusion(bf16[2048,1368]{1,0:T(8,128)(2,1)} %get-tuple-element.67.dg_ref, bf16[2048,2048]{1,0:T(8,128)(2,1)S(1)} %bitcast.80), kind=kOutput, calls=%fused_computation.18 | convolution fusion | flops 11475615744 | bytes 25198592 | tf_op jit(solution)/shard_map/sf,sd->fd/dot_general | solution.py:26
  496.1 0.0 slice-done
  496.2 15.3 %fusion.8 = f32[1368,2048]{1,0:T(8,128)} fusion(bf16[2048,1368]{1,0:T(8,128)(2,1)S(1)} %bitcast.82, bf16[1,2048,2048]{2,1,0:T(8,128)(2,1)S(1)} %bitcast.57), kind=kOutput, calls=%fused_computation.14 | convolution fusion | flops 11475615744 | bytes 25198592 | tf_op jit(solution)/shard_map/sf,sd->fd/dot_general | solution.py:26
  511.5 2.6 fusion.6
  514.0 2.2 all-gather.4.cloned.1.call-done.de_ref
  516.2 9.8 %fusion = f32[2048,576]{0,1:T(8,128)} fusion(bf16[2048,2048]{1,0:T(8,128)(2,1)} %get-tuple-element.86, bf16[2048,2688]{1,0:T(8,128)(2,1)} %all-gather.4.cloned.1.call-done.de_ref), kind=kOutput, calls=%fused_computation | convolution fusion | flops 4831838208 | bytes 15728640 | tf_op jit(solution)/shard_map/sc,sd->cd/dot_general | solution.py:26
  525.9 15.6 %scatter_rows.1 = bf16[12800,2048]{1,0:T(8,128)(2,1)} custom-call(s32[2176]{0:T(1024)} %concatenate.3.slot_ref, s32[2048]{0:T(1024)} %get-tuple-element.57.pos_ref, s32[1]{0:T(128)} %bitcast.1.cnt_ref, bf16[2048,2688]{1,0:T(8,128)(2,1)} %all-gather.4.cloned.1.call-done.de_ref, ...), custom_call_target="tpu_custom_call", output_to_operand_aliasing={{}: (4, {})} | custom-call | flops 20000000000 | bytes 20000000 | tf_op jit(solution)/shard_map/scatter_rows/pallas_call | solution.py:192
  541.6 1.2 copy.35
  542.8 1.2 copy.36
  (22 shorter events, 0.0 us)
Async XLA Ops:
  7.2 149.9 %all-gather.6.cloned.1.call-start = ((), (), s32[]{:S(2)}) async-start(), calls=%async_computation.3 | async-start | bytes 9437184 | tf_op jit(solution)/shard_map/all_gather | solution.py:898
  7.9 503.5 %reduce-scatter.2.cloned.1.call-start = ((), (), s32[]{:S(2)}) async-start(), calls=%async_computation.1 | async-start | bytes 9437184 | tf_op jit(solution)/shard_map/reduce_scatter | solution.py:902
  343.7 172.5 %all-gather.4.cloned.1.call-start = ((), (), s32[]{:S(2)}) async-start(), calls=%async_computation.2 | async-start | bytes 12386304 | tf_op jit(solution)/shard_map/all_gather | solution.py:898
  385.0 71.4 %copy-start.1 = (bf16[2,2048,192]{2,1,0:T(8,128)(2,1)S(1)}, bf16[2,2048,192]{2,1,0:T(8,128)(2,1)}, u32[]{:S(2)}) copy-start(bf16[2,2048,192]{2,1,0:T(8,128)(2,1)} %get-tuple-element.78.dq_ref) | copy-start | bytes 4718596
  456.4 9.1 %copy-start.4 = (f32[1,4608]{1,0:T(1,128)S(1)}, f32[1,4608]{1,0:T(1,128)}, u32[]{:S(2)}) copy-start(f32[1,4608]{1,0:T(1,128)} %get-tuple-element.92) | copy-start | bytes 55300
  456.4 9.7 %copy-start = (bf16[2048,256]{1,0:T(8,128)(2,1)S(1)}, bf16[2048,256]{1,0:T(8,128)(2,1)}, u32[]{:S(2)}) copy-start(bf16[2048,256]{1,0:T(8,128)(2,1)} %get-tuple-element.62.o_ref) | copy-start | bytes 3145732
  460.1 13.2 %slice-start.2 = ((s8[8388608]{0:T(1024)(128)(4,1)}), s8[4194304]{0:T(1024)(128)(4,1)S(1)}, s32[]{:S(2)}) async-start(s8[8388608]{0:T(1024)(128)(4,1)} %bitcast.77), calls=%async_computation.6 | async-start | bytes 8388608
  466.1 7.2 %copy-start.2 = (bf16[2,2048,192]{1,2,0:T(8,128)(2,1)S(1)}, bf16[2,2048,192]{1,2,0:T(8,128)(2,1)}, u32[]{:S(2)}) copy-start(bf16[2,2048,192]{1,2,0:T(8,128)(2,1)} %copy.32) | copy-start | bytes 4718596
  466.1 7.2 %slice-start.3 = ((s8[8388608]{0:T(1024)(128)(4,1)}), s8[4194304]{0:T(1024)(128)(4,1)S(1)}, s32[]{:S(2)}) async-start(s8[8388608]{0:T(1024)(128)(4,1)} %bitcast.77), calls=%async_computation.7 | async-start | bytes 8388608
  466.1 12.4 %slice-start.4 = ((s8[8388608]{0:T(1024)(128)(4,1)}), s8[4194304]{0:T(1024)(128)(4,1)S(1)}, s32[]{:S(2)}) async-start(s8[8388608]{0:T(1024)(128)(4,1)} %bitcast.79), calls=%async_computation.8 | async-start | bytes 8388608
  473.4 5.2 slice-start.5
  473.4 22.8 %slice-start = ((s8[8388608]{0:T(1024)(128)(4,1)}), s8[4194304]{0:T(1024)(128)(4,1)S(1)}, s32[]{:S(2)}) async-start(s8[8388608]{0:T(1024)(128)(4,1)} %bitcast.56), calls=%async_computation.4 | async-start | bytes 8388608
  473.4 22.8 %slice-start.6 = ((s8[5767168]{0:T(1024)(128)(4,1)}), s8[4194304]{0:T(1024)(128)(4,1)S(1)}, s32[]{:S(2)}) async-start(s8[5767168]{0:T(1024)(128)(4,1)} %bitcast.81), calls=%async_computation.10 | async-start | bytes 8388608
  478.6 17.6 %slice-start.1 = ((s8[8388608]{0:T(1024)(128)(4,1)}), s8[4194304]{0:T(1024)(128)(4,1)S(1)}, s32[]{:S(2)}) async-start(s8[8388608]{0:T(1024)(128)(4,1)} %bitcast.56), calls=%async_computation.5 | async-start | bytes 8388608
  478.6 17.6 %slice-start.7 = ((s8[5767168]{0:T(1024)(128)(4,1)}), s8[1572864]{0:T(1024)(128)(4,1)S(1)}, s32[]{:S(2)}) async-start(s8[5767168]{0:T(1024)(128)(4,1)} %bitcast.81), calls=%async_computation.11 | async-start | bytes 3145728
  496.2 15.3 %copy-start.3 = (bf16[256,2048]{1,0:T(8,128)(2,1)S(1)}, bf16[256,2048]{1,0:T(8,128)(2,1)}, u32[]{:S(2)}) copy-start(bf16[256,2048]{1,0:T(8,128)(2,1)} %get-tuple-element.64.h_ref) | copy-start | bytes 3145732
Sparse Core Ops, SparseCore 0:
  9.8 64.1 all-gather.5
  343.9 67.2 reduce-scatter.1
  456.5 59.6 all-gather.3

commit v5 on v4

--- a/solution.py
+++ b/solution.py
@@ -314,6 +314,7 @@
 HALF = 128
 SHARD = 256
 STEPS = 8
+PEERS = (1, 2, 4)
 MESH = pl.DeviceIdType.MESH
 
 
@@ -393,9 +394,9 @@
             c.wait()
 
 
-def ag_run(x_ref, full, send, recv, compute, before=None):
+def ag_run(x_ref, full, send, recv, compute, before=None, peers=None):
     t = lax.axis_index('tp')
-    partner, xn, yn = greet(t, (1, 2, 4))
+    partner, xn, yn = peers or greet(t, PEERS)
     sends = []
 
     def copy(src, shard, first, count, u_there, dev):
@@ -456,9 +457,9 @@
 AG_SEMS = [sems(18), sems(8, 4)]
 
 
-def rs_run(stage, fp, fx, fy, send, recv, produce, finish, after=None, others=(1, 2, 4)):
+def rs_run(stage, fp, fx, fy, send, recv, produce, finish, after=None, others=PEERS, peers=None):
     t = lax.axis_index('tp')
-    partner, xn, yn, *_ = greet(t, others)
+    partner, xn, yn, *_ = peers or greet(t, others)
     sends = []
 
     def copy(src, dst, dev):
@@ -714,31 +715,32 @@
                                         pltpu.SemaphoreType.DMA, sems(2), sems(2)])(o, w_o, e_loc, gain, dy, w_down)
 
 
-def ag_mlp(z, dh, w_gate, w_up):
+def mlp_block(z, dh, w_gate, w_up, h_loc, gain, dy):
     seq, ffn = dh.shape
     dim = z.shape[1]
 
-    def body(z_ref, dh_ref, wg_hbm, wu_hbm, z_out, hid_out, dg_out, du_out, full, wg, wu, dhb, st, send, recv, zsem, wsem, dsem, osem):
+    def body(z_ref, dh_ref, wg_hbm, wu_hbm, h_ref, g_ref, dy_ref, z_out, hid_out, dg_out, du_out, res_ref, resb_ref, dgain_ref,
+             full, wg, wu, dhb, st, dg, du, wsem, dsem, osem, gsem, send, recv, stage, fp, fx, fy, rs_send, rs_recv):
         t = lax.axis_index('tp')
+        peers = greet(t, PEERS)
         loads = [pltpu.make_async_copy(a, b, wsem.at[n]) for n, (a, b) in enumerate(((wg_hbm, wg), (wu_hbm, wu)))]
 
         def ins(i):
             return [pltpu.make_async_copy(dh_ref.at[at, :], dhb.at[i % 2, quarter(j), :], dsem.at[i % 2, j]) for j, at in enumerate(pieces(t, i))]
 
-        def z_copies(i):
-            return [pltpu.make_async_copy(full.at[at, :], z_out.at[at, :], zsem.at[i, j]) for j, at in enumerate(pieces(t, i))]
-
         def outs(i):
-            return [pltpu.make_async_copy(st.at[n, i % 2, quarter(j), :], o.at[at, :], osem.at[n, i % 2, j])
-                    for n, o in enumerate((hid_out, dg_out, du_out)) for j, at in enumerate(pieces(t, i))]
+            return [pltpu.make_async_copy(st.at[i % 2, quarter(j), :], hid_out.at[at, :], osem.at[i % 2, j]) for j, at in enumerate(pieces(t, i))]
+
+        def kept(i):
+            return [pltpu.make_async_copy(a.at[at, :], b.at[at, :], gsem.at[n, i, j])
+                    for n, (a, b) in enumerate(((full, z_out), (dg, dg_out), (du, du_out))) for j, at in enumerate(pieces(t, i))]
 
         for c in loads + ins(0):
             c.start()
+        dgain_ref[...] = jnp.zeros_like(dgain_ref)
 
         def compute(i, rows):
             begin(i, loads, ins, outs)
-            for c in z_copies(i):
-                c.start()
             z_b = join(full, rows)
             for cols in col_tiles(ffn):
                 gate = dot_nt(z_b, wg[cols, :])
@@ -746,57 +748,37 @@
                 d_hid = dhb[i % 2, :, cols]
                 sig = jax.nn.sigmoid(gate)
                 act = gate * sig
-                for n, val in enumerate((act * up, d_hid * up * sig * (1.0 + gate * (1.0 - sig)), d_hid * act)):
-                    st[n, i % 2, :, cols] = val.astype(BF16)
-            for c in outs(i):
+                st[i % 2, :, cols] = (act * up).astype(BF16)
+                for ref, val in ((dg, d_hid * up * sig * (1.0 + gate * (1.0 - sig))), (du, d_hid * act)):
+                    for j, at in enumerate(rows):
+                        ref[at, cols] = val[j * ROWS:(j + 1) * ROWS, :].astype(BF16)
+            for c in outs(i) + kept(i):
                 c.start()
 
-        ag_run(z_ref, full, send, recv, compute)
-        finish_all(outs)
-        for i in range(STEPS):
-            for c in z_copies(i):
-                c.wait()
-
-    act = struct(BF16, seq, ffn)
-    weight = pltpu.VMEM((ffn, dim), BF16)
-    return comm_call(body, 'ag_mlp', 3, [VM, ANY, ANY, ANY], [ANY] * 4, [struct(BF16, seq, dim), act, act, act],
-                     [pltpu.VMEM((seq, dim), BF16), weight, weight, pltpu.VMEM((2, SHARD, ffn), F32), pltpu.VMEM((3, 2, SHARD, ffn), BF16)] + AG_SEMS
-                     + [sems(STEPS, 4), sems(2), sems(2, 4), sems(3, 2, 4)])(z, dh, w_gate, w_up)
-
-
-def mlp_back_rs(d_gate, d_up, w_gate, w_up, h_loc, gain, dy):
-    ffn, dim = w_gate.shape
-
-    def body(dg_ref, du_ref, wg_hbm, wu_hbm, h_ref, g_ref, dy_ref, res_ref, resb_ref, dgain_ref, stage, fp, fx, fy, send, recv, wg, wu, blk, wsem, bsem):
-        t = lax.axis_index('tp')
-        loads = [pltpu.make_async_copy(a, b, wsem.at[n]) for n, (a, b) in enumerate(((wg_hbm, wg), (wu_hbm, wu)))]
-
-        def ins(i):
-            return [pltpu.make_async_copy(r.at[at, :], blk.at[n, i % 2, quarter(j), :], bsem.at[n, i % 2, j])
-                    for n, r in enumerate((dg_ref, du_ref)) for j, at in enumerate(pieces(t, STEPS - 1 - i))]
-
-        for c in ins(0) + loads:
-            c.start()
+        ag_run(z_ref, full, send, recv, compute, peers=peers)
 
         def produce(i, at):
-            begin(i, loads, ins, lambda i: [])
-            dg_b = blk[0, i % 2]
-            du_b = blk[1, i % 2]
+            dg_b, du_b = join(dg, at), join(du, at)
             for cols in col_tiles(dim):
                 stage[i, :, cols] = (dot_nn(dg_b, wg[:, cols]) + dot_nn(du_b, wu[:, cols])).astype(BF16)
-
-        dgain_ref[...] = jnp.zeros_like(dgain_ref)
 
         def finish(at, val):
             res = dy_ref[at, :].astype(F32) + back_rms_rows(h_ref, g_ref, dgain_ref, at, val)
             res_ref[at, :] = res
             resb_ref[at, :] = res.astype(BF16)
 
-        rs_run(stage, fp, fx, fy, send, recv, produce, finish)
-
-    weight = pltpu.VMEM((ffn, dim), BF16)
-    return comm_call(body, 'mlp_back_rs', 4, [ANY] * 4 + [VM] * 3, [VM] * 3, [struct(F32, SHARD, dim), struct(BF16, SHARD, dim), struct(F32, *gain.shape)],
-                     rs_scratch(dim) + [weight, weight, pltpu.VMEM((2, 2, SHARD, ffn), BF16), sems(2), sems(2, 2, 4)])(d_gate, d_up, w_gate, w_up, h_loc, gain, dy)
+        rs_run(stage, fp, fx, fy, rs_send, rs_recv, produce, finish, peers=peers)
+        finish_all(outs)
+        for i in range(STEPS):
+            for c in kept(i):
+                c.wait()
+
+    act = struct(BF16, seq, ffn)
+    weight, wide = pltpu.VMEM((ffn, dim), BF16), pltpu.VMEM((seq, ffn), BF16)
+    return comm_call(body, 'mlp_block', 3, [VM] + [ANY] * 3 + [VM] * 3, [ANY] * 4 + [VM] * 3,
+                     [struct(BF16, seq, dim), act, act, act, struct(F32, SHARD, dim), struct(BF16, SHARD, dim), struct(F32, *gain.shape)],
+                     [pltpu.VMEM((seq, dim), BF16), weight, weight, pltpu.VMEM((2, SHARD, ffn), F32), pltpu.VMEM((2, SHARD, ffn), BF16), wide, wide,
+                      sems(2), sems(2, 4), sems(2, 4), sems(3, STEPS, 4)] + AG_SEMS + rs_scratch(dim))(z, dh, w_gate, w_up, h_loc, gain, dy)
 
 
 def ag_dattn(x, w_o, hidden, w_down):
@@ -927,8 +909,7 @@
         u, q, latent, c_kv, k, kt, v, vt = ag_proj(u_loc, wq, wl, gkv, wuk, wuv, cos_t, sin_t)
         o, lse = attn_fwd(q, k, vt, scale)
         h_loc, z_loc, d_hidden = attn_out_rs(o, wo, e_loc, gml, dy_full, w_down)
-        z, hidden, d_gate, d_up = ag_mlp(z_loc, d_hidden, wg, wu)
-        d_res, d_res_b, dg_mlp = mlp_back_rs(d_gate, d_up, wg, wu, h_loc, gml, dy_loc)
+        z, hidden, d_gate, d_up, d_res, d_res_b, dg_mlp = mlp_block(z_loc, d_hidden, wg, wu, h_loc, gml, dy_loc)
         d_res_full, d_o, mlp_part = ag_dattn(d_res_b, wo, hidden, w_down)
 
         mlp_loc = scatter_seq(mlp_part)
@@ -946,7 +927,7 @@
         dw_uk = matmul_f32('sc,hse->che', c_kv, d_knope)
         dw_uv = matmul_f32('sc,hsv->chv', c_kv, d_value)
         dw_o = matmul_f32('sv,sd->vd', o, d_res_full).reshape(w_o.shape)
-        back_full, dw_gate, dw_down, dw_q, dw_uk, dw_uv, dw_o = lax.optimization_barrier((back_full, dw_gate, dw_down, dw_q, dw_uk, dw_uv, dw_o))
+        back_full, dw_gate, dw_down, dw_q, dw_o = lax.optimization_barrier((back_full, dw_gate, dw_down, dw_q, dw_o))
         dw_gate, dw_up = dw_gate.T, dw_up.T
         dw_dkv = matmul_f32('sc,sd->cd', back_full[:, model_dim:model_dim + w_dkv.shape[1]], u).T
         d_table = scatter_rows(slots, pos, cnt, back_full, zeros)

time: 562 us -> 553 us (0.984)
  Pallas kernels: 436 us -> 430 us
    pallas_call x2 -> x1, Pallas kernels: 99.9 us -> 93.1 us  [mlp_block(): comm_call(body, 'mlp_block', 3, [VM] + [ANY] * 3 + [VM] * 3, [ANY] * 4 +...]
  transfers between devices with their start and end apart: 3 -> 3, of which waited for: 1 -> 1; matrix products, arithmetic and copies ran while one was open for 15% -> 15% of each run, Pallas kernels for 42% -> 43%
where the time goes in v5:
time: 553 us; the launch traced here: 543 us
  Pallas kernels  430 us (78%)
  matrix products  76.6 us (14%)
  between operations  14.5 us (3%)
  other arithmetic  8.99 us (2%)
  local copies, waits for them, and re-layouts  8.56 us (2%)
    pallas_call x1, Pallas kernels, mlp_block(): comm_call(body, 'mlp_block', 3, [VM] + [ANY] * 3 + [VM] * 3, [ANY] * 4 +...  93.1 us
    dot_general x7, matrix products, matmul_f32(): return jnp.einsum(form, lhs, rhs, preferred_element_type=jnp.float32)  71.4 us
    pallas_call x1, Pallas kernels, attn_back_rs(): comm_call(body, 'attn_back_rs', 6, [VM] * 16, [VM] * 2, [struct(BF16, SHA...  71.3 us
    pallas_call x1, Pallas kernels, rs_rows(): comm_call(body, 'rs_rows', 0, [ANY, VM], [VM, VM], [loc, loc], rs_scratch...  57.2 us
    pallas_call x1, Pallas kernels, ag_proj(): comm_call(body, 'ag_proj', 1, [VM, VM, ANY] + [VM] * 5, [ANY] + [VM] * le...  48.6 us
    pallas_call x1, Pallas kernels, attn_out_rs(): comm_call(body, 'attn_out_rs', 2, [VM] * 4 + [ANY] * 2, [VM, VM, ANY], [l...  44.6 us
    pallas_call x1, Pallas kernels, ag_dattn(): comm_call(body, 'ag_dattn', 5, [VM, VM, ANY, ANY], [ANY, VM, ANY], [big,...  42.2 us
    pallas_call x1, Pallas kernels, attn_bwd(): local_call(functools.partial(attn_bwd_body, scale * LOG2E, scale), 'attn_...  22.6 us
  transfers between devices with their start and end apart: 3, of which 1 were waited for; matrix products, arithmetic and copies ran while one was open for 15% of the time, Pallas kernels for 43%

profile of v5, /device:TPU:0, one launch (start us, length us, event | category | flops | bytes accessed | tf_op | source)
XLA Modules:
  0.0 542.6 jit_solution(14940586452278542319)
XLA Ops:
  7.2 0.0 all-gather.6.cloned.1.call-start
  7.2 0.7 all-gather.6.cloned.1.call-update
  7.9 0.0 reduce-scatter.2.cloned.1.call-start
  8.0 0.7 broadcast_subtract_fusion
  8.7 0.7 convert_reduce_fusion
  9.3 5.0 sort.15
  14.4 0.6 concatenate.3.slot_ref
  15.0 1.9 copy_bitcast_fusion
  16.9 21.6 %gather_rows.1.rows_ref = bf16[2048,2048]{1,0:T(8,128)(2,1)} custom-call(s32[2176]{0:T(1024)} %concatenate.3.slot_ref, s32[2048]{0:T(1024)} %get-tuple-element.55.pos_ref, s32[1]{0:T(128)} %bitcast.1.cnt_ref, bf16[12800,2048]{1,0:T(8,128)(2,1)} %tab_ref.1), custom_call_target="tpu_custom_call" | custom-call | flops 20000000000 | bytes 20000000 | tf_op jit(solution)/shard_map/gather_rows/pallas_call | solution.py:139
  38.5 57.2 %rs_rows.1 = (bf16[256,2048]{1,0:T(8,128)(2,1)}, bf16[256,2048]{1,0:T(8,128)(2,1)}) custom-call(bf16[2048,2048]{1,0:T(8,128)(2,1)} %gather_rows.1.rows_ref, f32[1,2048]{1,0:T(1,128)} %bitcast.68), custom_call_target="tpu_custom_call" | custom-call | flops 40000000000 | bytes 20000000 | tf_op jit(solution)/shard_map/rs_rows/pallas_call | solution.py:595
  95.7 48.6 %ag_proj.1 = (bf16[2048,2048]{1,0:T(8,128)(2,1)}, bf16[2,2048,192]{2,1,0:T(8,128)(2,1)}, f32[2048,576]{1,0:T(8,128)}, bf16[2048,512]{1,0:T(8,128)(2,1)}, bf16[2,...) custom-call(bf16[256,2048]{1,0:T(8,128)(2,1)} %get-tuple-element.56., ...), custom_call_target="tpu_custom_call" | custom-call | flops 40000000000 | bytes 20000000 | tf_op jit(solution)/shard_map/ag_proj/pallas_call | solution.py:664
  144.3 12.7 %attn_fwd.1 = (bf16[2048,256]{1,0:T(8,128)(2,1)}, f32[2,1,2048]{2,1,0:T(1,128)}) custom-call(bf16[2,2048,192]{2,1,0:T(8,128)(2,1)} %get-tuple-element.57.q_ref, bf16[2,2048,192]{2,1,0:T(8,128)(2,1)} %get-tuple-element.58.k_ref, bf16[2,128,2048]{2,1,0:T(8,128)(2,1)} %get-tuple-element.59.vt_ref), custom_call_target="tpu_custom_call" | custom-call | flops 20000000000 | bytes 20000000 | tf_op jit(solution)/shard_map/attn_fwd/pallas_call | solution.py:245
  157.1 44.6 %attn_out_rs.1 = (bf16[256,2048]{1,0:T(8,128)(2,1)}, bf16[256,2048]{1,0:T(8,128)(2,1)}, f32[2048,1368]{1,0:T(8,128)}) custom-call(bf16[2048,256]{1,0:T(8,128)(2,1)} %get-tuple-element.60.o_ref, bf16[256,2048]{1,0:T(8,128)(2,1)} %bitcast.64, bf16[256,2048]{1,0:T(8,128)(2,1)} %get-tuple-element.61.e_ref, f32[1,2048]{1,0:T(1,128)} %bitcast.66, ...), custom_call_target="tpu_custom_call" | custom-call | flops 40000000000 | bytes 20000000 | tf_op jit(solution)/shard_map/attn_out_rs/pallas_call | solution.py:713
  201.7 93.1 %mlp_block.1 = (bf16[2048,2048]{1,0:T(8,128)(2,1)}, bf16[2048,1368]{1,0:T(8,128)(2,1)}, bf16[2048,1368]{1,0:T(8,128)(2,1)}, bf16[2048,1368]{1,0:T(8,128)(2,1)}, ...) custom-call(bf16[256,2048]{1,0:T(8,128)(2,1)} %get-tuple-element.63.z_ref, ...), custom_call_target="tpu_custom_call" | custom-call | flops 40000000000 | bytes 20000000 | tf_op jit(solution)/shard_map/mlp_block/pallas_call | solution.py:778
  294.8 42.2 %ag_dattn.1 = (bf16[2048,2048]{1,0:T(8,128)(2,1)}, bf16[2048,256]{1,0:T(8,128)(2,1)}, bf16[2048,2048]{1,0:T(8,128)(2,1)}) custom-call(bf16[256,2048]{1,0:T(8,128)(2,1)} %get-tuple-element.65.x_ref, bf16[256,2048]{1,0:T(8,128)(2,1)} %bitcast.65, bf16[2048,1368]{1,0:T(8,128)(2,1)} %get-tuple-element.66.hid_ref, bf16[1368,2048]{1,0:T(8,128)(2,1)} %wd_hbm.3), custom_call_target="tpu_custom_call" | custom-call | flops 40000000000 | bytes 20000000 | tf_op jit(solution)/shard_map/ag_dattn/pallas_call | solution.py:820
  337.0 0.0 reduce-scatter.2.cloned.1.call-update
  337.0 0.0 all-gather.4.cloned.1.call-start
  337.1 22.6 %attn_bwd.1 = (bf16[2,2048,192]{2,1,0:T(8,128)(2,1)}, bf16[2,2048,128]{2,1,0:T(8,128)(2,1)}, f32[2,2048,64]{2,1,0:T(8,128)}, bf16[2,2048,128]{2,1,0:T(8,128)(2,1)}, bf16[12800,2048]{1,0:T(8,128)(2,1)}) custom-call(bf16[2,2048,192]{2,1,0:T(8,128)(2,1)} %get-tuple-element.57.q_ref, bf16[2,2048,192]{2,1,0:T(8,128)(2,1)} %get-tuple-element.58.k_ref, ...), custom_call_target="tpu_custom_call" | custom-call | flops 20000000000 | bytes 20000000 | tf_op jit(solution)/shard_map/attn_bwd/pallas_call | solution.py:307
  359.7 18.7 %fusion.11 = f32[1368,2048]{1,0:T(8,128)} fusion(bf16[2048,1368]{1,0:T(8,128)(2,1)} %get-tuple-element.68, bf16[2048,2048]{1,0:T(8,128)(2,1)} %get-tuple-element.69), kind=kOutput, calls=%fused_computation.17 | convolution fusion | flops 11475615744 | bytes 25198592 | tf_op jit(solution)/shard_map/sf,sd->fd/dot_general | solution.py:26
  378.3 71.3 %attn_back_rs.1 = (bf16[256,2688]{1,0:T(8,128)(2,1)}, f32[1,4608]{1,0:T(1,128)}) custom-call(bf16[2,2048,192]{2,1,0:T(8,128)(2,1)} %get-tuple-element.75.dq_ref, bf16[2,2048,128]{2,1,0:T(8,128)(2,1)} %get-tuple-element.76.dk_ref, f32[2,2048,64]{2,1,0:T(8,128)} %get-tuple-element.77.dkp_ref, bf16[2,2048,128]{2,1,0:T(8,128)(2,1)} %get-tuple-element.78.dv_ref, ...), custom_call_target="tpu_custom_call" | custom-call | flops 40000000000 | bytes 20000000 | tf_op jit(solution)/shard_map/attn_back_rs/pallas_call | solution.py:874
  449.7 0.0 copy-start.5
  449.7 0.0 all-gather.4.cloned.1.call-update
  449.7 2.4 copy.32
  452.2 0.0 copy-start
  452.2 2.7 fusion.4
  454.9 1.2 copy.35
  456.1 2.5 fusion.2
  458.6 1.2 copy.36
  459.8 0.6 slice.30
  460.4 0.6 fusion.10
  461.0 0.0 copy-done
  461.0 0.0 slice-start.4
  461.0 0.0 slice-start.8
  461.0 7.2 %fusion.13 = f32[256,2048]{1,0:T(8,128)} fusion(bf16[2048,256]{1,0:T(8,128)(2,1)S(1)} %copy-done, bf16[2048,2048]{1,0:T(8,128)(2,1)} %get-tuple-element.85), kind=kOutput, calls=%fused_computation.19 | convolution fusion | flops 2147483648 | bytes 11534336 | tf_op jit(solution)/shard_map/sv,sd->vd/dot_general | solution.py:26
  468.2 0.0 slice-start.5
  468.2 0.0 slice-start.9
  468.2 0.0 slice-start
  468.3 0.0 slice-start.6
  468.3 5.2 fusion.14
  473.4 0.0 slice-done.4
  473.5 0.0 slice-start.1
  473.5 0.0 slice-start.7
  473.5 15.3 %fusion.12 = f32[1368,2048]{1,0:T(8,128)} fusion(bf16[2048,1368]{1,0:T(8,128)(2,1)S(1)} %bitcast.82, bf16[2048,2048]{1,0:T(8,128)(2,1)S(1)} %bitcast.78), kind=kOutput, calls=%fused_computation.18 | convolution fusion | flops 11475615744 | bytes 25198592 | tf_op jit(solution)/shard_map/sf,sd->fd/dot_general | solution.py:26
  488.8 15.0 %fusion.8 = f32[1368,2048]{1,0:T(8,128)} fusion(bf16[2048,1368]{1,0:T(8,128)(2,1)S(1)} %bitcast.80, bf16[1,2048,2048]{2,1,0:T(8,128)(2,1)S(1)} %bitcast.57), kind=kOutput, calls=%fused_computation.14 | convolution fusion | flops 11475615744 | bytes 25198592 | tf_op jit(solution)/shard_map/sf,sd->fd/dot_general | solution.py:26
  503.8 2.6 fusion.6
  506.4 3.1 all-gather.4.cloned.1.call-done.de_ref
  509.5 10.0 %fusion = f32[2048,576]{0,1:T(8,128)} fusion(bf16[2048,2048]{1,0:T(8,128)(2,1)} %get-tuple-element.84, bf16[2048,2688]{1,0:T(8,128)(2,1)} %all-gather.4.cloned.1.call-done.de_ref), kind=kOutput, calls=%fused_computation | convolution fusion | flops 4831838208 | bytes 15728640 | tf_op jit(solution)/shard_map/sc,sd->cd/dot_general | solution.py:26
  519.5 16.0 %scatter_rows.1 = bf16[12800,2048]{1,0:T(8,128)(2,1)} custom-call(s32[2176]{0:T(1024)} %concatenate.3.slot_ref, s32[2048]{0:T(1024)} %get-tuple-element.55.pos_ref, s32[1]{0:T(128)} %bitcast.1.cnt_ref, bf16[2048,2688]{1,0:T(8,128)(2,1)} %all-gather.4.cloned.1.call-done.de_ref, ...), custom_call_target="tpu_custom_call", output_to_operand_aliasing={{}: (4, {})} | custom-call | flops 20000000000 | bytes 20000000 | tf_op jit(solution)/shard_map/scatter_rows/pallas_call | solution.py:192
  (28 shorter events, 0.0 us)
Async XLA Ops:
  7.2 149.9 %all-gather.6.cloned.1.call-start = ((), (), s32[]{:S(2)}) async-start(), calls=%async_computation.3 | async-start | bytes 9437184 | tf_op jit(solution)/shard_map/all_gather | solution.py:880
  7.9 495.9 %reduce-scatter.2.cloned.1.call-start = ((), (), s32[]{:S(2)}) async-start(), calls=%async_computation.1 | async-start | bytes 9437184 | tf_op jit(solution)/shard_map/reduce_scatter | solution.py:884
  337.0 172.5 %all-gather.4.cloned.1.call-start = ((), (), s32[]{:S(2)}) async-start(), calls=%async_computation.2 | async-start | bytes 12386304 | tf_op jit(solution)/shard_map/all_gather | solution.py:880
  378.3 71.4 %copy-start.1 = (bf16[2,2048,192]{2,1,0:T(8,128)(2,1)S(1)}, bf16[2,2048,192]{2,1,0:T(8,128)(2,1)}, u32[]{:S(2)}) copy-start(bf16[2,2048,192]{2,1,0:T(8,128)(2,1)} %get-tuple-element.75.dq_ref) | copy-start | bytes 4718596
  449.7 6.4 %copy-start.5 = (bf16[2,2048,128]{2,1,0:T(8,128)(2,1)S(1)}, bf16[2,2048,128]{2,1,0:T(8,128)(2,1)}, u32[]{:S(2)}) copy-start(bf16[2,2048,128]{2,1,0:T(8,128)(2,1)} %get-tuple-element.78.dv_ref) | copy-start | bytes 3145732
  452.2 7.6 %copy-start.4 = (f32[1,4608]{1,0:T(1,128)S(1)}, f32[1,4608]{1,0:T(1,128)}, u32[]{:S(2)}) copy-start(f32[1,4608]{1,0:T(1,128)} %get-tuple-element.89) | copy-start | bytes 55300
  452.2 8.8 %copy-start = (bf16[2048,256]{1,0:T(8,128)(2,1)S(1)}, bf16[2048,256]{1,0:T(8,128)(2,1)}, u32[]{:S(2)}) copy-start(bf16[2048,256]{1,0:T(8,128)(2,1)} %get-tuple-element.60.o_ref) | copy-start | bytes 3145732
  456.1 12.1 %slice-start.2 = ((s8[8388608]{0:T(1024)(128)(4,1)}), s8[4194304]{0:T(1024)(128)(4,1)S(1)}, s32[]{:S(2)}) async-start(s8[8388608]{0:T(1024)(128)(4,1)} %bitcast.75), calls=%async_computation.6 | async-start | bytes 8388608
  461.0 7.2 %copy-start.2 = (bf16[2,2048,192]{1,2,0:T(8,128)(2,1)S(1)}, bf16[2,2048,192]{1,2,0:T(8,128)(2,1)}, u32[]{:S(2)}) copy-start(bf16[2,2048,192]{1,2,0:T(8,128)(2,1)} %copy.32) | copy-start | bytes 4718596
  461.0 7.2 %slice-start.3 = ((s8[8388608]{0:T(1024)(128)(4,1)}), s8[4194304]{0:T(1024)(128)(4,1)S(1)}, s32[]{:S(2)}) async-start(s8[8388608]{0:T(1024)(128)(4,1)} %bitcast.75), calls=%async_computation.7 | async-start | bytes 8388608
  461.0 12.5 %slice-start.4 = ((s8[8388608]{0:T(1024)(128)(4,1)}), s8[4194304]{0:T(1024)(128)(4,1)S(1)}, s32[]{:S(2)}) async-start(s8[8388608]{0:T(1024)(128)(4,1)} %bitcast.77), calls=%async_computation.8 | async-start | bytes 8388608
  461.0 12.5 %slice-start.8 = ((s8[5767168]{0:T(1024)(128)(4,1)}), s8[4194304]{0:T(1024)(128)(4,1)S(1)}, s32[]{:S(2)}) async-start(s8[5767168]{0:T(1024)(128)(4,1)} %bitcast.81), calls=%async_computation.12 | async-start | bytes 8388608
  468.2 5.2 slice-start.5
  468.2 5.2 slice-start.9
  468.2 20.5 %slice-start = ((s8[8388608]{0:T(1024)(128)(4,1)}), s8[4194304]{0:T(1024)(128)(4,1)S(1)}, s32[]{:S(2)}) async-start(s8[8388608]{0:T(1024)(128)(4,1)} %bitcast.56), calls=%async_computation.4 | async-start | bytes 8388608
  468.3 20.5 %slice-start.6 = ((s8[5767168]{0:T(1024)(128)(4,1)}), s8[4194304]{0:T(1024)(128)(4,1)S(1)}, s32[]{:S(2)}) async-start(s8[5767168]{0:T(1024)(128)(4,1)} %bitcast.79), calls=%async_computation.10 | async-start | bytes 8388608
  473.5 15.3 %slice-start.1 = ((s8[8388608]{0:T(1024)(128)(4,1)}), s8[4194304]{0:T(1024)(128)(4,1)S(1)}, s32[]{:S(2)}) async-start(s8[8388608]{0:T(1024)(128)(4,1)} %bitcast.56), calls=%async_computation.5 | async-start | bytes 8388608
  473.5 15.3 %slice-start.7 = ((s8[5767168]{0:T(1024)(128)(4,1)}), s8[1572864]{0:T(1024)(128)(4,1)S(1)}, s32[]{:S(2)}) async-start(s8[5767168]{0:T(1024)(128)(4,1)} %bitcast.79), calls=%async_computation.11 | async-start | bytes 3145728
  488.8 15.0 %copy-start.3 = (bf16[256,2048]{1,0:T(8,128)(2,1)S(1)}, bf16[256,2048]{1,0:T(8,128)(2,1)}, u32[]{:S(2)}) copy-start(bf16[256,2048]{1,0:T(8,128)(2,1)} %get-tuple-element.62.h_ref) | copy-start | bytes 3145732
Sparse Core Ops, SparseCore 0:
  9.8 64.4 all-gather.5
  337.2 67.2 reduce-scatter.1
  449.9 59.6 all-gather.3

commit v6 on v5

--- a/solution.py
+++ b/solution.py
@@ -566,46 +566,38 @@
     return d_x
 
 
-def rs_rows(rows, gain):
-    dim = rows.shape[1]
-
-    def body(rows_ref, g_ref, e_ref, u_ref, stage, fp, fx, fy, send, recv, load):
-        t = lax.axis_index('tp')
-
-        def fetch(i):
-            return [pltpu.make_async_copy(rows_ref.at[at, :], stage.at[i, quarter(j), :], load.at[i, j]) for j, at in enumerate(pieces(t, STEPS - 1 - i))]
-
-        for i in range(STEPS):
-            for c in fetch(i):
-                c.start()
-
-        def produce(i, at):
-            for c in fetch(i):
-                c.wait()
-
-        def finish(at, val):
-            e_b = val.astype(BF16)
-            e_ref[at, :] = e_b
-            x = e_b.astype(F32)
-            u_ref[at, :] = (x * rms_inv(x) * g_ref[...]).astype(BF16)
-
-        rs_run(stage, fp, fx, fy, send, recv, produce, finish)
-
-    loc = struct(BF16, SHARD, dim)
-    return comm_call(body, 'rs_rows', 0, [ANY, VM], [VM, VM], [loc, loc], rs_scratch(dim) + [sems(STEPS, 4)])(rows, gain)
-
-
-def ag_proj(x, w_q, w_dkv, g_kv, w_uk, w_uv, cos_t, sin_t):
+def embed_proj(rows, g_attn, w_q, w_dkv, g_kv, w_uk, w_uv, cos_t, sin_t):
     seq = cos_t.shape[0]
     heads, qk, dim = w_q.shape
     lat = w_dkv.shape[0]
     rank, nope = w_uk.shape[1:]
     vdim = w_uv.shape[2]
 
-    def body(x_ref, wq_ref, wl_hbm, g_ref, wk_ref, wv_ref, cos_ref, sin_ref, x_out, q_ref, l_ref, c_ref, k_ref, kt_ref, v_ref, vt_ref, full, send, recv, sem, wl, wsem):
+    def body(rows_ref, ga_ref, wq_ref, wl_hbm, g_ref, wk_ref, wv_ref, cos_ref, sin_ref, x_out, e_ref, q_ref, l_ref, c_ref, k_ref, kt_ref, v_ref, vt_ref,
+             full, send, recv, sem, wl, wsem, u_ref, load, stage, fp, fx, fy, rs_send, rs_recv):
         t = lax.axis_index('tp')
+
+        def fetch(i):
+            return [pltpu.make_async_copy(rows_ref.at[at, :], stage.at[i, quarter(j), :], load.at[i, j]) for j, at in enumerate(pieces(t, STEPS - 1 - i))]
+
+        for i in range(STEPS):
+            for c in fetch(i):
+                c.start()
         w_load = pltpu.make_async_copy(wl_hbm, wl, wsem)
         w_load.start()
+        peers = greet(t, PEERS)
+
+        def produce(i, at):
+            for c in fetch(i):
+                c.wait()
+
+        def finish(at, val):
+            e_b = val.astype(BF16)
+            e_ref[at, :] = e_b
+            x = e_b.astype(F32)
+            u_ref[at, :] = (x * rms_inv(x) * ga_ref[...]).astype(BF16)
+
+        rs_run(stage, fp, fx, fy, rs_send, rs_recv, produce, finish, peers=peers)
 
         def x_copies(i):
             return [pltpu.make_async_copy(full.at[at, :], x_out.at[at, :], sem.at[i, j]) for j, at in enumerate(pieces(t, i))]
@@ -655,14 +647,15 @@
                 for j in range(4):
                     turn(STEPS - 1, j)
 
-        ag_run(x_ref, full, send, recv, compute)
+        ag_run(u_ref, full, send, recv, compute, peers=peers)
         for i in range(STEPS):
             for c in x_copies(i):
                 c.wait()
 
-    per = [struct(BF16, heads, seq, qk), struct(F32, seq, lat), struct(BF16, seq, rank), struct(BF16, heads, seq, qk), struct(BF16, heads, qk, seq), struct(BF16, heads, seq, vdim), struct(BF16, heads, vdim, seq)]
-    return comm_call(body, 'ag_proj', 1, [VM, VM, ANY] + [VM] * 5, [ANY] + [VM] * len(per), [struct(BF16, seq, dim)] + per,
-                     [pltpu.VMEM((seq, dim), BF16)] + AG_SEMS + [sems(STEPS, 4), pltpu.VMEM((lat, dim), BF16), pltpu.SemaphoreType.DMA])(x, w_q, w_dkv, g_kv, w_uk, w_uv, cos_t, sin_t)
+    per = [struct(BF16, SHARD, dim), struct(BF16, heads, seq, qk), struct(F32, seq, lat), struct(BF16, seq, rank), struct(BF16, heads, seq, qk), struct(BF16, heads, qk, seq), struct(BF16, heads, seq, vdim), struct(BF16, heads, vdim, seq)]
+    return comm_call(body, 'embed_proj', 1, [ANY, VM, VM, ANY] + [VM] * 5, [ANY] + [VM] * len(per), [struct(BF16, seq, dim)] + per,
+                     [pltpu.VMEM((seq, dim), BF16)] + AG_SEMS + [sems(STEPS, 4), pltpu.VMEM((lat, dim), BF16), pltpu.SemaphoreType.DMA, pltpu.VMEM((SHARD, dim), BF16), sems(STEPS, 4)] + rs_scratch(dim))(
+                         rows, g_attn, w_q, w_dkv, g_kv, w_uk, w_uv, cos_t, sin_t)
 
 
 def shard_rows(i):
@@ -905,8 +898,7 @@
         slots = jnp.concatenate([slots, jnp.full((128,), vocab_local, jnp.int32)])
         cnt = jnp.sum(owned.astype(jnp.int32)).reshape(1)
         rows = gather_rows(slots, pos, cnt, embed_table, seq)
-        e_loc, u_loc = rs_rows(rows, gat)
-        u, q, latent, c_kv, k, kt, v, vt = ag_proj(u_loc, wq, wl, gkv, wuk, wuv, cos_t, sin_t)
+        u, e_loc, q, latent, c_kv, k, kt, v, vt = embed_proj(rows, gat, wq, wl, gkv, wuk, wuv, cos_t, sin_t)
         o, lse = attn_fwd(q, k, vt, scale)
         h_loc, z_loc, d_hidden = attn_out_rs(o, wo, e_loc, gml, dy_full, w_down)
         z, hidden, d_gate, d_up, d_res, d_res_b, dg_mlp = mlp_block(z_loc, d_hidden, wg, wu, h_loc, gml, dy_loc)

time: 553 us -> 549 us (level)
    pallas_call x2 -> x1, Pallas kernels: 106 us -> 102 us  [embed_proj(): comm_call(body, 'embed_proj', 1, [ANY, VM, VM, ANY] + [VM] * 5, [ANY] + [...]
  transfers between devices with their start and end apart: 3 -> 3, of which waited for: 1 -> 1; matrix products, arithmetic and copies ran while one was open for 15% -> 16% of each run, Pallas kernels for 43% -> 43%
where the time goes in v6:
time: 549 us; the launch traced here: 538 us
  Pallas kernels  426 us (78%)
  matrix products  76.6 us (14%)
  between operations  14.5 us (3%)
  other arithmetic  9.03 us (2%)
  local copies, waits for them, and re-layouts  8.56 us (2%)
    pallas_call x1, Pallas kernels, embed_proj(): comm_call(body, 'embed_proj', 1, [ANY, VM, VM, ANY] + [VM] * 5, [ANY] + [...  102 us
    pallas_call x1, Pallas kernels, mlp_block(): comm_call(body, 'mlp_block', 3, [VM] + [ANY] * 3 + [VM] * 3, [ANY] * 4 +...  93.3 us
    dot_general x7, matrix products, matmul_f32(): return jnp.einsum(form, lhs, rhs, preferred_element_type=jnp.float32)  71.4 us
    pallas_call x1, Pallas kernels, attn_back_rs(): comm_call(body, 'attn_back_rs', 6, [VM] * 16, [VM] * 2, [struct(BF16, SHA...  71.3 us
    pallas_call x1, Pallas kernels, attn_out_rs(): comm_call(body, 'attn_out_rs', 2, [VM] * 4 + [ANY] * 2, [VM, VM, ANY], [l...  43.8 us
    pallas_call x1, Pallas kernels, ag_dattn(): comm_call(body, 'ag_dattn', 5, [VM, VM, ANY, ANY], [ANY, VM, ANY], [big,...  42.2 us
    pallas_call x1, Pallas kernels, attn_bwd(): local_call(functools.partial(attn_bwd_body, scale * LOG2E, scale), 'attn_...  22.6 us
    pallas_call x1, Pallas kernels, gather_rows(): local_call(gather_body, 'gather_rows', jax.ShapeDtypeStruct((seq, dim), B...  21.6 us
  transfers between devices with their start and end apart: 3, of which 1 were waited for; matrix products, arithmetic and copies ran while one was open for 16% of the time, Pallas kernels for 43%

profile of v6, /device:TPU:0, one launch (start us, length us, event | category | flops | bytes accessed | tf_op | source)
XLA Modules:
  0.0 538.2 jit_solution(1092392972237468665)
XLA Ops:
  7.2 0.0 all-gather.6.cloned.1.call-start
  7.2 0.7 all-gather.6.cloned.1.call-update
  7.9 0.0 reduce-scatter.2.cloned.1.call-start
  8.0 0.7 broadcast_subtract_fusion
  8.7 0.7 convert_reduce_fusion
  9.4 5.0 sort.15
  14.4 0.6 concatenate.3.slot_ref
  15.0 1.9 copy_bitcast_fusion
  16.9 21.6 %gather_rows.1.rows_ref = bf16[2048,2048]{1,0:T(8,128)(2,1)} custom-call(s32[2176]{0:T(1024)} %concatenate.3.slot_ref, s32[2048]{0:T(1024)} %get-tuple-element.54.pos_ref, s32[1]{0:T(128)} %bitcast.1.cnt_ref, bf16[12800,2048]{1,0:T(8,128)(2,1)} %tab_ref.1), custom_call_target="tpu_custom_call" | custom-call | flops 20000000000 | bytes 20000000 | tf_op jit(solution)/shard_map/gather_rows/pallas_call | solution.py:139
  38.5 102.2 %embed_proj.1 = (bf16[2048,2048]{1,0:T(8,128)(2,1)}, bf16[256,2048]{1,0:T(8,128)(2,1)}, bf16[2,2048,192]{2,1,0:T(8,128)(2,1)}, f32[2048,576]{1,0:T(8,128)}, bf16...) custom-call(bf16[2048,2048]{1,0:T(8,128)(2,1)} %gather_rows.1.rows_r, ...), custom_call_target="tpu_custom_call" | custom-call | flops 40000000000 | bytes 20000000 | tf_op jit(solution)/shard_map/embed_proj/pallas_call | solution.py:656
  140.7 12.7 %attn_fwd.1 = (bf16[2048,256]{1,0:T(8,128)(2,1)}, f32[2,1,2048]{2,1,0:T(1,128)}) custom-call(bf16[2,2048,192]{2,1,0:T(8,128)(2,1)} %get-tuple-element.55.q_ref, bf16[2,2048,192]{2,1,0:T(8,128)(2,1)} %get-tuple-element.56.k_ref, bf16[2,128,2048]{2,1,0:T(8,128)(2,1)} %get-tuple-element.57.vt_ref), custom_call_target="tpu_custom_call" | custom-call | flops 20000000000 | bytes 20000000 | tf_op jit(solution)/shard_map/attn_fwd/pallas_call | solution.py:245
  153.4 43.8 %attn_out_rs.1 = (bf16[256,2048]{1,0:T(8,128)(2,1)}, bf16[256,2048]{1,0:T(8,128)(2,1)}, f32[2048,1368]{1,0:T(8,128)}) custom-call(bf16[2048,256]{1,0:T(8,128)(2,1)} %get-tuple-element.58.o_ref, bf16[256,2048]{1,0:T(8,128)(2,1)} %bitcast.64, bf16[256,2048]{1,0:T(8,128)(2,1)} %get-tuple-element.59.e_ref, f32[1,2048]{1,0:T(1,128)} %bitcast.66, ...), custom_call_target="tpu_custom_call" | custom-call | flops 40000000000 | bytes 20000000 | tf_op jit(solution)/shard_map/attn_out_rs/pallas_call | solution.py:706
  197.2 93.3 %mlp_block.1 = (bf16[2048,2048]{1,0:T(8,128)(2,1)}, bf16[2048,1368]{1,0:T(8,128)(2,1)}, bf16[2048,1368]{1,0:T(8,128)(2,1)}, bf16[2048,1368]{1,0:T(8,128)(2,1)}, ...) custom-call(bf16[256,2048]{1,0:T(8,128)(2,1)} %get-tuple-element.61.z_ref, ...), custom_call_target="tpu_custom_call" | custom-call | flops 40000000000 | bytes 20000000 | tf_op jit(solution)/shard_map/mlp_block/pallas_call | solution.py:771
  290.6 42.2 %ag_dattn.1 = (bf16[2048,2048]{1,0:T(8,128)(2,1)}, bf16[2048,256]{1,0:T(8,128)(2,1)}, bf16[2048,2048]{1,0:T(8,128)(2,1)}) custom-call(bf16[256,2048]{1,0:T(8,128)(2,1)} %get-tuple-element.63.x_ref, bf16[256,2048]{1,0:T(8,128)(2,1)} %bitcast.65, bf16[2048,1368]{1,0:T(8,128)(2,1)} %get-tuple-element.64.hid_ref, bf16[1368,2048]{1,0:T(8,128)(2,1)} %wd_hbm.3), custom_call_target="tpu_custom_call" | custom-call | flops 40000000000 | bytes 20000000 | tf_op jit(solution)/shard_map/ag_dattn/pallas_call | solution.py:813
  332.8 0.0 reduce-scatter.2.cloned.1.call-update
  332.8 0.0 all-gather.4.cloned.1.call-start
  332.8 22.6 %attn_bwd.1 = (bf16[2,2048,192]{2,1,0:T(8,128)(2,1)}, bf16[2,2048,128]{2,1,0:T(8,128)(2,1)}, f32[2,2048,64]{2,1,0:T(8,128)}, bf16[2,2048,128]{2,1,0:T(8,128)(2,1)}, bf16[12800,2048]{1,0:T(8,128)(2,1)}) custom-call(bf16[2,2048,192]{2,1,0:T(8,128)(2,1)} %get-tuple-element.55.q_ref, bf16[2,2048,192]{2,1,0:T(8,128)(2,1)} %get-tuple-element.56.k_ref, ...), custom_call_target="tpu_custom_call" | custom-call | flops 20000000000 | bytes 20000000 | tf_op jit(solution)/shard_map/attn_bwd/pallas_call | solution.py:307
  355.4 18.7 %fusion.11 = f32[1368,2048]{1,0:T(8,128)} fusion(bf16[2048,1368]{1,0:T(8,128)(2,1)} %get-tuple-element.66, bf16[2048,2048]{1,0:T(8,128)(2,1)} %get-tuple-element.67), kind=kOutput, calls=%fused_computation.17 | convolution fusion | flops 11475615744 | bytes 25198592 | tf_op jit(solution)/shard_map/sf,sd->fd/dot_general | solution.py:26
  374.1 71.3 %attn_back_rs.1 = (bf16[256,2688]{1,0:T(8,128)(2,1)}, f32[1,4608]{1,0:T(1,128)}) custom-call(bf16[2,2048,192]{2,1,0:T(8,128)(2,1)} %get-tuple-element.73.dq_ref, bf16[2,2048,128]{2,1,0:T(8,128)(2,1)} %get-tuple-element.74.dk_ref, f32[2,2048,64]{2,1,0:T(8,128)} %get-tuple-element.75.dkp_ref, bf16[2,2048,128]{2,1,0:T(8,128)(2,1)} %get-tuple-element.76.dv_ref, ...), custom_call_target="tpu_custom_call" | custom-call | flops 40000000000 | bytes 20000000 | tf_op jit(solution)/shard_map/attn_back_rs/pallas_call | solution.py:867
  445.4 0.0 copy-start.5
  445.4 0.0 all-gather.4.cloned.1.call-update
  445.5 0.0 copy-done.1
  445.5 2.4 copy.32
  447.9 0.0 copy-start
  447.9 2.7 fusion.4
  450.6 1.2 copy.35
  451.8 0.0 copy-done.5
  451.8 2.5 fusion.2
  454.3 1.2 copy.36
  455.5 0.0 copy-done.4
  455.5 0.6 slice.30
  456.1 0.6 fusion.10
  456.7 0.0 slice-start.4
  456.7 0.0 slice-start.8
  456.7 7.2 %fusion.13 = f32[256,2048]{1,0:T(8,128)} fusion(bf16[2048,256]{1,0:T(8,128)(2,1)S(1)} %copy-done, bf16[2048,2048]{1,0:T(8,128)(2,1)} %get-tuple-element.83), kind=kOutput, calls=%fused_computation.19 | convolution fusion | flops 2147483648 | bytes 11534336 | tf_op jit(solution)/shard_map/sv,sd->vd/dot_general | solution.py:26
  464.0 0.0 slice-start.5
  464.0 0.0 slice-start.9
  464.0 0.0 slice-start
  464.0 0.0 slice-start.6
  464.0 5.2 fusion.14
  469.2 0.0 slice-start.1
  469.2 0.0 slice-start.7
  469.2 15.3 %fusion.12 = f32[1368,2048]{1,0:T(8,128)} fusion(bf16[2048,1368]{1,0:T(8,128)(2,1)S(1)} %bitcast.82, bf16[2048,2048]{1,0:T(8,128)(2,1)S(1)} %bitcast.78), kind=kOutput, calls=%fused_computation.18 | convolution fusion | flops 11475615744 | bytes 25198592 | tf_op jit(solution)/shard_map/sf,sd->fd/dot_general | solution.py:26
  484.5 15.0 %fusion.8 = f32[1368,2048]{1,0:T(8,128)} fusion(bf16[2048,1368]{1,0:T(8,128)(2,1)S(1)} %bitcast.80, bf16[1,2048,2048]{2,1,0:T(8,128)(2,1)S(1)} %bitcast.57), kind=kOutput, calls=%fused_computation.14 | convolution fusion | flops 11475615744 | bytes 25198592 | tf_op jit(solution)/shard_map/sf,sd->fd/dot_general | solution.py:26
  499.6 2.6 fusion.6
  502.2 3.1 all-gather.4.cloned.1.call-done.de_ref
  505.2 10.0 %fusion = f32[2048,576]{0,1:T(8,128)} fusion(bf16[2048,2048]{1,0:T(8,128)(2,1)} %get-tuple-element.82, bf16[2048,2688]{1,0:T(8,128)(2,1)} %all-gather.4.cloned.1.call-done.de_ref), kind=kOutput, calls=%fused_computation | convolution fusion | flops 4831838208 | bytes 15728640 | tf_op jit(solution)/shard_map/sc,sd->cd/dot_general | solution.py:26
  515.3 15.9 %scatter_rows.1 = bf16[12800,2048]{1,0:T(8,128)(2,1)} custom-call(s32[2176]{0:T(1024)} %concatenate.3.slot_ref, s32[2048]{0:T(1024)} %get-tuple-element.54.pos_ref, s32[1]{0:T(128)} %bitcast.1.cnt_ref, bf16[2048,2688]{1,0:T(8,128)(2,1)} %all-gather.4.cloned.1.call-done.de_ref, ...), custom_call_target="tpu_custom_call", output_to_operand_aliasing={{}: (4, {})} | custom-call | flops 20000000000 | bytes 20000000 | tf_op jit(solution)/shard_map/scatter_rows/pallas_call | solution.py:192
  (27 shorter events, 0.0 us)
Async XLA Ops:
  7.2 146.2 %all-gather.6.cloned.1.call-start = ((), (), s32[]{:S(2)}) async-start(), calls=%async_computation.3 | async-start | bytes 9437184 | tf_op jit(solution)/shard_map/all_gather | solution.py:873
  7.9 491.7 %reduce-scatter.2.cloned.1.call-start = ((), (), s32[]{:S(2)}) async-start(), calls=%async_computation.1 | async-start | bytes 9437184 | tf_op jit(solution)/shard_map/reduce_scatter | solution.py:877
  332.8 172.4 %all-gather.4.cloned.1.call-start = ((), (), s32[]{:S(2)}) async-start(), calls=%async_computation.2 | async-start | bytes 12386304 | tf_op jit(solution)/shard_map/all_gather | solution.py:873
  374.1 71.4 %copy-start.1 = (bf16[2,2048,192]{2,1,0:T(8,128)(2,1)S(1)}, bf16[2,2048,192]{2,1,0:T(8,128)(2,1)}, u32[]{:S(2)}) copy-start(bf16[2,2048,192]{2,1,0:T(8,128)(2,1)} %get-tuple-element.73.dq_ref) | copy-start | bytes 4718596
  445.4 6.4 %copy-start.5 = (bf16[2,2048,128]{2,1,0:T(8,128)(2,1)S(1)}, bf16[2,2048,128]{2,1,0:T(8,128)(2,1)}, u32[]{:S(2)}) copy-start(bf16[2,2048,128]{2,1,0:T(8,128)(2,1)} %get-tuple-element.76.dv_ref) | copy-start | bytes 3145732
  447.9 7.6 %copy-start.4 = (f32[1,4608]{1,0:T(1,128)S(1)}, f32[1,4608]{1,0:T(1,128)}, u32[]{:S(2)}) copy-start(f32[1,4608]{1,0:T(1,128)} %get-tuple-element.87) | copy-start | bytes 55300
  447.9 8.8 %copy-start = (bf16[2048,256]{1,0:T(8,128)(2,1)S(1)}, bf16[2048,256]{1,0:T(8,128)(2,1)}, u32[]{:S(2)}) copy-start(bf16[2048,256]{1,0:T(8,128)(2,1)} %get-tuple-element.58.o_ref) | copy-start | bytes 3145732
  451.8 12.1 %slice-start.2 = ((s8[8388608]{0:T(1024)(128)(4,1)}), s8[4194304]{0:T(1024)(128)(4,1)S(1)}, s32[]{:S(2)}) async-start(s8[8388608]{0:T(1024)(128)(4,1)} %bitcast.75), calls=%async_computation.6 | async-start | bytes 8388608
  456.7 7.2 %copy-start.2 = (bf16[2,2048,192]{1,2,0:T(8,128)(2,1)S(1)}, bf16[2,2048,192]{1,2,0:T(8,128)(2,1)}, u32[]{:S(2)}) copy-start(bf16[2,2048,192]{1,2,0:T(8,128)(2,1)} %copy.32) | copy-start | bytes 4718596
  456.7 7.2 %slice-start.3 = ((s8[8388608]{0:T(1024)(128)(4,1)}), s8[4194304]{0:T(1024)(128)(4,1)S(1)}, s32[]{:S(2)}) async-start(s8[8388608]{0:T(1024)(128)(4,1)} %bitcast.75), calls=%async_computation.7 | async-start | bytes 8388608
  456.7 12.5 %slice-start.4 = ((s8[8388608]{0:T(1024)(128)(4,1)}), s8[4194304]{0:T(1024)(128)(4,1)S(1)}, s32[]{:S(2)}) async-start(s8[8388608]{0:T(1024)(128)(4,1)} %bitcast.77), calls=%async_computation.8 | async-start | bytes 8388608
  456.7 12.5 %slice-start.8 = ((s8[5767168]{0:T(1024)(128)(4,1)}), s8[4194304]{0:T(1024)(128)(4,1)S(1)}, s32[]{:S(2)}) async-start(s8[5767168]{0:T(1024)(128)(4,1)} %bitcast.81), calls=%async_computation.12 | async-start | bytes 8388608
  464.0 5.2 slice-start.5
  464.0 5.2 slice-start.9
  464.0 20.5 %slice-start = ((s8[8388608]{0:T(1024)(128)(4,1)}), s8[4194304]{0:T(1024)(128)(4,1)S(1)}, s32[]{:S(2)}) async-start(s8[8388608]{0:T(1024)(128)(4,1)} %bitcast.56), calls=%async_computation.4 | async-start | bytes 8388608
  464.0 20.5 %slice-start.6 = ((s8[5767168]{0:T(1024)(128)(4,1)}), s8[4194304]{0:T(1024)(128)(4,1)S(1)}, s32[]{:S(2)}) async-start(s8[5767168]{0:T(1024)(128)(4,1)} %bitcast.79), calls=%async_computation.10 | async-start | bytes 8388608
  469.2 15.3 %slice-start.1 = ((s8[8388608]{0:T(1024)(128)(4,1)}), s8[4194304]{0:T(1024)(128)(4,1)S(1)}, s32[]{:S(2)}) async-start(s8[8388608]{0:T(1024)(128)(4,1)} %bitcast.56), calls=%async_computation.5 | async-start | bytes 8388608
  469.2 15.3 %slice-start.7 = ((s8[5767168]{0:T(1024)(128)(4,1)}), s8[1572864]{0:T(1024)(128)(4,1)S(1)}, s32[]{:S(2)}) async-start(s8[5767168]{0:T(1024)(128)(4,1)} %bitcast.79), calls=%async_computation.11 | async-start | bytes 3145728
  484.5 15.0 %copy-start.3 = (bf16[256,2048]{1,0:T(8,128)(2,1)S(1)}, bf16[256,2048]{1,0:T(8,128)(2,1)}, u32[]{:S(2)}) copy-start(bf16[256,2048]{1,0:T(8,128)(2,1)} %get-tuple-element.60.h_ref) | copy-start | bytes 3145732
Sparse Core Ops, SparseCore 0:
  9.8 63.6 all-gather.5
  332.9 67.3 reduce-scatter.1
  445.6 59.6 all-gather.3
